TPU v7x, 512 devices: a whole 4x8x8 slice. The times are simulated.
512 devices in a mesh: tm: 256 (over x, z_hi, y, core), space: 2 (over z_lo).
Axes of the slice: x: 4, y: 8, z: 8 (z_hi: 4, z_lo: 2; z = z_hi * 2 + z_lo), core: 2. Of those that a mesh axis runs over, the one named last changes fastest.
Arguments:
- initial: float32 [256, 32, 64, 128], P('tm', 'space'), may hold values from -6 to 6
- source: float32 [256, 32, 64, 128], P('tm', 'space'), may hold values from -6 to 6
- diffusion: float32 [32, 64, 128], P('space'), may hold values from 0.1 to 1
- advection: float32 [3, 32, 64, 128], P(None, 'space'), may hold values from 0.05 to 0.5
Outputs:
- smoothed: float32 [256, 32, 64, 128], P('tm', 'space')
- residual: float32 [256, 32, 64, 128], P('tm', 'space')
All inputs are finite; a program needn't handle non-finite values.
Results may differ from a plain program's by a relative error of at most 0.00002.
Values sent between devices are 32-bit elements; how exact they have to be, the bound alone decides.
No kernel may reach another device: no remote copies, remote signals or barrier semaphores. Data moves between devices by JAX's collectives and lax.ppermute only.
A program may use at most 64 MiB of HBM per device.

v0:
```python
import jax
import jax.numpy as jnp
from jax import lax
from jax.sharding import PartitionSpec as P

SWEEPS = 2
ITERS = 4


def from_behind(value, axis, steps):
    count = lax.axis_size(axis)
    pairs = [(source, (source + steps) % count) for source in range(count)]
    return lax.ppermute(value, axis, pairs)


def extended_2(value, sides, width):
    for axis, dim in sides:
        count, length = (lax.axis_size(axis), value.shape[dim])
        up = [(i, (i + 1) % count) for i in range(count - 1)]
        down = [(j, i) for i, j in up]
        last = lax.slice_in_dim(value, length - width, length, axis=dim)
        first = lax.slice_in_dim(value, 0, width, axis=dim)
        before = lax.ppermute(last, axis, up)
        after = lax.ppermute(first, axis, down)
        value = jnp.concatenate([before, value, after], axis=dim)
    return value


def off_terms(padded, spread, upwind):
    low_z = padded[..., :-2, 1:-1, 1:-1]
    high_z = padded[..., 2:, 1:-1, 1:-1]
    low_x = padded[..., 1:-1, :-2, 1:-1]
    high_x = padded[..., 1:-1, 2:, 1:-1]
    low_y = padded[..., 1:-1, 1:-1, :-2]
    high_y = padded[..., 1:-1, 1:-1, 2:]
    total = spread * (high_z + low_z + high_x + low_x + high_y + low_y)
    return total + upwind[0] * low_x + upwind[1] * low_y + upwind[2] * low_z


def main_diagonal(spread, upwind):
    return 1.0 + 6.0 * spread + (upwind[0] + upwind[1] + upwind[2])


def earlier_steps(field):
    arrived = from_behind(field, "tm", 1)
    return jnp.concatenate([arrived, field[:-1]], 0)


def body(initial, source, diffusion, advection):
    diagonal = main_diagonal(diffusion, advection)
    smoothed = initial
    coefs = jnp.concatenate([diffusion[None], advection], 0)
    wide_coefs = extended_2(coefs, (("space", 1),), ITERS)
    wide_spread = wide_coefs[0]
    wide_upwind = wide_coefs[1:]
    wide_diagonal = main_diagonal(wide_spread, wide_upwind)
    for sweep in range(SWEEPS):
        forcing = earlier_steps(smoothed) + source
        stacked = jnp.stack([smoothed, forcing], 0)
        widened = extended_2(stacked, (("space", 2),), ITERS)
        current = widened[0]
        wide_forcing = widened[1]
        for step in range(ITERS):
            padded = jnp.pad(current, ((0, 0), (1, 1), (1, 1), (1, 1)))
            current = (wide_forcing + off_terms(padded, wide_spread, wide_upwind)) / wide_diagonal
        smoothed = current[:, ITERS:-ITERS]
    prior = earlier_steps(smoothed)
    extended = extended_2(smoothed, (("space", 1),), 1)
    padded = jnp.pad(extended, ((0, 0), (0, 0), (1, 1), (1, 1)))
    applied = diagonal * smoothed - off_terms(padded, diffusion, advection)
    residual = source + prior - applied
    return (smoothed, residual)


def solution(mesh):
    in_specs = (
        P("tm", "space", None, None),
        P("tm", "space", None, None),
        P("space", None, None),
        P(None, "space", None, None),
    )
    out_specs = (P("tm", "space", None, None), P("tm", "space", None, None))
    return jax.shard_map(body, mesh=mesh, in_specs=in_specs, out_specs=out_specs, check_vma=False)
```

profile of v0, /device:TPU:6, one launch (start us, length us, event | category | flops | bytes accessed | tf_op | source)
XLA Modules:
  0.0 100.6 jit_solution(1813798604223853301)
XLA Ops:
  0.6 1.9 %collective-permute-start = (f32[1,16,64,128]{3,2,1,0:T(8,128)}, f32[1,16,64,128]{3,2,1,0:T(8,128)S(1)}, u32[]{:S(2)}, u32[]{:S(2)}) collective-permute-start(f32[1,16,64,128]{3,2,1,0:T(8,128)} %param.4), channel_id=1, source_target_pairs={{0,2},{2,4},{4,6},{6,8},{8,10},{10,12},{12,14},{14,16},{16,18},{18... | collective-permute-start | bytes 1572872 | tf_op jit(solution)/shard_map/ppermute | solution.py:13
  2.6 0.0 copy-start.1
  2.6 1.3 %pad_maximum_fusion.6 = (f32[4,4,64,128]{3,2,1,0:T(8,128)S(1)}, f32[4,4,64,128]{3,2,1,0:T(8,128)S(1)}) fusion(f32[3,16,64,128]{3,2,1,0:T(8,128)} %param.7, f32[1,16,64,128]{3,2,1,0:T(8,128)} %bitcast.38), kind=kLoop, calls=%fused_computation.170 | loop fusion | flops 262144 | bytes 3145728 | tf_op jit(solution)/shard_map/slice | solution.py:21
  3.9 0.0 copy-start.4
  3.9 4.4 %collective-permute-start.3 = (f32[4,4,64,128]{3,2,1,0:T(8,128)S(1)}, f32[4,4,64,128]{3,2,1,0:T(8,128)S(1)}, u32[]{:S(2)}, u32[]{:S(2)}) collective-permute-start(f32[4,4,64,128]{3,2,1,0:T(8,128)S(1)} %get-tuple-element.8), channel_id=1, source_target_pairs={{0,1},{2,3},{4,5},{6,7},{8,9},{10,11},{12,13},{14,15},{16,17},{18,... | collective-permute-start | bytes 1572872 | tf_op jit(solution)/shard_map/ppermute | solution.py:23
  8.3 0.0 copy-start
  8.4 0.0 copy-start.2
  8.4 1.4 %collective-permute-start.4 = (f32[4,4,64,128]{3,2,1,0:T(8,128)S(1)}, f32[4,4,64,128]{3,2,1,0:T(8,128)S(1)}, u32[]{:S(2)}, u32[]{:S(2)}) collective-permute-start(f32[4,4,64,128]{3,2,1,0:T(8,128)S(1)} %get-tuple-element.9), channel_id=1, source_target_pairs={{1,0},{3,2},{5,4},{7,6},{9,8},{11,10},{13,12},{15,14},{17,16},{19,... | collective-permute-start | bytes 1572872 | tf_op jit(solution)/shard_map/ppermute | solution.py:24
  9.8 17.1 %collective-permute-done = f32[1,16,64,128]{3,2,1,0:T(8,128)S(1)} collective-permute-done((f32[1,16,64,128]{3,2,1,0:T(8,128)}, f32[1,16,64,128]{3,2,1,0:T(8,128)S(1)}, u32[]{:S(2)}, u32[]{:S(2)}) %collective-permute-start) | collective-permute-done | bytes 524320 | tf_op jit(solution)/shard_map/ppermute | solution.py:13
  26.9 0.0 copy-done.1
  26.9 0.1 add_bitcast_fusion.1
  26.9 0.0 copy-done.4
  27.0 3.1 %collective-permute-start.1 = (f32[2,1,4,64,128]{4,3,2,1,0:T(8,128)S(1)}, f32[2,1,4,64,128]{4,3,2,1,0:T(8,128)S(1)}, u32[]{:S(2)}, u32[]{:S(2)}) collective-permute-start(f32[2,1,4,64,128]{4,3,2,1,0:T(8,128)S(1)} %get-tuple-element.14), channel_id=1, source_target_pairs={{0,1},{2,3},{4,5},{6,7},{8,9},{10,11},{12,13},{14,15},{16,17},{18,... | collective-permute-start | bytes 786440 | tf_op jit(solution)/shard_map/ppermute | solution.py:23
  30.1 1.3 %collective-permute-start.2 = (f32[2,1,4,64,128]{4,3,2,1,0:T(8,128)S(1)}, f32[2,1,4,64,128]{4,3,2,1,0:T(8,128)S(1)}, u32[]{:S(2)}, u32[]{:S(2)}) collective-permute-start(f32[2,1,4,64,128]{4,3,2,1,0:T(8,128)S(1)} %get-tuple-element.15), channel_id=1, source_target_pairs={{1,0},{3,2},{5,4},{7,6},{9,8},{11,10},{13,12},{15,14},{17,16},{19,... | collective-permute-start | bytes 786440 | tf_op jit(solution)/shard_map/ppermute | solution.py:24
  31.4 0.2 collective-permute-done.3
  31.6 0.0 collective-permute-done.4
  31.6 0.4 pad_maximum_fusion
  32.0 5.2 %collective-permute-done.1 = f32[2,1,4,64,128]{4,3,2,1,0:T(8,128)S(1)} collective-permute-done((f32[2,1,4,64,128]{4,3,2,1,0:T(8,128)S(1)}, f32[2,1,4,64,128]{4,3,2,1,0:T(8,128)S(1)}, u32[]{:S(2)}, u32[]{:S(2)}) %collective-permute-start.1) | collective-permute-done | bytes 262176 | tf_op jit(solution)/shard_map/ppermute | solution.py:23
  37.2 1.1 %collective-permute-done.2 = f32[2,1,4,64,128]{4,3,2,1,0:T(8,128)S(1)} collective-permute-done((f32[2,1,4,64,128]{4,3,2,1,0:T(8,128)S(1)}, f32[2,1,4,64,128]{4,3,2,1,0:T(8,128)S(1)}, u32[]{:S(2)}, u32[]{:S(2)}) %collective-permute-start.2) | collective-permute-done | bytes 262176 | tf_op jit(solution)/shard_map/ppermute | solution.py:24
  38.3 0.1 pad_maximum_fusion.1
  38.5 0.2 slice_bitcast_fusion.2
  38.6 1.2 %fusion.97 = (f32[1,24,64,128]{3,2,1,0:T(8,128)S(1)}, f32[1,24,64,128]{3,2,1,0:T(8,128)S(1)}, f32[1,24,64,128]{3,2,1,0:T(8,128)S(1)}, f32[1,24,64,128]{3,2,1,0:T...) fusion(f32[4,24,64,128]{3,2,1,0:T(8,128)S(1)} %pad_maximum_fusion, ...), kind=kLoop, calls=%fused_computation.179 | loop fusion | flops 3735552 | bytes 9437184 | tf_op jit(solution)/shard_map/slice | solution.py:54
  39.8 0.8 fusion.24
  40.6 0.8 fusion.35
  41.4 0.8 fusion.40
  42.2 0.5 slice_divide_fusion
  42.8 1.9 %collective-permute-start.5 = (f32[1,16,64,128]{3,2,1,0:T(8,128)S(1)}, f32[1,16,64,128]{3,2,1,0:T(8,128)S(1)}, u32[]{:S(2)}, u32[]{:S(2)}) collective-permute-start(f32[1,16,64,128]{3,2,1,0:T(8,128)S(1)} %slice_divide_fusion), channel_id=1, source_target_pairs={{0,2},{2,4},{4,6},{6,8},{8,10},{10,12},{12,14},{14,16},{16,18},{18... | collective-permute-start | bytes 1572872 | tf_op jit(solution)/shard_map/ppermute | solution.py:13
  44.7 19.2 %collective-permute-done.5 = f32[1,16,64,128]{3,2,1,0:T(8,128)S(1)} collective-permute-done((f32[1,16,64,128]{3,2,1,0:T(8,128)S(1)}, f32[1,16,64,128]{3,2,1,0:T(8,128)S(1)}, u32[]{:S(2)}, u32[]{:S(2)}) %collective-permute-start.5) | collective-permute-done | bytes 524320 | tf_op jit(solution)/shard_map/ppermute | solution.py:13
  63.9 0.1 add_bitcast_fusion
  64.0 3.0 %collective-permute-start.6 = (f32[2,1,4,64,128]{4,3,2,1,0:T(8,128)S(1)}, f32[2,1,4,64,128]{4,3,2,1,0:T(8,128)S(1)}, u32[]{:S(2)}, u32[]{:S(2)}) collective-permute-start(f32[2,1,4,64,128]{4,3,2,1,0:T(8,128)S(1)} %get-tuple-element.12), channel_id=1, source_target_pairs={{0,1},{2,3},{4,5},{6,7},{8,9},{10,11},{12,13},{14,15},{16,17},{18,... | collective-permute-start | bytes 786440 | tf_op jit(solution)/shard_map/ppermute | solution.py:23
  67.0 1.3 %collective-permute-start.7 = (f32[2,1,4,64,128]{4,3,2,1,0:T(8,128)S(1)}, f32[2,1,4,64,128]{4,3,2,1,0:T(8,128)S(1)}, u32[]{:S(2)}, u32[]{:S(2)}) collective-permute-start(f32[2,1,4,64,128]{4,3,2,1,0:T(8,128)S(1)} %get-tuple-element.13), channel_id=1, source_target_pairs={{1,0},{3,2},{5,4},{7,6},{9,8},{11,10},{13,12},{15,14},{17,16},{19,... | collective-permute-start | bytes 786440 | tf_op jit(solution)/shard_map/ppermute | solution.py:24
  68.3 2.6 %collective-permute-done.6 = f32[2,1,4,64,128]{4,3,2,1,0:T(8,128)S(1)} collective-permute-done((f32[2,1,4,64,128]{4,3,2,1,0:T(8,128)S(1)}, f32[2,1,4,64,128]{4,3,2,1,0:T(8,128)S(1)}, u32[]{:S(2)}, u32[]{:S(2)}) %collective-permute-start.6) | collective-permute-done | bytes 262176 | tf_op jit(solution)/shard_map/ppermute | solution.py:23
  70.9 4.4 %collective-permute-done.7 = f32[2,1,4,64,128]{4,3,2,1,0:T(8,128)S(1)} collective-permute-done((f32[2,1,4,64,128]{4,3,2,1,0:T(8,128)S(1)}, f32[2,1,4,64,128]{4,3,2,1,0:T(8,128)S(1)}, u32[]{:S(2)}, u32[]{:S(2)}) %collective-permute-start.7) | collective-permute-done | bytes 262176 | tf_op jit(solution)/shard_map/ppermute | solution.py:24
  75.3 0.1 pad_maximum_fusion.2
  75.4 0.1 slice_bitcast_fusion
  75.5 0.8 fusion.51
  76.3 0.8 fusion.62
  77.1 0.8 fusion.73
  77.9 0.8 fusion.84
  78.8 0.0 copy-start.3
  78.8 1.9 %collective-permute-start.8 = (f32[1,16,64,128]{3,2,1,0:T(8,128)S(1)}, f32[1,16,64,128]{3,2,1,0:T(8,128)S(1)}, u32[]{:S(2)}, u32[]{:S(2)}) collective-permute-start(f32[1,16,64,128]{3,2,1,0:T(8,128)S(1)} %slice.355), channel_id=1, source_target_pairs={{0,2},{2,4},{4,6},{6,8},{8,10},{10,12},{12,14},{14,16},{16,18},{18... | collective-permute-start | bytes 1572872 | tf_op jit(solution)/shard_map/ppermute | solution.py:13
  80.7 1.4 %collective-permute-start.10 = (f32[1,1,64,128]{3,2,1,0:T(8,128)S(1)}, f32[1,1,64,128]{3,2,1,0:T(8,128)S(1)}, u32[]{:S(2)}, u32[]{:S(2)}) collective-permute-start(f32[1,1,64,128]{3,2,1,0:T(8,128)S(1)} %get-tuple-element.16), channel_id=1, source_target_pairs={{0,1},{2,3},{4,5},{6,7},{8,9},{10,11},{12,13},{14,15},{16,17},{18,... | collective-permute-start | bytes 98312 | tf_op jit(solution)/shard_map/ppermute | solution.py:23
  82.2 1.3 %collective-permute-start.9 = (f32[1,1,64,128]{3,2,1,0:T(8,128)S(1)}, f32[1,1,64,128]{3,2,1,0:T(8,128)S(1)}, u32[]{:S(2)}, u32[]{:S(2)}) collective-permute-start(f32[1,1,64,128]{3,2,1,0:T(8,128)S(1)} %get-tuple-element.17), channel_id=1, source_target_pairs={{1,0},{3,2},{5,4},{7,6},{9,8},{11,10},{13,12},{15,14},{17,16},{19,... | collective-permute-start | bytes 98312 | tf_op jit(solution)/shard_map/ppermute | solution.py:24
  83.5 0.3 collective-permute-done.10
  83.7 4.2 %collective-permute-done.9 = f32[1,1,64,128]{3,2,1,0:T(8,128)S(1)} collective-permute-done((f32[1,1,64,128]{3,2,1,0:T(8,128)S(1)}, f32[1,1,64,128]{3,2,1,0:T(8,128)S(1)}, u32[]{:S(2)}, u32[]{:S(2)}) %collective-permute-start.9) | collective-permute-done | bytes 32800 | tf_op jit(solution)/shard_map/ppermute | solution.py:24
  88.0 0.4 select_maximum_fusion
  88.4 10.7 %collective-permute-done.8 = f32[1,16,64,128]{3,2,1,0:T(8,128)S(1)} collective-permute-done((f32[1,16,64,128]{3,2,1,0:T(8,128)S(1)}, f32[1,16,64,128]{3,2,1,0:T(8,128)S(1)}, u32[]{:S(2)}, u32[]{:S(2)}) %collective-permute-start.8) | collective-permute-done | bytes 524320 | tf_op jit(solution)/shard_map/ppermute | solution.py:13
  99.1 1.5 %fusion.91 = f32[1,16,64,128]{3,2,1,0:T(8,128)} fusion(f32[1,18,66,130]{3,2,1,0:T(8,128)S(1)} %select_maximum_fusion, f32[1,1,64,128]{3,2,1,0:T(8,128)S(1)} %collective-permute-done.9, f32[1,16,64,128]{3,2,1,0:T(8,128)S(1)} %slice.355, f32[1,1,64,128]{3,2,1,0:T(8,128)S(1)} %collective-permute-done.10, f32[3,16,64,128]{3,2,1,0:T(8,128)S(1)} %copy-done, ...), kind=kLoop, calls=%fused_computation.154 | loop fusion | flops 3014656 | bytes 6356992 | tf_op jit(solution)/shard_map/sub | solution.py:71
  (7 shorter events, 0.1 us)
Async XLA Ops:
  0.6 26.2 %collective-permute-start = (f32[1,16,64,128]{3,2,1,0:T(8,128)}, f32[1,16,64,128]{3,2,1,0:T(8,128)S(1)}, u32[]{:S(2)}, u32[]{:S(2)}) collective-permute-start(f32[1,16,64,128]{3,2,1,0:T(8,128)} %param.4), channel_id=1, source_target_pairs={{0,2},{2,4},{4,6},{6,8},{8,10},{10,12},{12,14},{14,16},{16,18},{18... | collective-permute-start | bytes 1572872 | tf_op jit(solution)/shard_map/ppermute | solution.py:13
  2.6 24.3 %copy-start.1 = (f32[1,16,64,128]{3,2,1,0:T(8,128)S(1)}, f32[1,16,64,128]{3,2,1,0:T(8,128)}, u32[]{:S(2)}) copy-start(f32[1,16,64,128]{3,2,1,0:T(8,128)} %param.5) | copy-start | bytes 1572868
  3.9 23.0 %copy-start.4 = (f32[1,16,64,128]{3,2,1,0:T(8,128)S(1)}, f32[1,16,64,128]{3,2,1,0:T(8,128)}, u32[]{:S(2)}) copy-start(f32[1,16,64,128]{3,2,1,0:T(8,128)} %param.4) | copy-start | bytes 1572868
  3.9 27.7 %collective-permute-start.3 = (f32[4,4,64,128]{3,2,1,0:T(8,128)S(1)}, f32[4,4,64,128]{3,2,1,0:T(8,128)S(1)}, u32[]{:S(2)}, u32[]{:S(2)}) collective-permute-start(f32[4,4,64,128]{3,2,1,0:T(8,128)S(1)} %get-tuple-element.8), channel_id=1, source_target_pairs={{0,1},{2,3},{4,5},{6,7},{8,9},{10,11},{12,13},{14,15},{16,17},{18,... | collective-permute-start | bytes 1572872 | tf_op jit(solution)/shard_map/ppermute | solution.py:23
  8.3 23.3 %copy-start = (f32[3,16,64,128]{3,2,1,0:T(8,128)S(1)}, f32[3,16,64,128]{3,2,1,0:T(8,128)}, u32[]{:S(2)}) copy-start(f32[3,16,64,128]{3,2,1,0:T(8,128)} %param.7) | copy-start | bytes 4718596
  8.4 23.2 %copy-start.2 = (f32[16,64,128]{2,1,0:T(8,128)S(1)}, f32[16,64,128]{2,1,0:T(8,128)}, u32[]{:S(2)}) copy-start(f32[16,64,128]{2,1,0:T(8,128)} %param.6) | copy-start | bytes 1572868
  8.4 23.2 %collective-permute-start.4 = (f32[4,4,64,128]{3,2,1,0:T(8,128)S(1)}, f32[4,4,64,128]{3,2,1,0:T(8,128)S(1)}, u32[]{:S(2)}, u32[]{:S(2)}) collective-permute-start(f32[4,4,64,128]{3,2,1,0:T(8,128)S(1)} %get-tuple-element.9), channel_id=1, source_target_pairs={{1,0},{3,2},{5,4},{7,6},{9,8},{11,10},{13,12},{15,14},{17,16},{19,... | collective-permute-start | bytes 1572872 | tf_op jit(solution)/shard_map/ppermute | solution.py:24
  27.0 10.2 %collective-permute-start.1 = (f32[2,1,4,64,128]{4,3,2,1,0:T(8,128)S(1)}, f32[2,1,4,64,128]{4,3,2,1,0:T(8,128)S(1)}, u32[]{:S(2)}, u32[]{:S(2)}) collective-permute-start(f32[2,1,4,64,128]{4,3,2,1,0:T(8,128)S(1)} %get-tuple-element.14), channel_id=1, source_target_pairs={{0,1},{2,3},{4,5},{6,7},{8,9},{10,11},{12,13},{14,15},{16,17},{18,... | collective-permute-start | bytes 786440 | tf_op jit(solution)/shard_map/ppermute | solution.py:23
  30.1 8.3 %collective-permute-start.2 = (f32[2,1,4,64,128]{4,3,2,1,0:T(8,128)S(1)}, f32[2,1,4,64,128]{4,3,2,1,0:T(8,128)S(1)}, u32[]{:S(2)}, u32[]{:S(2)}) collective-permute-start(f32[2,1,4,64,128]{4,3,2,1,0:T(8,128)S(1)} %get-tuple-element.15), channel_id=1, source_target_pairs={{1,0},{3,2},{5,4},{7,6},{9,8},{11,10},{13,12},{15,14},{17,16},{19,... | collective-permute-start | bytes 786440 | tf_op jit(solution)/shard_map/ppermute | solution.py:24
  42.8 21.1 %collective-permute-start.5 = (f32[1,16,64,128]{3,2,1,0:T(8,128)S(1)}, f32[1,16,64,128]{3,2,1,0:T(8,128)S(1)}, u32[]{:S(2)}, u32[]{:S(2)}) collective-permute-start(f32[1,16,64,128]{3,2,1,0:T(8,128)S(1)} %slice_divide_fusion), channel_id=1, source_target_pairs={{0,2},{2,4},{4,6},{6,8},{8,10},{10,12},{12,14},{14,16},{16,18},{18... | collective-permute-start | bytes 1572872 | tf_op jit(solution)/shard_map/ppermute | solution.py:13
  64.0 6.8 %collective-permute-start.6 = (f32[2,1,4,64,128]{4,3,2,1,0:T(8,128)S(1)}, f32[2,1,4,64,128]{4,3,2,1,0:T(8,128)S(1)}, u32[]{:S(2)}, u32[]{:S(2)}) collective-permute-start(f32[2,1,4,64,128]{4,3,2,1,0:T(8,128)S(1)} %get-tuple-element.12), channel_id=1, source_target_pairs={{0,1},{2,3},{4,5},{6,7},{8,9},{10,11},{12,13},{14,15},{16,17},{18,... | collective-permute-start | bytes 786440 | tf_op jit(solution)/shard_map/ppermute | solution.py:23
  67.0 8.3 %collective-permute-start.7 = (f32[2,1,4,64,128]{4,3,2,1,0:T(8,128)S(1)}, f32[2,1,4,64,128]{4,3,2,1,0:T(8,128)S(1)}, u32[]{:S(2)}, u32[]{:S(2)}) collective-permute-start(f32[2,1,4,64,128]{4,3,2,1,0:T(8,128)S(1)} %get-tuple-element.13), channel_id=1, source_target_pairs={{1,0},{3,2},{5,4},{7,6},{9,8},{11,10},{13,12},{15,14},{17,16},{19,... | collective-permute-start | bytes 786440 | tf_op jit(solution)/shard_map/ppermute | solution.py:24
  78.8 21.9 %copy-start.3 = (f32[1,16,64,128]{3,2,1,0:T(8,128)}, f32[1,16,64,128]{3,2,1,0:T(8,128)S(1)}, u32[]{:S(2)}) copy-start(f32[1,16,64,128]{3,2,1,0:T(8,128)S(1)} %slice.355) | copy-start | bytes 1572868
  78.8 20.3 %collective-permute-start.8 = (f32[1,16,64,128]{3,2,1,0:T(8,128)S(1)}, f32[1,16,64,128]{3,2,1,0:T(8,128)S(1)}, u32[]{:S(2)}, u32[]{:S(2)}) collective-permute-start(f32[1,16,64,128]{3,2,1,0:T(8,128)S(1)} %slice.355), channel_id=1, source_target_pairs={{0,2},{2,4},{4,6},{6,8},{8,10},{10,12},{12,14},{14,16},{16,18},{18... | collective-permute-start | bytes 1572872 | tf_op jit(solution)/shard_map/ppermute | solution.py:13
  80.7 3.0 %collective-permute-start.10 = (f32[1,1,64,128]{3,2,1,0:T(8,128)S(1)}, f32[1,1,64,128]{3,2,1,0:T(8,128)S(1)}, u32[]{:S(2)}, u32[]{:S(2)}) collective-permute-start(f32[1,1,64,128]{3,2,1,0:T(8,128)S(1)} %get-tuple-element.16), channel_id=1, source_target_pairs={{0,1},{2,3},{4,5},{6,7},{8,9},{10,11},{12,13},{14,15},{16,17},{18,... | collective-permute-start | bytes 98312 | tf_op jit(solution)/shard_map/ppermute | solution.py:23
  82.2 5.8 %collective-permute-start.9 = (f32[1,1,64,128]{3,2,1,0:T(8,128)S(1)}, f32[1,1,64,128]{3,2,1,0:T(8,128)S(1)}, u32[]{:S(2)}, u32[]{:S(2)}) collective-permute-start(f32[1,1,64,128]{3,2,1,0:T(8,128)S(1)} %get-tuple-element.17), channel_id=1, source_target_pairs={{1,0},{3,2},{5,4},{7,6},{9,8},{11,10},{13,12},{15,14},{17,16},{19,... | collective-permute-start | bytes 98312 | tf_op jit(solution)/shard_map/ppermute | solution.py:24
where the time goes:
time: 101 us
  waiting for transfers between devices  65 us (64%)
  starting transfers between devices  23 us (23%)
  other arithmetic  11.4 us (11%)
    ppermute x3, waiting for transfers between devices, from_behind(): return lax.ppermute(value, axis, pairs)  47 us
    ppermute x4, starting transfers between devices, extended_2(): before = lax.ppermute(last, axis, up)  11.9 us
    ppermute x4, waiting for transfers between devices, extended_2(): after = lax.ppermute(first, axis, down)  9.77 us
    ppermute x4, waiting for transfers between devices, extended_2(): before = lax.ppermute(last, axis, up)  8.25 us
    ppermute x3, starting transfers between devices, from_behind(): return lax.ppermute(value, axis, pairs)  5.76 us
    div x7, other arithmetic, body(): (wide_forcing + off_terms(padded, wide_spread, wide_upwind)) / wide_diagonal  5.41 us
    ppermute x4, starting transfers between devices, extended_2(): after = lax.ppermute(first, axis, down)  5.3 us
  transfers between devices with their start and end apart: 11, of which 10 were waited for; matrix products, arithmetic and copies ran while one was open for 2% of the time, Pallas kernels for 0%

commit v1 on v0

v1 whole, which is shorter than its diff:
```python
import jax
import jax.numpy as jnp
from jax import lax
from jax.experimental import pallas as pl
from jax.experimental.pallas import tpu as pltpu
from jax.sharding import PartitionSpec as P

SWEEPS = 2
ITERS = 4
THIN = ITERS - 1
F32 = jnp.float32
ROLE, SIDE = 0, 1


def in_vmem(count):
    return [pl.BlockSpec(memory_space=pltpu.VMEM)] * count


def call(kernel, outs, scalars, *operands, scratch=()):
    return pl.pallas_call(
        kernel,
        out_shape=[jax.ShapeDtypeStruct(o, F32) for o in outs],
        in_specs=[pl.BlockSpec(memory_space=pltpu.SMEM)] + in_vmem(len(operands)),
        out_specs=in_vmem(len(outs)),
        scratch_shapes=list(scratch),
        compiler_params=pltpu.CompilerParams(vmem_limit_bytes=16 * 1024 * 1024),
    )(scalars, *operands)


def coef_kernel(scal, spread_ref, upwind_ref, halo_ref, c_ref, x_ref, y_ref, z_ref, inv_ref, diag_ref):
    side = scal[SIDE]
    depth, nx, ny = spread_ref.shape
    row = lax.broadcasted_iota(jnp.int32, (nx, ny), 0)
    lane = lax.broadcasted_iota(jnp.int32, (nx, ny), 1)

    def one(spread, ux, uy, uz, at):
        diagonal = 1.0 + 6.0 * spread + (ux + uy + uz)
        inv = 1.0 / diagonal
        c_ref[at] = spread * inv
        x_ref[at] = jnp.where(row == 0, 0.0, (spread + ux) * inv)
        y_ref[at] = jnp.where(lane == 0, 0.0, (spread + uy) * inv)
        z_ref[at] = (spread + uz) * inv
        inv_ref[at] = inv
        return diagonal

    def own(z, carry):
        diag_ref[z] = one(spread_ref[z], upwind_ref[0, z], upwind_ref[1, z], upwind_ref[2, z], ITERS * side + z)
        return carry

    lax.fori_loop(0, depth, own, 0, unroll=2)
    for q in range(THIN):
        at = jnp.where(side == 1, 1 + q, depth + q)
        one(halo_ref[q], halo_ref[THIN + q], halo_ref[2 * THIN + q], halo_ref[3 * THIN + q], at)


def stencil(below, here, above, c, cx, cy, cz, row_last, lane_last):
    nx, ny = here.shape
    low_x = pltpu.roll(here, 1, 0)
    high_x = jnp.where(row_last, 0.0, pltpu.roll(here, nx - 1, 0))
    low_y = pltpu.roll(here, 1, 1)
    high_y = jnp.where(lane_last, 0.0, pltpu.roll(here, ny - 1, 1))
    return c * ((above + high_x) + high_y) + (cx * low_x + cz * below) + cy * low_y


def last_masks(nx, ny):
    row = lax.broadcasted_iota(jnp.int32, (nx, ny), 0)
    lane = lax.broadcasted_iota(jnp.int32, (nx, ny), 1)
    return row == nx - 1, lane == ny - 1


def sweep_kernel(role, pass_on, scal, *refs):
    if pass_on:
        other_ref, *refs = refs
    (v_ref, vh_ref, s_ref, sh_ref, p_ref, ph_ref, c_ref, x_ref, y_ref, z_ref, inv_ref, out_ref, edge4_ref, edge3_ref, va, vb, g) = refs
    side = scal[SIDE]
    depth, nx, ny = v_ref.shape

    @pl.when(scal[ROLE] == role)
    def _():
        row_last, lane_last = last_masks(nx, ny)
        zero = jnp.zeros((nx, ny), F32)
        for buf in (va, vb):
            buf[0] = zero
            buf[depth + ITERS + 1] = zero

        def fill(z, carry):
            at = ITERS * side + z
            va[1 + at] = v_ref[z]
            g[at] = (s_ref[z] + p_ref[z]) * inv_ref[at]
            return carry

        lax.fori_loop(0, depth, fill, 0, unroll=4)
        for q in range(ITERS):
            va[1 + jnp.where(side == 1, q, depth + q)] = vh_ref[q]
        for q in range(THIN):
            at = jnp.where(side == 1, 1 + q, depth + q)
            g[at] = (sh_ref[q] + ph_ref[q]) * inv_ref[at]
        src, dst = va, vb
        for k in range(ITERS):
            start = side * (1 + k)
            last = k == ITERS - 1

            def layer(j, carry, src=src, dst=dst, start=start, last=last):
                e = start + j
                new = g[e] + stencil(
                    src[e], src[e + 1], src[e + 2], c_ref[e], x_ref[e], y_ref[e], z_ref[e], row_last, lane_last
                )
                if last:
                    out_ref[j] = new
                else:
                    dst[e + 1] = new
                return carry

            count = depth + ITERS - 1 - k
            lax.fori_loop(0, count, layer, 0, unroll=True)
            src, dst = dst, src

    if pass_on:

        @pl.when(scal[ROLE] != role)
        def _():
            out_ref[...] = other_ref[...]

        for q in range(edge4_ref.shape[0]):
            edge4_ref[q] = out_ref[jnp.where(side == 1, q, depth - edge4_ref.shape[0] + q)]
    for q in range(THIN):
        edge3_ref[q] = out_ref[jnp.where(side == 1, q, depth - THIN + q)]


def defect_kernel(scal, v_ref, h_ref, s_ref, c_ref, x_ref, y_ref, z_ref, diag_ref, out_ref, va):
    side = scal[SIDE]
    depth, nx, ny = v_ref.shape
    row_last, lane_last = last_masks(nx, ny)
    zero = jnp.zeros((nx, ny), F32)
    va[0] = jnp.where(side == 1, h_ref[0], zero)
    va[depth + 1] = jnp.where(side == 1, zero, h_ref[0])
    for z in range(depth):
        va[1 + z] = v_ref[z]

    def layer(z, carry):
        e = ITERS * side + z
        here = va[1 + z]
        m = stencil(va[z], here, va[z + 2], c_ref[e], x_ref[e], y_ref[e], z_ref[e], row_last, lane_last)
        out_ref[z] = s_ref[z] - diag_ref[z] * (here - m)
        return carry

    lax.fori_loop(0, depth, layer, 0, unroll=True)


def body(initial, source, diffusion, advection):
    tm, space = (lax.axis_size("tm"), lax.axis_size("space"))
    role = lax.axis_index("tm") % 2
    side = lax.axis_index("space")
    scalars = jnp.stack([role, side]).astype(jnp.int32)
    shape = initial.shape[1:]
    depth = shape[0]
    initial, source = (initial[0], source[0])

    def number(t, s):
        return (t % tm) * space + s

    def permute(value, pairs):
        return lax.ppermute(value, ("tm", "space"), pairs)

    sides = range(space)
    into_odd = [(number(t, s), number(t + 1, s)) for t in range(0, tm, 2) for s in sides]
    into_even = [(number(t, s), number(t + 1, s)) for t in range(1, tm, 2) for s in sides]
    across = [(number(t, s), number(t, 1 - s)) for t in range(tm) for s in sides]
    odd_across = [(number(t, s), number(t + 1, 1 - s)) for t in range(0, tm, 2) for s in sides]
    even_across = [(number(t, s), number(t + 1, 1 - s)) for t in range(1, tm, 2) for s in sides]

    def edge(value, width, axis=0):
        return lax.dynamic_slice_in_dim(value, (1 - side) * (depth - width), width, axis)

    ext = (depth + ITERS,) + shape[1:]
    padded = (depth + ITERS + 2,) + shape[1:]
    scratch = [pltpu.VMEM(padded, F32), pltpu.VMEM(padded, F32), pltpu.VMEM(ext, F32)]
    thin = (THIN,) + shape[1:]
    wide = (ITERS,) + shape[1:]

    b1 = permute(initial, into_even)
    d1 = permute(edge(initial, THIN), odd_across + even_across)
    halo = jnp.concatenate(
        [edge(diffusion, THIN), edge(advection, THIN, 1).reshape((3 * THIN,) + shape[1:]), edge(source, THIN), edge(initial, ITERS)], 0
    )
    halo = permute(halo, across)
    a1 = permute(initial, into_odd)
    *coefs, diag = call(coef_kernel, [ext] * 5 + [shape], scalars, diffusion, advection, halo)
    source_halo = halo[4 * THIN : 5 * THIN]
    initial_halo = halo[5 * THIN :]

    def sweep(mine, other, v, vh, p, ph):
        import functools

        outs = [shape, wide if mine == 0 else (1,) + shape[1:], thin]
        pass_on = other is not None
        extra = [other] if pass_on else []
        return call(
            functools.partial(sweep_kernel, mine, pass_on), outs, scalars, *extra, v, vh, source, source_halo, p, ph, *coefs, scratch=scratch
        )

    x, _, xt = sweep(1, None, initial, initial_halo, a1, d1)
    b2 = permute(x, into_even)
    dx = permute(xt, even_across)
    s1, s1w, s1t = sweep(0, x, initial, initial_halo, b1, d1)
    dy = permute(s1t, odd_across)
    s1h = permute(s1w, across)
    a2 = permute(s1, into_odd)
    z, _, _ = sweep(1, None, s1, s1h, a2, dy)
    b3 = permute(z, into_even)
    s2, s2w, _ = sweep(0, z, s1, s1h, b2, dx)
    a3 = permute(s2, into_odd)
    side_edge = edge(s2, 1)
    s2h = permute(side_edge, across)
    (defect,) = call(defect_kernel, [shape], scalars, s2, s2h, source, *coefs[:4], diag, scratch=[pltpu.VMEM((depth + 2,) + shape[1:], F32)])
    residual = defect + (a3 + b3)
    return (s2[None], residual[None])


def solution(mesh):
    in_specs = (
        P("tm", "space", None, None),
        P("tm", "space", None, None),
        P("space", None, None),
        P(None, "space", None, None),
    )
    out_specs = (P("tm", "space", None, None), P("tm", "space", None, None))
    return jax.shard_map(body, mesh=mesh, in_specs=in_specs, out_specs=out_specs, check_vma=False)
```

time: 101 us -> 103 us (1.020)
  the two profiles are of different devices: /device:TPU:6 before, /device:TPU:64 now
where the time goes in v1:
time: 103 us; the launch traced here: 102 us
  waiting for transfers between devices  50 us (49%)
  starting transfers between devices  24.7 us (24%)
  local copies, waits for them, and re-layouts  12.7 us (12%)
  Pallas kernels  11.4 us (11%)
  other arithmetic  2.22 us (2%)
    ppermute x12, waiting for transfers between devices, permute(): return lax.ppermute(value, ('tm', 'space'), pairs)  50 us
    ppermute x12, starting transfers between devices, permute(): return lax.ppermute(value, ('tm', 'space'), pairs)  24.7 us
    pallas_call x6, Pallas kernels, call(): pl.pallas_call(kernel, out_shape=[jax.ShapeDtypeStruct(o, F32) for o in o...  11.4 us
    unnamed x16, local copies, waits for them, and re-layouts  7.27 us
    dynamic_slice x6, local copies, waits for them, and re-layouts, edge(): lax.dynamic_slice_in_dim(value, (1 - side) * (depth - width), width, axis)  5.38 us
    broadcast_in_dim x1, other arithmetic, body(): return (s2[None], residual[None])  2.09 us
  transfers between devices with their start and end apart: 12, of which 6 were waited for; matrix products, arithmetic and copies ran while one was open for 2% of the time, Pallas kernels for 5%

profile of v1, /device:TPU:64, one launch (start us, length us, event | category | flops | bytes accessed | tf_op | source)
XLA Modules:
  0.0 101.9 jit_solution(2105961829595079815)
XLA Ops:
  0.6 1.0 constant_dynamic-slice_fusion.1
  1.6 0.9 constant_dynamic-slice_fusion.2
  2.5 0.9 dynamic-slice_bitcast_fusion.2
  3.4 0.9 dynamic-slice_bitcast_fusion
  4.4 6.9 %collective-permute-start = (f32[19,64,128]{2,1,0:T(8,128)S(1)}, f32[19,64,128]{2,1,0:T(8,128)S(1)}, u32[]{:S(2)}, u32[]{:S(2)}) collective-permute-start(f32[19,64,128]{2,1,0:T(8,128)S(1)} %pad_maximum_fusion), channel_id=1, source_target_pairs={{0,1},{1,0},{2,3},{3,2},{4,5},{5,4},{6,7},{7,6},{8,9},{9,8},{10,11... | collective-permute-start | bytes 1867784 | tf_op jit(solution)/shard_map/ppermute | solution.py:163
  11.3 2.1 %collective-permute-start.1 = (f32[16,64,128]{2,1,0:T(8,128)}, f32[16,64,128]{2,1,0:T(8,128)}, u32[]{:S(2)}, u32[]{:S(2)}) collective-permute-start(f32[16,64,128]{2,1,0:T(8,128)} %bitcast.2.refs_0_.refs_1_), channel_id=1, source_target_pairs={{0,2},{1,3},{4,6},{5,7},{8,10},{9,11},{12,14},{13,15},{16,18},{17,... | collective-permute-start | bytes 1572872 | tf_op jit(solution)/shard_map/ppermute | solution.py:163
  13.4 1.3 %collective-permute-start.3 = (f32[16,64,128]{2,1,0:T(8,128)}, f32[16,64,128]{2,1,0:T(8,128)}, u32[]{:S(2)}, u32[]{:S(2)}) collective-permute-start(f32[16,64,128]{2,1,0:T(8,128)} %bitcast.2.refs_0_.refs_1_), channel_id=1, source_target_pairs={{2,4},{3,5},{6,8},{7,9},{10,12},{11,13},{14,16},{15,17},{18,20},{1... | collective-permute-start | bytes 1572872 | tf_op jit(solution)/shard_map/ppermute | solution.py:163
  14.7 0.9 dynamic-slice_bitcast_fusion.1
  15.6 1.9 %collective-permute-start.2 = (f32[3,64,128]{2,1,0:T(8,128)S(1)}, f32[3,64,128]{2,1,0:T(8,128)S(1)}, u32[]{:S(2)}, u32[]{:S(2)}) collective-permute-start(f32[3,64,128]{2,1,0:T(8,128)S(1)} %dynamic-slice_bitcast_fusion.1), channel_id=1, source_target_pairs={{0,3},{1,2},{4,7},{5,6},{8,11},{9,10},{12,15},{13,14},{16,19},{17,... | collective-permute-start | bytes 294920 | tf_op jit(solution)/shard_map/ppermute | solution.py:163
  17.6 0.1 pad_add_fusion.scal
  17.6 17.8 %collective-permute-done.halo_ref = f32[19,64,128]{2,1,0:T(8,128)S(1)} collective-permute-done((f32[19,64,128]{2,1,0:T(8,128)S(1)}, f32[19,64,128]{2,1,0:T(8,128)S(1)}, u32[]{:S(2)}, u32[]{:S(2)}) %collective-permute-start) | collective-permute-done | bytes 622624 | tf_op jit(solution)/shard_map/ppermute | solution.py:163
  35.4 0.0 copy-start.2
  35.5 0.9 copy-done.2
  36.3 1.4 %copy-done.1 = f32[3,16,64,128]{3,2,1,0:T(8,128)S(1)} copy-done((f32[3,16,64,128]{3,2,1,0:T(8,128)S(1)}, f32[3,16,64,128]{3,2,1,0:T(8,128)}, u32[]{:S(2)}) %copy-start.1) | copy-done | bytes 1572888
  37.7 1.1 %copy-done.3 = f32[19,64,128]{2,1,0:T(8,128)S(1)} copy-done((f32[19,64,128]{2,1,0:T(8,128)S(1)}, f32[19,64,128]{2,1,0:T(8,128)}, u32[]{:S(2)}) %copy-start.3) | copy-done | bytes 622616
  38.8 1.0 %copy-done.4 = f32[16,64,128]{2,1,0:T(8,128)S(1)} copy-done((f32[16,64,128]{2,1,0:T(8,128)S(1)}, f32[16,64,128]{2,1,0:T(8,128)}, u32[]{:S(2)}) %copy-start.4) | copy-done | bytes 524312
  39.8 0.9 shard_map.59
  40.7 0.0 copy-start.6
  40.7 0.8 copy-done.6
  41.5 0.0 collective-permute-done.2.refs_5_.refs_6_
  41.5 0.0 collective-permute-done.1.refs_4_
  41.5 0.0 copy-done
  41.5 1.8 %shard_map.60 = (f32[16,64,128]{2,1,0:T(8,128)S(1)}, f32[1,64,128]{2,1,0:T(8,128)}, f32[3,64,128]{2,1,0:T(8,128)S(1)}) custom-call(s32[2]{0:T(128)S(1)} %pad_add_fusion.scal, f32[16,64,128]{2,1,0:T(8,128)} %bitcast.2.refs_0_.refs_1_, f32[4,64,128]{2,1,0:T(8,128)S(1)} %slice.8.refs_1_.refs_2_, f32[16,64,128]{2,1,0:T(8,128)S(1)} %bitcast.14, ...), custom_call_target="tpu_custom_call" | custom-call | tf_op jit(solution)/shard_map/pallas_call | solution.py:20
  43.4 0.0 collective-permute-done.3.refs_5_
  43.4 2.9 %shard_map.61 = (f32[16,64,128]{2,1,0:T(8,128)S(1)}, f32[4,64,128]{2,1,0:T(8,128)S(1)}, f32[3,64,128]{2,1,0:T(8,128)S(1)}) custom-call(s32[2]{0:T(128)S(1)} %pad_add_fusion.scal, f32[16,64,128]{2,1,0:T(8,128)S(1)} %get-tuple-element.20.refs_0_, f32[16,64,128]{2,1,0:T(8,128)} %bitcast.2.refs_0_.refs_1_, f32[4,64,128]{2,1,0:T(8,128)S(1)} %slice.8.refs_1_.refs_2_, ...), custom_call_target="tpu_custom_call" | custom-call | tf_op jit(solution)/shard_map/pallas_call | solution.py:20
  46.3 1.3 %collective-permute-start.5 = (f32[16,64,128]{2,1,0:T(8,128)S(1)}, f32[16,64,128]{2,1,0:T(8,128)S(1)}, u32[]{:S(2)}, u32[]{:S(2)}) collective-permute-start(f32[16,64,128]{2,1,0:T(8,128)S(1)} %get-tuple-element.21.refs_0_.refs_1_), channel_id=1, source_target_pairs={{0,2},{1,3},{4,6},{5,7},{8,10},{9,11},{12,14},{13,15},{16,18},{17,... | collective-permute-start | bytes 1572872 | tf_op jit(solution)/shard_map/ppermute | solution.py:163
  47.6 1.3 %collective-permute-start.7 = (f32[16,64,128]{2,1,0:T(8,128)S(1)}, f32[16,64,128]{2,1,0:T(8,128)S(1)}, u32[]{:S(2)}, u32[]{:S(2)}) collective-permute-start(f32[16,64,128]{2,1,0:T(8,128)S(1)} %get-tuple-element.20.refs_0_), channel_id=1, source_target_pairs={{2,4},{3,5},{6,8},{7,9},{10,12},{11,13},{14,16},{15,17},{18,20},{1... | collective-permute-start | bytes 1572872 | tf_op jit(solution)/shard_map/ppermute | solution.py:163
  48.9 1.9 %collective-permute-start.4 = (f32[4,64,128]{2,1,0:T(8,128)S(1)}, f32[4,64,128]{2,1,0:T(8,128)S(1)}, u32[]{:S(2)}, u32[]{:S(2)}) collective-permute-start(f32[4,64,128]{2,1,0:T(8,128)S(1)} %get-tuple-element.22), channel_id=1, source_target_pairs={{0,1},{1,0},{2,3},{3,2},{4,5},{5,4},{6,7},{7,6},{8,9},{9,8},{10,11... | collective-permute-start | bytes 393224 | tf_op jit(solution)/shard_map/ppermute | solution.py:163
  50.8 1.3 %collective-permute-start.6 = (f32[3,64,128]{2,1,0:T(8,128)S(1)}, f32[3,64,128]{2,1,0:T(8,128)S(1)}, u32[]{:S(2)}, u32[]{:S(2)}) collective-permute-start(f32[3,64,128]{2,1,0:T(8,128)S(1)} %get-tuple-element.23), channel_id=1, source_target_pairs={{0,3},{1,2},{4,7},{5,6},{8,11},{9,10},{12,15},{13,14},{16,19},{17,... | collective-permute-start | bytes 294920 | tf_op jit(solution)/shard_map/ppermute | solution.py:163
  52.1 1.3 %collective-permute-start.8 = (f32[3,64,128]{2,1,0:T(8,128)S(1)}, f32[3,64,128]{2,1,0:T(8,128)S(1)}, u32[]{:S(2)}, u32[]{:S(2)}) collective-permute-start(f32[3,64,128]{2,1,0:T(8,128)S(1)} %get-tuple-element.25), channel_id=1, source_target_pairs={{2,5},{3,4},{6,9},{7,8},{10,13},{11,12},{14,17},{15,16},{18,21},{1... | collective-permute-start | bytes 294920 | tf_op jit(solution)/shard_map/ppermute | solution.py:163
  53.4 0.9 collective-permute-done.6.refs_5_
  54.3 1.4 %collective-permute-done.4.refs_1_.refs_2_ = f32[4,64,128]{2,1,0:T(8,128)S(1)} collective-permute-done((f32[4,64,128]{2,1,0:T(8,128)S(1)}, f32[4,64,128]{2,1,0:T(8,128)S(1)}, u32[]{:S(2)}, u32[]{:S(2)}) %collective-permute-start.4) | collective-permute-done | bytes 131104 | tf_op jit(solution)/shard_map/ppermute | solution.py:163
  55.8 0.0 collective-permute-done.5.refs_4_
  55.8 1.4 %shard_map.62 = (f32[16,64,128]{2,1,0:T(8,128)}, f32[1,64,128]{2,1,0:T(8,128)}, f32[3,64,128]{2,1,0:T(8,128)}) custom-call(s32[2]{0:T(128)S(1)} %pad_add_fusion.scal, f32[16,64,128]{2,1,0:T(8,128)S(1)} %get-tuple-element.21.refs_0_.refs_1_, f32[4,64,128]{2,1,0:T(8,128)S(1)} %collective-permute-done.4.refs_1_.refs_2_, f32[16,64,128]{2,1,0:T(8,128)S(1)} %bitcast.16, ...), custom_call_target="tpu_custom_call" | custom-call | tf_op jit(solution)/shard_map/pallas_call | solution.py:20
  57.1 14.8 %collective-permute-done.8.refs_6_ = f32[3,64,128]{2,1,0:T(8,128)S(1)} collective-permute-done((f32[3,64,128]{2,1,0:T(8,128)S(1)}, f32[3,64,128]{2,1,0:T(8,128)S(1)}, u32[]{:S(2)}, u32[]{:S(2)}) %collective-permute-start.8) | collective-permute-done | bytes 98336 | tf_op jit(solution)/shard_map/ppermute | solution.py:163
  71.9 0.0 collective-permute-done.7.refs_5_
  71.9 3.6 %shard_map.63 = (f32[16,64,128]{2,1,0:T(8,128)}, f32[4,64,128]{2,1,0:T(8,128)}, f32[3,64,128]{2,1,0:T(8,128)}) custom-call(s32[2]{0:T(128)S(1)} %pad_add_fusion.scal, f32[16,64,128]{2,1,0:T(8,128)} %get-tuple-element.24.refs_0_, f32[16,64,128]{2,1,0:T(8,128)S(1)} %get-tuple-element.21.refs_0_.refs_1_, ...), custom_call_target="tpu_custom_call" | custom-call | tf_op jit(solution)/shard_map/pallas_call | solution.py:20
  75.5 2.2 %collective-permute-start.10 = (f32[16,64,128]{2,1,0:T(8,128)}, f32[16,64,128]{2,1,0:T(8,128)}, u32[]{:S(2)}, u32[]{:S(2)}) collective-permute-start(f32[16,64,128]{2,1,0:T(8,128)} %get-tuple-element.26.v_ref), channel_id=1, source_target_pairs={{0,2},{1,3},{4,6},{5,7},{8,10},{9,11},{12,14},{13,15},{16,18},{17,... | collective-permute-start | bytes 1572872 | tf_op jit(solution)/shard_map/ppermute | solution.py:163
  77.7 1.3 %collective-permute-start.11 = (f32[16,64,128]{2,1,0:T(8,128)}, f32[16,64,128]{2,1,0:T(8,128)}, u32[]{:S(2)}, u32[]{:S(2)}) collective-permute-start(f32[16,64,128]{2,1,0:T(8,128)} %get-tuple-element.24.refs_0_), channel_id=1, source_target_pairs={{2,4},{3,5},{6,8},{7,9},{10,12},{11,13},{14,16},{15,17},{18,20},{1... | collective-permute-start | bytes 1572872 | tf_op jit(solution)/shard_map/ppermute | solution.py:163
  79.0 0.8 constant_dynamic-slice_fusion
  79.7 1.9 %collective-permute-start.9 = (f32[1,64,128]{2,1,0:T(8,128)S(1)}, f32[1,64,128]{2,1,0:T(8,128)S(1)}, u32[]{:S(2)}, u32[]{:S(2)}) collective-permute-start(f32[1,64,128]{2,1,0:T(8,128)S(1)} %constant_dynamic-slice_fusion), channel_id=1, source_target_pairs={{0,1},{1,0},{2,3},{3,2},{4,5},{5,4},{6,7},{7,6},{8,9},{9,8},{10,11... | collective-permute-start | bytes 98312 | tf_op jit(solution)/shard_map/ppermute | solution.py:163
  81.6 3.9 %collective-permute-done.9.h_ref = f32[1,64,128]{2,1,0:T(8,128)S(1)} collective-permute-done((f32[1,64,128]{2,1,0:T(8,128)S(1)}, f32[1,64,128]{2,1,0:T(8,128)S(1)}, u32[]{:S(2)}, u32[]{:S(2)}) %collective-permute-start.9) | collective-permute-done | bytes 32800 | tf_op jit(solution)/shard_map/ppermute | solution.py:163
  85.5 1.0 %copy-done.5 = f32[16,64,128]{2,1,0:T(8,128)S(1)} copy-done((f32[16,64,128]{2,1,0:T(8,128)S(1)}, f32[16,64,128]{2,1,0:T(8,128)}, u32[]{:S(2)}) %copy-start.5) | copy-done | bytes 524312
  86.6 1.0 %copy-done.7 = f32[16,64,128]{2,1,0:T(8,128)S(1)} copy-done((f32[16,64,128]{2,1,0:T(8,128)S(1)}, f32[16,64,128]{2,1,0:T(8,128)}, u32[]{:S(2)}) %copy-start.7) | copy-done | bytes 524312
  87.6 0.9 shard_map.64
  88.5 0.0 collective-permute-done.10
  88.5 11.2 %collective-permute-done.11 = f32[16,64,128]{2,1,0:T(8,128)} collective-permute-done((f32[16,64,128]{2,1,0:T(8,128)}, f32[16,64,128]{2,1,0:T(8,128)}, u32[]{:S(2)}, u32[]{:S(2)}) %collective-permute-start.11) | collective-permute-done | bytes 524320 | tf_op jit(solution)/shard_map/ppermute | solution.py:163
  99.8 2.1 %add_bitcast_fusion = f32[1,16,64,128]{3,2,1,0:T(8,128)} fusion(f32[16,64,128]{2,1,0:T(8,128)S(1)} %shard_map.64, f32[16,64,128]{2,1,0:T(8,128)} %collective-permute-done.10, f32[16,64,128]{2,1,0:T(8,128)} %collective-permute-done.11), kind=kLoop, calls=%fused_computation.1 | loop fusion | flops 262144 | bytes 2097152 | tf_op jit(solution)/shard_map/broadcast_in_dim | solution.py:217
  (9 shorter events, 0.1 us)
Async XLA Ops:
  4.4 31.0 %collective-permute-start = (f32[19,64,128]{2,1,0:T(8,128)S(1)}, f32[19,64,128]{2,1,0:T(8,128)S(1)}, u32[]{:S(2)}, u32[]{:S(2)}) collective-permute-start(f32[19,64,128]{2,1,0:T(8,128)S(1)} %pad_maximum_fusion), channel_id=1, source_target_pairs={{0,1},{1,0},{2,3},{3,2},{4,5},{5,4},{6,7},{7,6},{8,9},{9,8},{10,11... | collective-permute-start | bytes 1867784 | tf_op jit(solution)/shard_map/ppermute | solution.py:163
  11.3 30.2 %collective-permute-start.1 = (f32[16,64,128]{2,1,0:T(8,128)}, f32[16,64,128]{2,1,0:T(8,128)}, u32[]{:S(2)}, u32[]{:S(2)}) collective-permute-start(f32[16,64,128]{2,1,0:T(8,128)} %bitcast.2.refs_0_.refs_1_), channel_id=1, source_target_pairs={{0,2},{1,3},{4,6},{5,7},{8,10},{9,11},{12,14},{13,15},{16,18},{17,... | collective-permute-start | bytes 1572872 | tf_op jit(solution)/shard_map/ppermute | solution.py:163
  13.4 30.0 %collective-permute-start.3 = (f32[16,64,128]{2,1,0:T(8,128)}, f32[16,64,128]{2,1,0:T(8,128)}, u32[]{:S(2)}, u32[]{:S(2)}) collective-permute-start(f32[16,64,128]{2,1,0:T(8,128)} %bitcast.2.refs_0_.refs_1_), channel_id=1, source_target_pairs={{2,4},{3,5},{6,8},{7,9},{10,12},{11,13},{14,16},{15,17},{18,20},{1... | collective-permute-start | bytes 1572872 | tf_op jit(solution)/shard_map/ppermute | solution.py:163
  15.6 25.9 %collective-permute-start.2 = (f32[3,64,128]{2,1,0:T(8,128)S(1)}, f32[3,64,128]{2,1,0:T(8,128)S(1)}, u32[]{:S(2)}, u32[]{:S(2)}) collective-permute-start(f32[3,64,128]{2,1,0:T(8,128)S(1)} %dynamic-slice_bitcast_fusion.1), channel_id=1, source_target_pairs={{0,3},{1,2},{4,7},{5,6},{8,11},{9,10},{12,15},{13,14},{16,19},{17,... | collective-permute-start | bytes 294920 | tf_op jit(solution)/shard_map/ppermute | solution.py:163
  17.6 23.9 %copy-start = (f32[1,16,64,128]{3,2,1,0:T(8,128)S(1)}, f32[1,16,64,128]{3,2,1,0:T(8,128)}, u32[]{:S(2)}) copy-start(f32[1,16,64,128]{3,2,1,0:T(8,128)} %param.5) | copy-start | bytes 1572868
  35.4 0.9 copy-start.2
  36.3 1.4 %copy-start.1 = (f32[3,16,64,128]{3,2,1,0:T(8,128)S(1)}, f32[3,16,64,128]{3,2,1,0:T(8,128)}, u32[]{:S(2)}) copy-start(f32[3,16,64,128]{3,2,1,0:T(8,128)} %upwind_ref.1) | copy-start | bytes 4718596
  37.7 1.1 %copy-start.3 = (f32[19,64,128]{2,1,0:T(8,128)S(1)}, f32[19,64,128]{2,1,0:T(8,128)}, u32[]{:S(2)}) copy-start(f32[19,64,128]{2,1,0:T(8,128)} %copy-done.2) | copy-start | bytes 1867780
  38.8 1.0 %copy-start.4 = (f32[16,64,128]{2,1,0:T(8,128)S(1)}, f32[16,64,128]{2,1,0:T(8,128)}, u32[]{:S(2)}) copy-start(f32[16,64,128]{2,1,0:T(8,128)} %spread_ref.1) | copy-start | bytes 1572868
  40.7 0.8 copy-start.6
  46.3 9.5 %collective-permute-start.5 = (f32[16,64,128]{2,1,0:T(8,128)S(1)}, f32[16,64,128]{2,1,0:T(8,128)S(1)}, u32[]{:S(2)}, u32[]{:S(2)}) collective-permute-start(f32[16,64,128]{2,1,0:T(8,128)S(1)} %get-tuple-element.21.refs_0_.refs_1_), channel_id=1, source_target_pairs={{0,2},{1,3},{4,6},{5,7},{8,10},{9,11},{12,14},{13,15},{16,18},{17,... | collective-permute-start | bytes 1572872 | tf_op jit(solution)/shard_map/ppermute | solution.py:163
  47.6 24.3 %collective-permute-start.7 = (f32[16,64,128]{2,1,0:T(8,128)S(1)}, f32[16,64,128]{2,1,0:T(8,128)S(1)}, u32[]{:S(2)}, u32[]{:S(2)}) collective-permute-start(f32[16,64,128]{2,1,0:T(8,128)S(1)} %get-tuple-element.20.refs_0_), channel_id=1, source_target_pairs={{2,4},{3,5},{6,8},{7,9},{10,12},{11,13},{14,16},{15,17},{18,20},{1... | collective-permute-start | bytes 1572872 | tf_op jit(solution)/shard_map/ppermute | solution.py:163
  48.9 6.9 %collective-permute-start.4 = (f32[4,64,128]{2,1,0:T(8,128)S(1)}, f32[4,64,128]{2,1,0:T(8,128)S(1)}, u32[]{:S(2)}, u32[]{:S(2)}) collective-permute-start(f32[4,64,128]{2,1,0:T(8,128)S(1)} %get-tuple-element.22), channel_id=1, source_target_pairs={{0,1},{1,0},{2,3},{3,2},{4,5},{5,4},{6,7},{7,6},{8,9},{9,8},{10,11... | collective-permute-start | bytes 393224 | tf_op jit(solution)/shard_map/ppermute | solution.py:163
  50.8 3.5 %collective-permute-start.6 = (f32[3,64,128]{2,1,0:T(8,128)S(1)}, f32[3,64,128]{2,1,0:T(8,128)S(1)}, u32[]{:S(2)}, u32[]{:S(2)}) collective-permute-start(f32[3,64,128]{2,1,0:T(8,128)S(1)} %get-tuple-element.23), channel_id=1, source_target_pairs={{0,3},{1,2},{4,7},{5,6},{8,11},{9,10},{12,15},{13,14},{16,19},{17,... | collective-permute-start | bytes 294920 | tf_op jit(solution)/shard_map/ppermute | solution.py:163
  52.1 19.8 %collective-permute-start.8 = (f32[3,64,128]{2,1,0:T(8,128)S(1)}, f32[3,64,128]{2,1,0:T(8,128)S(1)}, u32[]{:S(2)}, u32[]{:S(2)}) collective-permute-start(f32[3,64,128]{2,1,0:T(8,128)S(1)} %get-tuple-element.25), channel_id=1, source_target_pairs={{2,5},{3,4},{6,9},{7,8},{10,13},{11,12},{14,17},{15,16},{18,21},{1... | collective-permute-start | bytes 294920 | tf_op jit(solution)/shard_map/ppermute | solution.py:163
  75.5 13.0 %collective-permute-start.10 = (f32[16,64,128]{2,1,0:T(8,128)}, f32[16,64,128]{2,1,0:T(8,128)}, u32[]{:S(2)}, u32[]{:S(2)}) collective-permute-start(f32[16,64,128]{2,1,0:T(8,128)} %get-tuple-element.26.v_ref), channel_id=1, source_target_pairs={{0,2},{1,3},{4,6},{5,7},{8,10},{9,11},{12,14},{13,15},{16,18},{17,... | collective-permute-start | bytes 1572872 | tf_op jit(solution)/shard_map/ppermute | solution.py:163
  77.7 22.1 %collective-permute-start.11 = (f32[16,64,128]{2,1,0:T(8,128)}, f32[16,64,128]{2,1,0:T(8,128)}, u32[]{:S(2)}, u32[]{:S(2)}) collective-permute-start(f32[16,64,128]{2,1,0:T(8,128)} %get-tuple-element.24.refs_0_), channel_id=1, source_target_pairs={{2,4},{3,5},{6,8},{7,9},{10,12},{11,13},{14,16},{15,17},{18,20},{1... | collective-permute-start | bytes 1572872 | tf_op jit(solution)/shard_map/ppermute | solution.py:163
  79.7 5.8 %collective-permute-start.9 = (f32[1,64,128]{2,1,0:T(8,128)S(1)}, f32[1,64,128]{2,1,0:T(8,128)S(1)}, u32[]{:S(2)}, u32[]{:S(2)}) collective-permute-start(f32[1,64,128]{2,1,0:T(8,128)S(1)} %constant_dynamic-slice_fusion), channel_id=1, source_target_pairs={{0,1},{1,0},{2,3},{3,2},{4,5},{5,4},{6,7},{7,6},{8,9},{9,8},{10,11... | collective-permute-start | bytes 98312 | tf_op jit(solution)/shard_map/ppermute | solution.py:163
  85.5 1.0 %copy-start.5 = (f32[16,64,128]{2,1,0:T(8,128)S(1)}, f32[16,64,128]{2,1,0:T(8,128)}, u32[]{:S(2)}) copy-start(f32[16,64,128]{2,1,0:T(8,128)} %get-tuple-element.26.v_ref) | copy-start | bytes 1572868
  86.6 1.0 %copy-start.7 = (f32[16,64,128]{2,1,0:T(8,128)S(1)}, f32[16,64,128]{2,1,0:T(8,128)}, u32[]{:S(2)}) copy-start(f32[16,64,128]{2,1,0:T(8,128)} %copy-done.6) | copy-start | bytes 1572868

commit v2 on v1

v2 whole, which is shorter than its diff:
```python
import functools

import jax
import jax.numpy as jnp
from jax import lax
from jax.experimental import pallas as pl
from jax.experimental.pallas import tpu as pltpu
from jax.sharding import PartitionSpec as P


ITERS = 4
THIN = ITERS - 1
F32 = jnp.float32
ROLE, SIDE = 0, 1
ROW, RUNS = 16, 4


def call(kernel, outs, scalars, *operands, far=(), scratch=(), aliases=None):
    far = [pltpu.with_memory_space_constraint(o, pltpu.HBM) for o in far]
    near = [pltpu.with_memory_space_constraint(o, pltpu.VMEM) for o in operands]
    return pl.pallas_call(
        kernel,
        out_shape=[o if not isinstance(o, tuple) else pltpu.VMEM(o, F32) for o in outs],
        in_specs=[pl.BlockSpec(memory_space=pltpu.SMEM)]
        + [pl.BlockSpec(memory_space=pltpu.HBM)] * len(far)
        + [pl.BlockSpec(memory_space=pltpu.VMEM)] * len(near),
        out_specs=[pl.BlockSpec(memory_space=pltpu.VMEM if isinstance(o, tuple) else pltpu.HBM) for o in outs],
        scratch_shapes=list(scratch),
        input_output_aliases=aliases or {},
        compiler_params=pltpu.CompilerParams(vmem_limit_bytes=16 * 1024 * 1024),
    )(scalars, *far, *near)


def pack_kernel(scal, init_ref, source_ref, spread_ref, upwind_ref, coef_out, field_out, thin_out, sem):
    side = scal[SIDE]
    depth = init_ref.shape[0]
    thin = pl.ds((1 - side) * (depth - THIN), THIN)
    wide = pl.ds((1 - side) * (depth - ITERS), ITERS)
    copies = [
        pltpu.make_async_copy(init_ref.at[wide], field_out.at[pl.ds(0, ITERS)], sem.at[0]),
        pltpu.make_async_copy(source_ref.at[thin], field_out.at[pl.ds(ITERS, THIN)], sem.at[1]),
        pltpu.make_async_copy(init_ref.at[thin], thin_out, sem.at[6]),
        pltpu.make_async_copy(spread_ref.at[thin], coef_out.at[pl.ds(0, THIN)], sem.at[2]),
    ]
    for i in range(3):
        copies.append(pltpu.make_async_copy(upwind_ref.at[i, thin], coef_out.at[pl.ds((1 + i) * THIN, THIN)], sem.at[3 + i]))
    for copy in copies:
        copy.start()
    for copy in copies:
        copy.wait()


def weights(spread, ux, uy, uz, at, refs):
    c_ref, x_ref, y_ref, z_ref, inv_ref = refs
    nx, ny = spread.shape
    row = lax.broadcasted_iota(jnp.int32, (nx, ny), 0)
    lane = lax.broadcasted_iota(jnp.int32, (nx, ny), 1)
    diagonal = 1.0 + 6.0 * spread + (ux + uy + uz)
    inv = 1.0 / diagonal
    c_ref[at] = spread * inv
    x_ref[at] = jnp.where(row == 0, 0.0, (spread + ux) * inv)
    y_ref[at] = jnp.where(lane == 0, 0.0, (spread + uy) * inv)
    z_ref[at] = (spread + uz) * inv
    inv_ref[at] = inv
    return diagonal


def own_kernel(scal, init_far, source_far, spread_far, upwind_far, c_ref, x_ref, y_ref, z_ref, inv_ref, diag_ref, init_ref, source_ref, spread_ref, upwind_ref, sem):
    side = scal[SIDE]
    depth = init_far.shape[0]
    copies = [
        pltpu.make_async_copy(spread_far, spread_ref, sem.at[0]),
        pltpu.make_async_copy(upwind_far, upwind_ref, sem.at[1]),
        pltpu.make_async_copy(init_far, init_ref, sem.at[2]),
        pltpu.make_async_copy(source_far, source_ref, sem.at[3]),
    ]
    for copy in copies:
        copy.start()
    for copy in copies[:2]:
        copy.wait()

    def own(z, carry):
        diag_ref[z] = weights(
            spread_ref[z], upwind_ref[0, z], upwind_ref[1, z], upwind_ref[2, z], ITERS * side + z, (c_ref, x_ref, y_ref, z_ref, inv_ref)
        )
        return carry

    lax.fori_loop(0, depth, own, 0, unroll=2)
    for copy in copies[2:]:
        copy.wait()


def rim_kernel(scal, first_ref, second_ref, *refs):
    side = scal[SIDE]
    outs = refs[5:]
    depth = outs[0].shape[0] - ITERS
    for q in range(THIN):
        at = jnp.where(side == 1, 1 + q, depth + q)
        parts = [first_ref[i * THIN + q] + second_ref[i * THIN + q] for i in range(4)]
        weights(*parts, at, outs)


def stencil(below, here, above, c, cx, cy, cz, row_last, lane_last):
    nx, ny = here.shape
    low_x = pltpu.roll(here, 1, 0)
    high_x = jnp.where(row_last, 0.0, pltpu.roll(here, nx - 1, 0))
    low_y = pltpu.roll(here, 1, 1)
    high_y = jnp.where(lane_last, 0.0, pltpu.roll(here, ny - 1, 1))
    return c * ((above + high_x) + high_y) + (cx * low_x + cz * below) + cy * low_y


def last_masks(nx, ny):
    row = lax.broadcasted_iota(jnp.int32, (nx, ny), 0)
    lane = lax.broadcasted_iota(jnp.int32, (nx, ny), 1)
    return row == nx - 1, lane == ny - 1


def sweep_kernel(role, pass_on, widths, scal, *refs):
    if pass_on:
        other_ref, *refs = refs
    count = len(refs) - len(widths) - 3
    edge_refs = refs[count : count + len(widths)]
    refs = refs[:count] + refs[count + len(widths) :]
    (v_ref, vh_ref, s_ref, rim_ref, p_ref, ph_ref, c_ref, x_ref, y_ref, z_ref, inv_ref, out_ref, va, vb, g) = refs
    side = scal[SIDE]
    depth, nx, ny = v_ref.shape

    @pl.when(scal[ROLE] == role)
    def _():
        row_last, lane_last = last_masks(nx, ny)
        zero = jnp.zeros((nx, ny), F32)
        for buf in (va, vb):
            buf[0] = zero
            buf[depth + ITERS + 1] = zero

        def fill(z, carry):
            at = ITERS * side + z
            va[1 + at] = v_ref[z]
            g[at] = (s_ref[z] + p_ref[z]) * inv_ref[at]
            return carry

        lax.fori_loop(0, depth, fill, 0, unroll=4)
        for q in range(ITERS):
            va[1 + jnp.where(side == 1, q, depth + q)] = vh_ref[q]
        for q in range(THIN):
            at = jnp.where(side == 1, 1 + q, depth + q)
            g[at] = (rim_ref[ITERS + q] + ph_ref[q]) * inv_ref[at]
        src, dst = va, vb
        for k in range(ITERS):
            start = side * (1 + k)
            last = k == ITERS - 1

            def layer(j, carry, src=src, dst=dst, start=start, last=last):
                e = start + j
                new = g[e] + stencil(
                    src[e], src[e + 1], src[e + 2], c_ref[e], x_ref[e], y_ref[e], z_ref[e], row_last, lane_last
                )
                if last:
                    out_ref[j] = new
                else:
                    dst[e + 1] = new
                return carry

            count = depth + ITERS - 1 - k
            lax.fori_loop(0, count, layer, 0, unroll=True)
            src, dst = dst, src

    if pass_on:

        @pl.when(scal[ROLE] != role)
        def _():
            out_ref[...] = other_ref[...]

    for width, edge_ref in zip(widths, edge_refs):
        for q in range(width):
            edge_ref[q] = out_ref[jnp.where(side == 1, q, depth - width + q)]


def defect_kernel(scal, v_ref, h_ref, s_ref, c_ref, x_ref, y_ref, z_ref, diag_ref, out_ref, far_out, va, sem):
    side = scal[SIDE]
    depth, nx, ny = v_ref.shape
    copy = pltpu.make_async_copy(v_ref, far_out, sem)
    copy.start()
    row_last, lane_last = last_masks(nx, ny)
    zero = jnp.zeros((nx, ny), F32)
    va[0] = jnp.where(side == 1, h_ref[0], zero)
    va[depth + 1] = jnp.where(side == 1, zero, h_ref[0])
    for z in range(depth):
        va[1 + z] = v_ref[z]

    def layer(z, carry):
        e = ITERS * side + z
        here = va[1 + z]
        m = stencil(va[z], here, va[z + 2], c_ref[e], x_ref[e], y_ref[e], z_ref[e], row_last, lane_last)
        out_ref[z] = s_ref[z] - diag_ref[z] * (here - m)
        return carry

    lax.fori_loop(0, depth, layer, 0, unroll=True)
    copy.wait()


def add_kernel(scal, a_ref, b_ref, c_ref, far_out, out_ref, sem):
    pieces = sem.shape[0]
    size = out_ref.shape[0] // pieces
    copies = []
    for i in range(pieces):
        part = pl.ds(i * size, size)
        out_ref[part] = a_ref[part] + (b_ref[part] + c_ref[part])
        copies.append(pltpu.make_async_copy(out_ref.at[part], far_out.at[part], sem.at[i]))
        copies[-1].start()
    for copy in copies:
        copy.wait()


def body(initial, source, diffusion, advection):
    tm, space = (lax.axis_size("tm"), lax.axis_size("space"))
    role = lax.axis_index("tm") % 2
    side = lax.axis_index("space")
    scalars = jnp.stack([role, side]).astype(jnp.int32)
    shape = initial.shape[1:]
    depth = shape[0]
    initial, source = (initial[0], source[0])

    def number(t, s):
        return (t % tm) * space + s

    def permute(value, pairs):
        return lax.ppermute(value, ("tm", "space"), pairs)

    sides = range(space)
    stride, group = ROW, ROW * RUNS
    even, odd = range(0, tm, 2), range(1, tm, 2)
    into_odd = [(number(t, s), number(t + 1, s)) for t in even for s in sides]
    into_even = [(number(t, s), number(t + 1, s)) for t in odd for s in sides]
    across_even = [(number(t, s), number(t, 1 - s)) for t in even for s in sides]
    across_odd = [(number(t, s), number(t, 1 - s)) for t in odd for s in sides]
    odd_across = [(number(t, s), number(t + 1, 1 - s)) for t in even for s in sides]
    even_across = [(number(t, s), number(t + 1, 1 - s)) for t in odd for s in sides]
    lower_odd = [(number(t, 1), number(t, 0)) for t in odd]
    lower_odd += [(number(t, 0), number(t - stride if t % group >= stride else t - stride + group, 1)) for t in odd]
    back = [(number(t, s), number(t - 1, s)) for t in odd for s in sides]

    plane = shape[1:]
    ext = (depth + ITERS,) + plane
    padded = (depth + ITERS + 2,) + plane
    scratch = [pltpu.VMEM(padded, F32), pltpu.VMEM(padded, F32), pltpu.VMEM(ext, F32)]
    thin = (THIN,) + plane
    far = (initial, source, diffusion, advection)

    coef_edge, field_edge, thin_edge = call(
        pack_kernel, [(4 * THIN,) + plane, (ITERS + THIN,) + plane, thin], scalars, far=far, scratch=[pltpu.SemaphoreType.DMA((7,))]
    )
    sc = permute(coef_edge, lower_odd)
    b1 = permute(initial, into_even)
    rim = permute(field_edge, across_even + across_odd)
    d1 = permute(thin_edge, odd_across + even_across)
    a1 = permute(initial, into_odd)
    *coefs, diag, initial_near, source_near = call(
        own_kernel,
        [ext] * 5 + [shape] * 3,
        scalars,
        far=far,
        scratch=[pltpu.VMEM(shape, F32), pltpu.VMEM((3,) + shape, F32), pltpu.SemaphoreType.DMA((4,))],
    )
    ac = permute(sc, back)
    coefs = call(rim_kernel, [ext] * 5, scalars, sc, ac, *coefs, aliases={3 + i: i for i in range(5)})

    def sweep(mine, other, v, vh, p, ph, widths):
        outs = [shape] + [(w,) + plane for w in widths]
        extra = [other] if other is not None else []
        kernel = functools.partial(sweep_kernel, mine, other is not None, widths)
        return call(kernel, outs, scalars, *extra, v, vh, source_near, rim, p, ph, *coefs, scratch=scratch)

    x, xw, xt = sweep(1, None, initial_near, rim, a1, d1, (ITERS, THIN))
    b2 = permute(x, into_even)
    sx = permute(xw, across_odd)
    dx = permute(xt, even_across)
    s1, yw, yt = sweep(0, x, initial_near, rim, b1, d1, (ITERS, THIN))
    dy = permute(yt, odd_across)
    a2 = permute(s1, into_odd)
    sy = permute(yw, across_even)
    (z,) = sweep(1, None, s1, sx, a2, dy, ())
    b3 = permute(z, into_even)
    s2, s2w = sweep(0, z, s1, sy, b2, dx, (1,))
    a3 = permute(s2, into_odd)
    s2h = permute(s2w, across_even + across_odd)
    defect, s2_far = call(
        defect_kernel,
        [shape, pltpu.HBM(shape, F32)],
        scalars,
        s2,
        s2h,
        source_near,
        *coefs[:4],
        diag,
        scratch=[pltpu.VMEM((depth + 2,) + plane, F32), pltpu.SemaphoreType.DMA],
    )
    (residual,) = call(
        add_kernel, [pltpu.HBM(shape, F32)], scalars, defect, a3, b3, scratch=[pltpu.VMEM(shape, F32), pltpu.SemaphoreType.DMA((4,))]
    )
    return (s2_far[None], residual[None])


def solution(mesh):
    in_specs = (
        P("tm", "space", None, None),
        P("tm", "space", None, None),
        P("space", None, None),
        P(None, "space", None, None),
    )
    out_specs = (P("tm", "space", None, None), P("tm", "space", None, None))
    return jax.shard_map(body, mesh=mesh, in_specs=in_specs, out_specs=out_specs, check_vma=False)
```

time: 103 us -> 92.6 us (0.90)
  the two profiles are of different devices: /device:TPU:64 before, /device:TPU:6 now
where the time goes in v2:
time: 92.6 us; the launch traced here: 91.7 us
  starting transfers between devices  38.6 us (42%)
  waiting for transfers between devices  38.6 us (42%)
  Pallas kernels  13.5 us (15%)
    ppermute x15, waiting for transfers between devices, permute(): return lax.ppermute(value, ('tm', 'space'), pairs)  38.6 us
    ppermute x15, starting transfers between devices, permute(): return lax.ppermute(value, ('tm', 'space'), pairs)  38.6 us
    pallas_call x9, Pallas kernels, call(): pl.pallas_call(kernel, out_shape=[o if not isinstance(o, tuple) else pltp...  13.5 us
  transfers between devices with their start and end apart: 15, of which 5 were waited for; matrix products, arithmetic and copies ran while one was open for 0% of the time, Pallas kernels for 6%

profile of v2, /device:TPU:6, one launch (start us, length us, event | category | flops | bytes accessed | tf_op | source)
XLA Modules:
  0.0 91.7 jit_solution(9750110198006099021)
XLA Ops:
  0.6 0.1 pad_add_fusion.scal
  0.7 0.0 copy-start
  0.7 1.8 %shard_map.60 = (f32[12,64,128]{2,1,0:T(8,128)S(1)}, f32[7,64,128]{2,1,0:T(8,128)S(1)}, f32[3,64,128]{2,1,0:T(8,128)S(1)}) custom-call(s32[2]{0:T(128)S(1)} %pad_add_fusion.scal, f32[16,64,128]{2,1,0:T(8,128)} %bitcast.8, f32[16,64,128]{2,1,0:T(8,128)} %bitcast.6, f32[16,64,128]{2,1,0:T(8,128)} %spread_ref.1, f32[3,16,64,128]{3,2,1,0:T(8,128)} %upwind_ref.1), custom_call_target="tpu_custom_call" | custom-call | tf_op jit(solution)/shard_map/pallas_call | solution.py:21
  2.5 0.7 collective-permute-start.3
  3.2 0.0 copy-done
  3.2 11.8 %collective-permute-start.1 = (f32[16,64,128]{2,1,0:T(8,128)S(1)}, f32[16,64,128]{2,1,0:T(8,128)S(1)}, u32[]{:S(2)}, u32[]{:S(2)}) collective-permute-start(f32[16,64,128]{2,1,0:T(8,128)S(1)} %bitcast.10), channel_id=1, source_target_pairs={{0,2},{1,3},{4,6},{5,7},{8,10},{9,11},{12,14},{13,15},{16,18},{17,... | collective-permute-start | bytes 1572872 | tf_op jit(solution)/shard_map/ppermute | solution.py:228
  15.0 1.3 %collective-permute-start.5 = (f32[16,64,128]{2,1,0:T(8,128)S(1)}, f32[16,64,128]{2,1,0:T(8,128)S(1)}, u32[]{:S(2)}, u32[]{:S(2)}) collective-permute-start(f32[16,64,128]{2,1,0:T(8,128)S(1)} %bitcast.11), channel_id=1, source_target_pairs={{2,4},{3,5},{6,8},{7,9},{10,12},{11,13},{14,16},{15,17},{18,20},{1... | collective-permute-start | bytes 1572872 | tf_op jit(solution)/shard_map/ppermute | solution.py:228
  16.3 0.0 collective-permute-done.3.first_ref
  16.3 1.3 %collective-permute-start.4 = (f32[12,64,128]{2,1,0:T(8,128)S(1)}, f32[12,64,128]{2,1,0:T(8,128)S(1)}, u32[]{:S(2)}, u32[]{:S(2)}) collective-permute-start(f32[12,64,128]{2,1,0:T(8,128)S(1)} %collective-permute-done.3.first_ref), channel_id=1, source_target_pairs={{2,0},{3,1},{6,4},{7,5},{10,8},{11,9},{14,12},{15,13},{18,16},{19,... | collective-permute-start | bytes 1179656 | tf_op jit(solution)/shard_map/ppermute | solution.py:228
  17.6 1.9 %collective-permute-start = (f32[7,64,128]{2,1,0:T(8,128)S(1)}, f32[7,64,128]{2,1,0:T(8,128)S(1)}, u32[]{:S(2)}, u32[]{:S(2)}) collective-permute-start(f32[7,64,128]{2,1,0:T(8,128)S(1)} %get-tuple-element.29), channel_id=1, source_target_pairs={{0,1},{1,0},{4,5},{5,4},{8,9},{9,8},{12,13},{13,12},{16,17},{17,16... | collective-permute-start | bytes 688136 | tf_op jit(solution)/shard_map/ppermute | solution.py:228
  19.5 5.6 %collective-permute-start.2 = (f32[3,64,128]{2,1,0:T(8,128)S(1)}, f32[3,64,128]{2,1,0:T(8,128)S(1)}, u32[]{:S(2)}, u32[]{:S(2)}) collective-permute-start(f32[3,64,128]{2,1,0:T(8,128)S(1)} %get-tuple-element.31), channel_id=1, source_target_pairs={{0,3},{1,2},{4,7},{5,6},{8,11},{9,10},{12,15},{13,14},{16,19},{17,... | collective-permute-start | bytes 294920 | tf_op jit(solution)/shard_map/ppermute | solution.py:228
  25.1 2.5 %shard_map.59 = (f32[20,64,128]{2,1,0:T(8,128)S(1)}, f32[20,64,128]{2,1,0:T(8,128)S(1)}, f32[20,64,128]{2,1,0:T(8,128)S(1)}, f32[20,64,128]{2,1,0:T(8,128)S(1)},...) custom-call(s32[2]{0:T(128)S(1)} %pad_add_fusion.scal, ...), custom_call_target="tpu_custom_call" | custom-call | tf_op jit(solution)/shard_map/pallas_call | solution.py:21
  27.6 0.0 collective-permute-done.4.second_ref
  27.6 0.6 shard_map.61
  28.2 10.0 %collective-permute-done.2.refs_5_.refs_6_ = f32[3,64,128]{2,1,0:T(8,128)S(1)} collective-permute-done((f32[3,64,128]{2,1,0:T(8,128)S(1)}, f32[3,64,128]{2,1,0:T(8,128)S(1)}, u32[]{:S(2)}, u32[]{:S(2)}) %collective-permute-start.2) | collective-permute-done | bytes 98336 | tf_op jit(solution)/shard_map/ppermute | solution.py:228
  38.2 0.0 collective-permute-done.refs_1_.refs_3_.refs_2_.refs_4_
  38.2 0.0 collective-permute-done.1.refs_4_
  38.2 0.6 shard_map.62
  38.8 0.0 collective-permute-done.5.refs_5_
  38.8 2.4 %shard_map.63 = (f32[16,64,128]{2,1,0:T(8,128)S(1)}, f32[4,64,128]{2,1,0:T(8,128)S(1)}, f32[3,64,128]{2,1,0:T(8,128)S(1)}) custom-call(s32[2]{0:T(128)S(1)} %pad_add_fusion.scal, f32[16,64,128]{2,1,0:T(8,128)S(1)} %get-tuple-element.43.refs_0_, f32[16,64,128]{2,1,0:T(8,128)S(1)} %get-tuple-element.28.refs_0_.refs_1_, ...), custom_call_target="tpu_custom_call" | custom-call | tf_op jit(solution)/shard_map/pallas_call | solution.py:21
  41.2 1.3 %collective-permute-start.7 = (f32[16,64,128]{2,1,0:T(8,128)S(1)}, f32[16,64,128]{2,1,0:T(8,128)S(1)}, u32[]{:S(2)}, u32[]{:S(2)}) collective-permute-start(f32[16,64,128]{2,1,0:T(8,128)S(1)} %get-tuple-element.44.refs_0_.refs_1_), channel_id=1, source_target_pairs={{0,2},{1,3},{4,6},{5,7},{8,10},{9,11},{12,14},{13,15},{16,18},{17,... | collective-permute-start | bytes 1572872 | tf_op jit(solution)/shard_map/ppermute | solution.py:228
  42.6 1.3 %collective-permute-start.10 = (f32[16,64,128]{2,1,0:T(8,128)S(1)}, f32[16,64,128]{2,1,0:T(8,128)S(1)}, u32[]{:S(2)}, u32[]{:S(2)}) collective-permute-start(f32[16,64,128]{2,1,0:T(8,128)S(1)} %get-tuple-element.43.refs_0_), channel_id=1, source_target_pairs={{2,4},{3,5},{6,8},{7,9},{10,12},{11,13},{14,16},{15,17},{18,20},{1... | collective-permute-start | bytes 1572872 | tf_op jit(solution)/shard_map/ppermute | solution.py:228
  43.9 3.8 %collective-permute-start.8 = (f32[3,64,128]{2,1,0:T(8,128)S(1)}, f32[3,64,128]{2,1,0:T(8,128)S(1)}, u32[]{:S(2)}, u32[]{:S(2)}) collective-permute-start(f32[3,64,128]{2,1,0:T(8,128)S(1)} %get-tuple-element.46), channel_id=1, source_target_pairs={{0,3},{1,2},{4,7},{5,6},{8,11},{9,10},{12,15},{13,14},{16,19},{17,... | collective-permute-start | bytes 294920 | tf_op jit(solution)/shard_map/ppermute | solution.py:228
  47.7 0.7 collective-permute-start.6
  48.4 2.3 %collective-permute-start.9 = (f32[4,64,128]{2,1,0:T(8,128)S(1)}, f32[4,64,128]{2,1,0:T(8,128)S(1)}, u32[]{:S(2)}, u32[]{:S(2)}) collective-permute-start(f32[4,64,128]{2,1,0:T(8,128)S(1)} %get-tuple-element.47), channel_id=1, source_target_pairs={{0,1},{1,0},{4,5},{5,4},{8,9},{9,8},{12,13},{13,12},{16,17},{17,16... | collective-permute-start | bytes 393224 | tf_op jit(solution)/shard_map/ppermute | solution.py:228
  50.7 1.1 %collective-permute-done.8.refs_5_ = f32[3,64,128]{2,1,0:T(8,128)S(1)} collective-permute-done((f32[3,64,128]{2,1,0:T(8,128)S(1)}, f32[3,64,128]{2,1,0:T(8,128)S(1)}, u32[]{:S(2)}, u32[]{:S(2)}) %collective-permute-start.8) | collective-permute-done | bytes 98336 | tf_op jit(solution)/shard_map/ppermute | solution.py:228
  51.8 1.3 %collective-permute-start.11 = (f32[3,64,128]{2,1,0:T(8,128)S(1)}, f32[3,64,128]{2,1,0:T(8,128)S(1)}, u32[]{:S(2)}, u32[]{:S(2)}) collective-permute-start(f32[3,64,128]{2,1,0:T(8,128)S(1)} %get-tuple-element.48), channel_id=1, source_target_pairs={{2,5},{3,4},{6,9},{7,8},{10,13},{11,12},{14,17},{15,16},{18,21},{1... | collective-permute-start | bytes 294920 | tf_op jit(solution)/shard_map/ppermute | solution.py:228
  53.1 0.0 collective-permute-done.6.refs_1_
  53.1 0.0 collective-permute-done.7.refs_4_
  53.1 0.6 shard_map.64.refs_0_
  53.6 12.4 %collective-permute-done.11.refs_6_ = f32[3,64,128]{2,1,0:T(8,128)S(1)} collective-permute-done((f32[3,64,128]{2,1,0:T(8,128)S(1)}, f32[3,64,128]{2,1,0:T(8,128)S(1)}, u32[]{:S(2)}, u32[]{:S(2)}) %collective-permute-start.11) | collective-permute-done | bytes 98336 | tf_op jit(solution)/shard_map/ppermute | solution.py:228
  66.0 0.0 collective-permute-done.9.refs_2_
  66.0 0.0 collective-permute-done.10.refs_5_
  66.0 2.4 %shard_map.65 = (f32[16,64,128]{2,1,0:T(8,128)S(1)}, f32[1,64,128]{2,1,0:T(8,128)S(1)}) custom-call(s32[2]{0:T(128)S(1)} %pad_add_fusion.scal, f32[16,64,128]{2,1,0:T(8,128)S(1)} %shard_map.64.refs_0_, f32[16,64,128]{2,1,0:T(8,128)S(1)} %get-tuple-element.44.refs_0_.refs_1_, f32[4,64,128]{2,1,0:T(8,128)S(1)} %collective-permute-done.9.refs_2_, ...), custom_call_target="tpu_custom_call" | custom-call | tf_op jit(solution)/shard_map/pallas_call | solution.py:21
  68.4 1.3 %collective-permute-start.13 = (f32[16,64,128]{2,1,0:T(8,128)S(1)}, f32[16,64,128]{2,1,0:T(8,128)S(1)}, u32[]{:S(2)}, u32[]{:S(2)}) collective-permute-start(f32[16,64,128]{2,1,0:T(8,128)S(1)} %get-tuple-element.49.v_ref), channel_id=1, source_target_pairs={{0,2},{1,3},{4,6},{5,7},{8,10},{9,11},{12,14},{13,15},{16,18},{17,... | collective-permute-start | bytes 1572872 | tf_op jit(solution)/shard_map/ppermute | solution.py:228
  69.8 1.3 %collective-permute-start.14 = (f32[16,64,128]{2,1,0:T(8,128)S(1)}, f32[16,64,128]{2,1,0:T(8,128)S(1)}, u32[]{:S(2)}, u32[]{:S(2)}) collective-permute-start(f32[16,64,128]{2,1,0:T(8,128)S(1)} %shard_map.64.refs_0_), channel_id=1, source_target_pairs={{2,4},{3,5},{6,8},{7,9},{10,12},{11,13},{14,16},{15,17},{18,20},{1... | collective-permute-start | bytes 1572872 | tf_op jit(solution)/shard_map/ppermute | solution.py:228
  71.1 2.7 %collective-permute-start.12 = (f32[1,64,128]{2,1,0:T(8,128)S(1)}, f32[1,64,128]{2,1,0:T(8,128)S(1)}, u32[]{:S(2)}, u32[]{:S(2)}) collective-permute-start(f32[1,64,128]{2,1,0:T(8,128)S(1)} %get-tuple-element.50), channel_id=1, source_target_pairs={{0,1},{1,0},{4,5},{5,4},{8,9},{9,8},{12,13},{13,12},{16,17},{17,16... | collective-permute-start | bytes 98312 | tf_op jit(solution)/shard_map/ppermute | solution.py:228
  73.8 3.1 %collective-permute-done.12.h_ref = f32[1,64,128]{2,1,0:T(8,128)S(1)} collective-permute-done((f32[1,64,128]{2,1,0:T(8,128)S(1)}, f32[1,64,128]{2,1,0:T(8,128)S(1)}, u32[]{:S(2)}, u32[]{:S(2)}) %collective-permute-start.12) | collective-permute-done | bytes 32800 | tf_op jit(solution)/shard_map/ppermute | solution.py:228
  76.9 1.3 %shard_map.66 = (f32[16,64,128]{2,1,0:T(8,128)S(1)}, f32[16,64,128]{2,1,0:T(8,128)}) custom-call(s32[2]{0:T(128)S(1)} %pad_add_fusion.scal, f32[16,64,128]{2,1,0:T(8,128)S(1)} %get-tuple-element.49.v_ref, f32[1,64,128]{2,1,0:T(8,128)S(1)} %collective-permute-done.12.h_ref, f32[16,64,128]{2,1,0:T(8,128)S(1)} %get-tuple-element.30.refs_2_.refs_3_.s_ref, ...), custom_call_target="tpu_custom_call" | custom-call | tf_op jit(solution)/shard_map/pallas_call | solution.py:21
  78.2 0.0 collective-permute-done.13.b_ref
  78.2 12.1 %collective-permute-done.14.c_ref = f32[16,64,128]{2,1,0:T(8,128)S(1)} collective-permute-done((f32[16,64,128]{2,1,0:T(8,128)S(1)}, f32[16,64,128]{2,1,0:T(8,128)S(1)}, u32[]{:S(2)}, u32[]{:S(2)}) %collective-permute-start.14) | collective-permute-done | bytes 524320 | tf_op jit(solution)/shard_map/ppermute | solution.py:228
  90.3 1.4 %shard_map.67 = f32[16,64,128]{2,1,0:T(8,128)} custom-call(s32[2]{0:T(128)S(1)} %pad_add_fusion.scal, f32[16,64,128]{2,1,0:T(8,128)S(1)} %get-tuple-element.53.a_ref, f32[16,64,128]{2,1,0:T(8,128)S(1)} %collective-permute-done.13.b_ref, f32[16,64,128]{2,1,0:T(8,128)S(1)} %collective-permute-done.14.c_ref), custom_call_target="tpu_custom_call" | custom-call | tf_op jit(solution)/shard_map/pallas_call | solution.py:21
Async XLA Ops:
  0.7 2.5 %copy-start = (f32[1,16,64,128]{3,2,1,0:T(8,128)S(1)}, f32[1,16,64,128]{3,2,1,0:T(8,128)}, u32[]{:S(2)}) copy-start(f32[1,16,64,128]{3,2,1,0:T(8,128)} %param.4) | copy-start | bytes 1572868
  2.5 13.8 %collective-permute-start.3 = (f32[12,64,128]{2,1,0:T(8,128)S(1)}, f32[12,64,128]{2,1,0:T(8,128)S(1)}, u32[]{:S(2)}, u32[]{:S(2)}) collective-permute-start(f32[12,64,128]{2,1,0:T(8,128)S(1)} %get-tuple-element.32), channel_id=1, source_target_pairs={{3,2},{7,6},{11,10},{15,14},{19,18},{23,22},{27,26},{31,30},{35,34... | collective-permute-start | bytes 1179656 | tf_op jit(solution)/shard_map/ppermute | solution.py:228
  3.2 35.0 %collective-permute-start.1 = (f32[16,64,128]{2,1,0:T(8,128)S(1)}, f32[16,64,128]{2,1,0:T(8,128)S(1)}, u32[]{:S(2)}, u32[]{:S(2)}) collective-permute-start(f32[16,64,128]{2,1,0:T(8,128)S(1)} %bitcast.10), channel_id=1, source_target_pairs={{0,2},{1,3},{4,6},{5,7},{8,10},{9,11},{12,14},{13,15},{16,18},{17,... | collective-permute-start | bytes 1572872 | tf_op jit(solution)/shard_map/ppermute | solution.py:228
  15.0 23.8 %collective-permute-start.5 = (f32[16,64,128]{2,1,0:T(8,128)S(1)}, f32[16,64,128]{2,1,0:T(8,128)S(1)}, u32[]{:S(2)}, u32[]{:S(2)}) collective-permute-start(f32[16,64,128]{2,1,0:T(8,128)S(1)} %bitcast.11), channel_id=1, source_target_pairs={{2,4},{3,5},{6,8},{7,9},{10,12},{11,13},{14,16},{15,17},{18,20},{1... | collective-permute-start | bytes 1572872 | tf_op jit(solution)/shard_map/ppermute | solution.py:228
  16.3 11.3 %collective-permute-start.4 = (f32[12,64,128]{2,1,0:T(8,128)S(1)}, f32[12,64,128]{2,1,0:T(8,128)S(1)}, u32[]{:S(2)}, u32[]{:S(2)}) collective-permute-start(f32[12,64,128]{2,1,0:T(8,128)S(1)} %collective-permute-done.3.first_ref), channel_id=1, source_target_pairs={{2,0},{3,1},{6,4},{7,5},{10,8},{11,9},{14,12},{15,13},{18,16},{19,... | collective-permute-start | bytes 1179656 | tf_op jit(solution)/shard_map/ppermute | solution.py:228
  17.6 20.6 %collective-permute-start = (f32[7,64,128]{2,1,0:T(8,128)S(1)}, f32[7,64,128]{2,1,0:T(8,128)S(1)}, u32[]{:S(2)}, u32[]{:S(2)}) collective-permute-start(f32[7,64,128]{2,1,0:T(8,128)S(1)} %get-tuple-element.29), channel_id=1, source_target_pairs={{0,1},{1,0},{4,5},{5,4},{8,9},{9,8},{12,13},{13,12},{16,17},{17,16... | collective-permute-start | bytes 688136 | tf_op jit(solution)/shard_map/ppermute | solution.py:228
  19.5 18.7 %collective-permute-start.2 = (f32[3,64,128]{2,1,0:T(8,128)S(1)}, f32[3,64,128]{2,1,0:T(8,128)S(1)}, u32[]{:S(2)}, u32[]{:S(2)}) collective-permute-start(f32[3,64,128]{2,1,0:T(8,128)S(1)} %get-tuple-element.31), channel_id=1, source_target_pairs={{0,3},{1,2},{4,7},{5,6},{8,11},{9,10},{12,15},{13,14},{16,19},{17,... | collective-permute-start | bytes 294920 | tf_op jit(solution)/shard_map/ppermute | solution.py:228
  41.2 11.8 %collective-permute-start.7 = (f32[16,64,128]{2,1,0:T(8,128)S(1)}, f32[16,64,128]{2,1,0:T(8,128)S(1)}, u32[]{:S(2)}, u32[]{:S(2)}) collective-permute-start(f32[16,64,128]{2,1,0:T(8,128)S(1)} %get-tuple-element.44.refs_0_.refs_1_), channel_id=1, source_target_pairs={{0,2},{1,3},{4,6},{5,7},{8,10},{9,11},{12,14},{13,15},{16,18},{17,... | collective-permute-start | bytes 1572872 | tf_op jit(solution)/shard_map/ppermute | solution.py:228
  42.6 23.4 %collective-permute-start.10 = (f32[16,64,128]{2,1,0:T(8,128)S(1)}, f32[16,64,128]{2,1,0:T(8,128)S(1)}, u32[]{:S(2)}, u32[]{:S(2)}) collective-permute-start(f32[16,64,128]{2,1,0:T(8,128)S(1)} %get-tuple-element.43.refs_0_), channel_id=1, source_target_pairs={{2,4},{3,5},{6,8},{7,9},{10,12},{11,13},{14,16},{15,17},{18,20},{1... | collective-permute-start | bytes 1572872 | tf_op jit(solution)/shard_map/ppermute | solution.py:228
  43.9 7.9 %collective-permute-start.8 = (f32[3,64,128]{2,1,0:T(8,128)S(1)}, f32[3,64,128]{2,1,0:T(8,128)S(1)}, u32[]{:S(2)}, u32[]{:S(2)}) collective-permute-start(f32[3,64,128]{2,1,0:T(8,128)S(1)} %get-tuple-element.46), channel_id=1, source_target_pairs={{0,3},{1,2},{4,7},{5,6},{8,11},{9,10},{12,15},{13,14},{16,19},{17,... | collective-permute-start | bytes 294920 | tf_op jit(solution)/shard_map/ppermute | solution.py:228
  47.7 5.3 %collective-permute-start.6 = (f32[4,64,128]{2,1,0:T(8,128)S(1)}, f32[4,64,128]{2,1,0:T(8,128)S(1)}, u32[]{:S(2)}, u32[]{:S(2)}) collective-permute-start(f32[4,64,128]{2,1,0:T(8,128)S(1)} %get-tuple-element.45), channel_id=1, source_target_pairs={{2,3},{3,2},{6,7},{7,6},{10,11},{11,10},{14,15},{15,14},{18,19},{1... | collective-permute-start | bytes 393224 | tf_op jit(solution)/shard_map/ppermute | solution.py:228
  48.4 17.6 %collective-permute-start.9 = (f32[4,64,128]{2,1,0:T(8,128)S(1)}, f32[4,64,128]{2,1,0:T(8,128)S(1)}, u32[]{:S(2)}, u32[]{:S(2)}) collective-permute-start(f32[4,64,128]{2,1,0:T(8,128)S(1)} %get-tuple-element.47), channel_id=1, source_target_pairs={{0,1},{1,0},{4,5},{5,4},{8,9},{9,8},{12,13},{13,12},{16,17},{17,16... | collective-permute-start | bytes 393224 | tf_op jit(solution)/shard_map/ppermute | solution.py:228
  51.8 14.2 %collective-permute-start.11 = (f32[3,64,128]{2,1,0:T(8,128)S(1)}, f32[3,64,128]{2,1,0:T(8,128)S(1)}, u32[]{:S(2)}, u32[]{:S(2)}) collective-permute-start(f32[3,64,128]{2,1,0:T(8,128)S(1)} %get-tuple-element.48), channel_id=1, source_target_pairs={{2,5},{3,4},{6,9},{7,8},{10,13},{11,12},{14,17},{15,16},{18,21},{1... | collective-permute-start | bytes 294920 | tf_op jit(solution)/shard_map/ppermute | solution.py:228
  68.4 9.8 %collective-permute-start.13 = (f32[16,64,128]{2,1,0:T(8,128)S(1)}, f32[16,64,128]{2,1,0:T(8,128)S(1)}, u32[]{:S(2)}, u32[]{:S(2)}) collective-permute-start(f32[16,64,128]{2,1,0:T(8,128)S(1)} %get-tuple-element.49.v_ref), channel_id=1, source_target_pairs={{0,2},{1,3},{4,6},{5,7},{8,10},{9,11},{12,14},{13,15},{16,18},{17,... | collective-permute-start | bytes 1572872 | tf_op jit(solution)/shard_map/ppermute | solution.py:228
  69.8 20.6 %collective-permute-start.14 = (f32[16,64,128]{2,1,0:T(8,128)S(1)}, f32[16,64,128]{2,1,0:T(8,128)S(1)}, u32[]{:S(2)}, u32[]{:S(2)}) collective-permute-start(f32[16,64,128]{2,1,0:T(8,128)S(1)} %shard_map.64.refs_0_), channel_id=1, source_target_pairs={{2,4},{3,5},{6,8},{7,9},{10,12},{11,13},{14,16},{15,17},{18,20},{1... | collective-permute-start | bytes 1572872 | tf_op jit(solution)/shard_map/ppermute | solution.py:228
  71.1 5.8 %collective-permute-start.12 = (f32[1,64,128]{2,1,0:T(8,128)S(1)}, f32[1,64,128]{2,1,0:T(8,128)S(1)}, u32[]{:S(2)}, u32[]{:S(2)}) collective-permute-start(f32[1,64,128]{2,1,0:T(8,128)S(1)} %get-tuple-element.50), channel_id=1, source_target_pairs={{0,1},{1,0},{4,5},{5,4},{8,9},{9,8},{12,13},{13,12},{16,17},{17,16... | collective-permute-start | bytes 98312 | tf_op jit(solution)/shard_map/ppermute | solution.py:228

commit v3 on v2

--- a/solution.py
+++ b/solution.py
@@ -12,7 +12,8 @@
 THIN = ITERS - 1
 F32 = jnp.float32
 ROLE, SIDE = 0, 1
-ROW, RUNS = 16, 4
+ROW, RUNS, CORES = 16, 4, 2
+HELPER = 6
 
 
 def call(kernel, outs, scalars, *operands, far=(), scratch=(), aliases=None):
@@ -65,38 +66,42 @@
     return diagonal
 
 
-def own_kernel(scal, init_far, source_far, spread_far, upwind_far, c_ref, x_ref, y_ref, z_ref, inv_ref, diag_ref, init_ref, source_ref, spread_ref, upwind_ref, sem):
+def own_kernel(role, held, scal, init_far, source_far, spread_far, upwind_far, *refs):
+    c_ref, x_ref, y_ref, z_ref, inv_ref, diag_ref, init_ref, source_ref, spread_ref, upwind_ref, sem = refs[held:]
     side = scal[SIDE]
     depth = init_far.shape[0]
-    copies = [
-        pltpu.make_async_copy(spread_far, spread_ref, sem.at[0]),
-        pltpu.make_async_copy(upwind_far, upwind_ref, sem.at[1]),
-        pltpu.make_async_copy(init_far, init_ref, sem.at[2]),
-        pltpu.make_async_copy(source_far, source_ref, sem.at[3]),
-    ]
-    for copy in copies:
-        copy.start()
-    for copy in copies[:2]:
-        copy.wait()
-
-    def own(z, carry):
-        diag_ref[z] = weights(
-            spread_ref[z], upwind_ref[0, z], upwind_ref[1, z], upwind_ref[2, z], ITERS * side + z, (c_ref, x_ref, y_ref, z_ref, inv_ref)
-        )
-        return carry
-
-    lax.fori_loop(0, depth, own, 0, unroll=2)
-    for copy in copies[2:]:
-        copy.wait()
-
-
-def rim_kernel(scal, first_ref, second_ref, *refs):
-    side = scal[SIDE]
-    outs = refs[5:]
+
+    @pl.when(scal[ROLE] == role)
+    def _():
+        copies = [
+            pltpu.make_async_copy(spread_far, spread_ref, sem.at[0]),
+            pltpu.make_async_copy(upwind_far, upwind_ref, sem.at[1]),
+            pltpu.make_async_copy(init_far, init_ref, sem.at[2]),
+            pltpu.make_async_copy(source_far, source_ref, sem.at[3]),
+        ]
+        for copy in copies:
+            copy.start()
+        for copy in copies[:2]:
+            copy.wait()
+
+        def own(z, carry):
+            diag_ref[z] = weights(
+                spread_ref[z], upwind_ref[0, z], upwind_ref[1, z], upwind_ref[2, z], ITERS * side + z, (c_ref, x_ref, y_ref, z_ref, inv_ref)
+            )
+            return carry
+
+        lax.fori_loop(0, depth, own, 0, unroll=2)
+        for copy in copies[2:]:
+            copy.wait()
+
+
+def rim_kernel(count, scal, *refs):
+    side = scal[SIDE]
+    sources, outs = refs[:count], refs[count + 5 :]
     depth = outs[0].shape[0] - ITERS
     for q in range(THIN):
         at = jnp.where(side == 1, 1 + q, depth + q)
-        parts = [first_ref[i * THIN + q] + second_ref[i * THIN + q] for i in range(4)]
+        parts = [sum(ref[i * THIN + q] for ref in sources) for i in range(4)]
         weights(*parts, at, outs)
 
 
@@ -115,13 +120,14 @@
     return row == nx - 1, lane == ny - 1
 
 
-def sweep_kernel(role, pass_on, widths, scal, *refs):
+def sweep_kernel(role, pass_on, widths, halo_at, scal, *refs):
     if pass_on:
         other_ref, *refs = refs
     count = len(refs) - len(widths) - 3
     edge_refs = refs[count : count + len(widths)]
     refs = refs[:count] + refs[count + len(widths) :]
-    (v_ref, vh_ref, s_ref, rim_ref, p_ref, ph_ref, c_ref, x_ref, y_ref, z_ref, inv_ref, out_ref, va, vb, g) = refs
+    v_ref, vh_ref, s_ref, rim_ref, p_ref, *ph_refs = refs[:-9]
+    c_ref, x_ref, y_ref, z_ref, inv_ref, out_ref, va, vb, g = refs[-9:]
     side = scal[SIDE]
     depth, nx, ny = v_ref.shape
 
@@ -144,7 +150,7 @@
             va[1 + jnp.where(side == 1, q, depth + q)] = vh_ref[q]
         for q in range(THIN):
             at = jnp.where(side == 1, 1 + q, depth + q)
-            g[at] = (rim_ref[ITERS + q] + ph_ref[q]) * inv_ref[at]
+            g[at] = (rim_ref[ITERS + q] + sum(ref[halo_at * side + q] for ref in ph_refs)) * inv_ref[at]
         src, dst = va, vb
         for k in range(ITERS):
             start = side * (1 + k)
@@ -176,38 +182,29 @@
             edge_ref[q] = out_ref[jnp.where(side == 1, q, depth - width + q)]
 
 
-def defect_kernel(scal, v_ref, h_ref, s_ref, c_ref, x_ref, y_ref, z_ref, diag_ref, out_ref, far_out, va, sem):
+def residual_kernel(scal, v_ref, h_ref, h2_ref, s_ref, c_ref, x_ref, y_ref, z_ref, diag_ref, p_ref, p2_ref, far_v, far_out, va, out_ref, sem):
     side = scal[SIDE]
     depth, nx, ny = v_ref.shape
-    copy = pltpu.make_async_copy(v_ref, far_out, sem)
-    copy.start()
+    copies = [pltpu.make_async_copy(v_ref, far_v, sem.at[0])]
+    copies[0].start()
     row_last, lane_last = last_masks(nx, ny)
     zero = jnp.zeros((nx, ny), F32)
-    va[0] = jnp.where(side == 1, h_ref[0], zero)
-    va[depth + 1] = jnp.where(side == 1, zero, h_ref[0])
+    halo = h_ref[0] + h2_ref[0]
+    va[0] = jnp.where(side == 1, halo, zero)
+    va[depth + 1] = jnp.where(side == 1, zero, halo)
     for z in range(depth):
         va[1 + z] = v_ref[z]
-
-    def layer(z, carry):
+    pieces = sem.shape[0] - 1
+    size = depth // pieces
+    for z in range(depth):
         e = ITERS * side + z
         here = va[1 + z]
         m = stencil(va[z], here, va[z + 2], c_ref[e], x_ref[e], y_ref[e], z_ref[e], row_last, lane_last)
-        out_ref[z] = s_ref[z] - diag_ref[z] * (here - m)
-        return carry
-
-    lax.fori_loop(0, depth, layer, 0, unroll=True)
-    copy.wait()
-
-
-def add_kernel(scal, a_ref, b_ref, c_ref, far_out, out_ref, sem):
-    pieces = sem.shape[0]
-    size = out_ref.shape[0] // pieces
-    copies = []
-    for i in range(pieces):
-        part = pl.ds(i * size, size)
-        out_ref[part] = a_ref[part] + (b_ref[part] + c_ref[part])
-        copies.append(pltpu.make_async_copy(out_ref.at[part], far_out.at[part], sem.at[i]))
-        copies[-1].start()
+        out_ref[z] = (s_ref[z] - diag_ref[z] * (here - m)) + (p_ref[z] + p2_ref[z])
+        if (z + 1) % size == 0:
+            part = pl.ds(z + 1 - size, size)
+            copies.append(pltpu.make_async_copy(out_ref.at[part], far_out.at[part], sem.at[len(copies)]))
+            copies[-1].start()
     for copy in copies:
         copy.wait()
 
@@ -237,7 +234,11 @@
     odd_across = [(number(t, s), number(t + 1, 1 - s)) for t in even for s in sides]
     even_across = [(number(t, s), number(t + 1, 1 - s)) for t in odd for s in sides]
     lower_odd = [(number(t, 1), number(t, 0)) for t in odd]
-    lower_odd += [(number(t, 0), number(t - stride if t % group >= stride else t - stride + group, 1)) for t in odd]
+    lower_odd += [(number(t, 0), number(t - stride, 1)) for t in odd if t % group >= stride]
+    for t in odd:
+        if t % group >= group - stride:
+            far_source = t - t % group + HELPER if t % stride < CORES else t - 1
+            lower_odd.append((number(far_source, 0), number(t, 1)))
     back = [(number(t, s), number(t - 1, s)) for t in odd for s in sides]
 
     plane = shape[1:]
@@ -250,53 +251,62 @@
     coef_edge, field_edge, thin_edge = call(
         pack_kernel, [(4 * THIN,) + plane, (ITERS + THIN,) + plane, thin], scalars, far=far, scratch=[pltpu.SemaphoreType.DMA((7,))]
     )
+    si = permute(field_edge, across_even + across_odd)
+    de = permute(thin_edge, even_across)
+    b1 = permute(initial, into_even)
     sc = permute(coef_edge, lower_odd)
-    b1 = permute(initial, into_even)
-    rim = permute(field_edge, across_even + across_odd)
-    d1 = permute(thin_edge, odd_across + even_across)
     a1 = permute(initial, into_odd)
-    *coefs, diag, initial_near, source_near = call(
-        own_kernel,
-        [ext] * 5 + [shape] * 3,
-        scalars,
-        far=far,
-        scratch=[pltpu.VMEM(shape, F32), pltpu.VMEM((3,) + shape, F32), pltpu.SemaphoreType.DMA((4,))],
-    )
+    ao = permute(si, into_odd)
+
+    def own(mine, *held):
+        outs = [ext] * 5 + [shape] * 3
+        room = [pltpu.VMEM(shape, F32), pltpu.VMEM((3,) + shape, F32), pltpu.SemaphoreType.DMA((4,))]
+        aliases = {5 + i: i for i in range(len(held))}
+        return call(functools.partial(own_kernel, mine, len(held)), outs, scalars, *held, far=far, scratch=room, aliases=aliases)
+
+    held = own(1)
     ac = permute(sc, back)
-    coefs = call(rim_kernel, [ext] * 5, scalars, sc, ac, *coefs, aliases={3 + i: i for i in range(5)})
-
-    def sweep(mine, other, v, vh, p, ph, widths):
+
+    def rim(coefs, *sources):
+        n = len(sources)
+        return call(functools.partial(rim_kernel, n), [ext] * 5, scalars, *sources, *coefs, aliases={1 + n + i: i for i in range(5)})
+
+    def sweep(mine, other, coefs, source_near, v, vh, p, *ph, widths=(), halo_at=0):
         outs = [shape] + [(w,) + plane for w in widths]
         extra = [other] if other is not None else []
-        kernel = functools.partial(sweep_kernel, mine, other is not None, widths)
-        return call(kernel, outs, scalars, *extra, v, vh, source_near, rim, p, ph, *coefs, scratch=scratch)
-
-    x, xw, xt = sweep(1, None, initial_near, rim, a1, d1, (ITERS, THIN))
+        kernel = functools.partial(sweep_kernel, mine, other is not None, widths, halo_at)
+        return call(kernel, outs, scalars, *extra, v, vh, source_near, si, p, *ph, *coefs, scratch=scratch)
+
+    coefs = rim(held[:5], sc)
+    x, xw, xt = sweep(1, None, coefs, held[7], held[6], si, a1, ao, widths=(ITERS, THIN), halo_at=1)
     b2 = permute(x, into_even)
     sx = permute(xw, across_odd)
     dx = permute(xt, even_across)
-    s1, yw, yt = sweep(0, x, initial_near, rim, b1, d1, (ITERS, THIN))
+    *coefs, diag, initial_near, source_near = own(0, *coefs, *held[5:])
+    coefs = rim(coefs, sc, ac)
+    s1, yw, yt = sweep(0, x, coefs, source_near, initial_near, si, b1, de, widths=(ITERS, THIN))
     dy = permute(yt, odd_across)
     a2 = permute(s1, into_odd)
+    z, zw = sweep(1, None, coefs, source_near, s1, sx, a2, dy, widths=(1,))
+    b3 = permute(z, into_even)
     sy = permute(yw, across_even)
-    (z,) = sweep(1, None, s1, sx, a2, dy, ())
-    b3 = permute(z, into_even)
-    s2, s2w = sweep(0, z, s1, sy, b2, dx, (1,))
+    sz = permute(zw, across_odd)
+    s2, s2w = sweep(0, z, coefs, source_near, s1, sy, b2, dx, widths=(1,))
     a3 = permute(s2, into_odd)
-    s2h = permute(s2w, across_even + across_odd)
-    defect, s2_far = call(
-        defect_kernel,
-        [shape, pltpu.HBM(shape, F32)],
+    sw = permute(s2w, across_even)
+    s2_far, residual = call(
+        residual_kernel,
+        [pltpu.HBM(shape, F32)] * 2,
         scalars,
         s2,
-        s2h,
+        sz,
+        sw,
         source_near,
         *coefs[:4],
         diag,
-        scratch=[pltpu.VMEM((depth + 2,) + plane, F32), pltpu.SemaphoreType.DMA],
-    )
-    (residual,) = call(
-        add_kernel, [pltpu.HBM(shape, F32)], scalars, defect, a3, b3, scratch=[pltpu.VMEM(shape, F32), pltpu.SemaphoreType.DMA((4,))]
+        a3,
+        b3,
+        scratch=[pltpu.VMEM((depth + 2,) + plane, F32), pltpu.VMEM(shape, F32), pltpu.SemaphoreType.DMA((5,))],
     )
     return (s2_far[None], residual[None])
 

time: 92.6 us -> 97.5 us (1.053)
  the two profiles are of different devices: /device:TPU:6 before, /device:TPU:64 now
where the time goes in v3:
time: 97.5 us; the launch traced here: 97 us
  waiting for transfers between devices  53.2 us (55%)
  starting transfers between devices  29.1 us (30%)
  Pallas kernels  13.7 us (14%)
    ppermute x17, waiting for transfers between devices, permute(): return lax.ppermute(value, ('tm', 'space'), pairs)  53.2 us
    ppermute x17, starting transfers between devices, permute(): return lax.ppermute(value, ('tm', 'space'), pairs)  29.1 us
    pallas_call x10, Pallas kernels, call(): pl.pallas_call(kernel, out_shape=[o if not isinstance(o, tuple) else pltp...  13.7 us
  transfers between devices with their start and end apart: 17, of which 6 were waited for; matrix products, arithmetic and copies ran while one was open for 0% of the time, Pallas kernels for 6%

profile of v3, /device:TPU:64, one launch (start us, length us, event | category | flops | bytes accessed | tf_op | source)
XLA Modules:
  0.0 97.0 jit_solution(14141646725992414178)
XLA Ops:
  0.6 0.1 pad_add_fusion.scal
  0.7 0.0 copy-start
  0.7 1.8 %shard_map.60 = (f32[12,64,128]{2,1,0:T(8,128)S(1)}, f32[7,64,128]{2,1,0:T(8,128)S(1)}, f32[3,64,128]{2,1,0:T(8,128)S(1)}) custom-call(s32[2]{0:T(128)S(1)} %pad_add_fusion.scal, f32[16,64,128]{2,1,0:T(8,128)} %bitcast.9, f32[16,64,128]{2,1,0:T(8,128)} %bitcast.6, f32[16,64,128]{2,1,0:T(8,128)} %spread_far.3, f32[3,16,64,128]{3,2,1,0:T(8,128)} %upwind_far.3), custom_call_target="tpu_custom_call" | custom-call | tf_op jit(solution)/shard_map/pallas_call | solution.py:22
  2.5 0.7 collective-permute-start.3
  3.2 0.0 copy-done
  3.2 3.0 %collective-permute-start.1 = (f32[16,64,128]{2,1,0:T(8,128)S(1)}, f32[16,64,128]{2,1,0:T(8,128)S(1)}, u32[]{:S(2)}, u32[]{:S(2)}) collective-permute-start(f32[16,64,128]{2,1,0:T(8,128)S(1)} %bitcast.12), channel_id=1, source_target_pairs={{0,2},{1,3},{4,6},{5,7},{8,10},{9,11},{12,14},{13,15},{16,18},{17,... | collective-permute-start | bytes 1572872 | tf_op jit(solution)/shard_map/ppermute | solution.py:225
  6.2 1.3 %collective-permute-start.4 = (f32[16,64,128]{2,1,0:T(8,128)S(1)}, f32[16,64,128]{2,1,0:T(8,128)S(1)}, u32[]{:S(2)}, u32[]{:S(2)}) collective-permute-start(f32[16,64,128]{2,1,0:T(8,128)S(1)} %bitcast.13), channel_id=1, source_target_pairs={{2,4},{3,5},{6,8},{7,9},{10,12},{11,13},{14,16},{15,17},{18,20},{1... | collective-permute-start | bytes 1572872 | tf_op jit(solution)/shard_map/ppermute | solution.py:225
  7.5 5.2 %collective-permute-start = (f32[7,64,128]{2,1,0:T(8,128)S(1)}, f32[7,64,128]{2,1,0:T(8,128)S(1)}, u32[]{:S(2)}, u32[]{:S(2)}) collective-permute-start(f32[7,64,128]{2,1,0:T(8,128)S(1)} %get-tuple-element.44), channel_id=1, source_target_pairs={{0,1},{1,0},{4,5},{5,4},{8,9},{9,8},{12,13},{13,12},{16,17},{17,16... | collective-permute-start | bytes 688136 | tf_op jit(solution)/shard_map/ppermute | solution.py:225
  12.8 0.0 collective-permute-done.3.refs_0_
  12.8 1.3 %collective-permute-start.6 = (f32[12,64,128]{2,1,0:T(8,128)S(1)}, f32[12,64,128]{2,1,0:T(8,128)S(1)}, u32[]{:S(2)}, u32[]{:S(2)}) collective-permute-start(f32[12,64,128]{2,1,0:T(8,128)S(1)} %collective-permute-done.3.refs_0_), channel_id=1, source_target_pairs={{2,0},{3,1},{6,4},{7,5},{10,8},{11,9},{14,12},{15,13},{18,16},{19,... | collective-permute-start | bytes 1179656 | tf_op jit(solution)/shard_map/ppermute | solution.py:225
  14.1 16.3 %collective-permute-done.refs_1_.refs_3_.refs_2_.refs_4_ = f32[7,64,128]{2,1,0:T(8,128)S(1)} collective-permute-done((f32[7,64,128]{2,1,0:T(8,128)S(1)}, f32[7,64,128]{2,1,0:T(8,128)S(1)}, u32[]{:S(2)}, u32[]{:S(2)}) %collective-permute-start) | collective-permute-done | bytes 229408 | tf_op jit(solution)/shard_map/ppermute | solution.py:225
  30.4 2.0 %collective-permute-start.2 = (f32[7,64,128]{2,1,0:T(8,128)S(1)}, f32[7,64,128]{2,1,0:T(8,128)S(1)}, u32[]{:S(2)}, u32[]{:S(2)}) collective-permute-start(f32[7,64,128]{2,1,0:T(8,128)S(1)} %collective-permute-done.refs_1_.refs_3_.refs_2_.refs_4_), channel_id=1, source_target_pairs={{0,2},{1,3},{4,6},{5,7},{8,10},{9,11},{12,14},{13,15},{16,18},{17,... | collective-permute-start | bytes 688136 | tf_op jit(solution)/shard_map/ppermute | solution.py:225
  32.4 1.3 %collective-permute-start.5 = (f32[3,64,128]{2,1,0:T(8,128)S(1)}, f32[3,64,128]{2,1,0:T(8,128)S(1)}, u32[]{:S(2)}, u32[]{:S(2)}) collective-permute-start(f32[3,64,128]{2,1,0:T(8,128)S(1)} %get-tuple-element.61), channel_id=1, source_target_pairs={{2,5},{3,4},{6,9},{7,8},{10,13},{11,12},{14,17},{15,16},{18,21},{1... | collective-permute-start | bytes 294920 | tf_op jit(solution)/shard_map/ppermute | solution.py:225
  33.7 0.6 shard_map.59
  34.3 0.6 shard_map.61
  34.9 0.0 collective-permute-done.2.refs_5_
  34.9 0.0 collective-permute-done.1.refs_4_
  34.9 0.6 shard_map.62
  35.5 2.5 %shard_map.63 = (f32[20,64,128]{2,1,0:T(8,128)S(1)}, f32[20,64,128]{2,1,0:T(8,128)S(1)}, f32[20,64,128]{2,1,0:T(8,128)S(1)}, f32[20,64,128]{2,1,0:T(8,128)S(1)},...) custom-call(s32[2]{0:T(128)S(1)} %pad_add_fusion.scal, ...), custom_call_target="tpu_custom_call", output_to_operand_aliasing={{0}: (5, {}), {1}: (6, {}), {2}: (7, {}), {3}: (8, {}), {4}... | custom-call | tf_op jit(solution)/shard_map/pallas_call | solution.py:22
  38.0 0.0 collective-permute-done.6.refs_1_
  38.0 0.6 shard_map.64
  38.6 7.2 %collective-permute-done.5.refs_6_ = f32[3,64,128]{2,1,0:T(8,128)S(1)} collective-permute-done((f32[3,64,128]{2,1,0:T(8,128)S(1)}, f32[3,64,128]{2,1,0:T(8,128)S(1)}, u32[]{:S(2)}, u32[]{:S(2)}) %collective-permute-start.5) | collective-permute-done | bytes 98336 | tf_op jit(solution)/shard_map/ppermute | solution.py:225
  45.8 0.0 collective-permute-done.4.refs_5_
  45.8 2.4 %shard_map.65 = (f32[16,64,128]{2,1,0:T(8,128)S(1)}, f32[4,64,128]{2,1,0:T(8,128)S(1)}, f32[3,64,128]{2,1,0:T(8,128)S(1)}) custom-call(s32[2]{0:T(128)S(1)} %pad_add_fusion.scal, f32[16,64,128]{2,1,0:T(8,128)S(1)} %get-tuple-element.57.refs_0_, f32[16,64,128]{2,1,0:T(8,128)S(1)} %get-tuple-element.59.refs_1_, ...), custom_call_target="tpu_custom_call" | custom-call | tf_op jit(solution)/shard_map/pallas_call | solution.py:22
  48.2 1.3 %collective-permute-start.8 = (f32[16,64,128]{2,1,0:T(8,128)S(1)}, f32[16,64,128]{2,1,0:T(8,128)S(1)}, u32[]{:S(2)}, u32[]{:S(2)}) collective-permute-start(f32[16,64,128]{2,1,0:T(8,128)S(1)} %get-tuple-element.72.refs_0_.refs_1_), channel_id=1, source_target_pairs={{0,2},{1,3},{4,6},{5,7},{8,10},{9,11},{12,14},{13,15},{16,18},{17,... | collective-permute-start | bytes 1572872 | tf_op jit(solution)/shard_map/ppermute | solution.py:225
  49.5 1.3 %collective-permute-start.11 = (f32[16,64,128]{2,1,0:T(8,128)S(1)}, f32[16,64,128]{2,1,0:T(8,128)S(1)}, u32[]{:S(2)}, u32[]{:S(2)}) collective-permute-start(f32[16,64,128]{2,1,0:T(8,128)S(1)} %get-tuple-element.57.refs_0_), channel_id=1, source_target_pairs={{2,4},{3,5},{6,8},{7,9},{10,12},{11,13},{14,16},{15,17},{18,20},{1... | collective-permute-start | bytes 1572872 | tf_op jit(solution)/shard_map/ppermute | solution.py:225
  50.8 0.7 collective-permute-start.7
  51.5 1.9 %collective-permute-start.10 = (f32[4,64,128]{2,1,0:T(8,128)S(1)}, f32[4,64,128]{2,1,0:T(8,128)S(1)}, u32[]{:S(2)}, u32[]{:S(2)}) collective-permute-start(f32[4,64,128]{2,1,0:T(8,128)S(1)} %get-tuple-element.76), channel_id=1, source_target_pairs={{0,1},{1,0},{4,5},{5,4},{8,9},{9,8},{12,13},{13,12},{16,17},{17,16... | collective-permute-start | bytes 393224 | tf_op jit(solution)/shard_map/ppermute | solution.py:225
  53.5 1.3 %collective-permute-start.9 = (f32[3,64,128]{2,1,0:T(8,128)S(1)}, f32[3,64,128]{2,1,0:T(8,128)S(1)}, u32[]{:S(2)}, u32[]{:S(2)}) collective-permute-start(f32[3,64,128]{2,1,0:T(8,128)S(1)} %get-tuple-element.74), channel_id=1, source_target_pairs={{0,3},{1,2},{4,7},{5,6},{8,11},{9,10},{12,15},{13,14},{16,19},{17,... | collective-permute-start | bytes 294920 | tf_op jit(solution)/shard_map/ppermute | solution.py:225
  54.8 0.0 collective-permute-done.7.refs_1_
  54.8 1.3 %collective-permute-start.12 = (f32[3,64,128]{2,1,0:T(8,128)S(1)}, f32[3,64,128]{2,1,0:T(8,128)S(1)}, u32[]{:S(2)}, u32[]{:S(2)}) collective-permute-start(f32[3,64,128]{2,1,0:T(8,128)S(1)} %get-tuple-element.77), channel_id=1, source_target_pairs={{2,5},{3,4},{6,9},{7,8},{10,13},{11,12},{14,17},{15,16},{18,21},{1... | collective-permute-start | bytes 294920 | tf_op jit(solution)/shard_map/ppermute | solution.py:225
  56.1 0.9 collective-permute-done.9.refs_5_
  57.0 0.0 collective-permute-done.8.refs_4_
  57.0 0.6 shard_map.66
  57.5 12.9 %collective-permute-done.12.refs_6_ = f32[3,64,128]{2,1,0:T(8,128)S(1)} collective-permute-done((f32[3,64,128]{2,1,0:T(8,128)S(1)}, f32[3,64,128]{2,1,0:T(8,128)S(1)}, u32[]{:S(2)}, u32[]{:S(2)}) %collective-permute-start.12) | collective-permute-done | bytes 98336 | tf_op jit(solution)/shard_map/ppermute | solution.py:225
  70.4 0.0 collective-permute-done.10.refs_2_
  70.4 0.0 collective-permute-done.11.refs_5_
  70.4 2.4 %shard_map.67 = (f32[16,64,128]{2,1,0:T(8,128)S(1)}, f32[1,64,128]{2,1,0:T(8,128)S(1)}) custom-call(s32[2]{0:T(128)S(1)} %pad_add_fusion.scal, f32[16,64,128]{2,1,0:T(8,128)S(1)} %get-tuple-element.75.refs_0_, f32[16,64,128]{2,1,0:T(8,128)S(1)} %get-tuple-element.72.refs_0_.refs_1_, f32[4,64,128]{2,1,0:T(8,128)S(1)} %collective-permute-done.10.refs_2_, ...), custom_call_target="tpu_custom_call" | custom-call | tf_op jit(solution)/shard_map/pallas_call | solution.py:22
  72.9 1.3 %collective-permute-start.15 = (f32[16,64,128]{2,1,0:T(8,128)S(1)}, f32[16,64,128]{2,1,0:T(8,128)S(1)}, u32[]{:S(2)}, u32[]{:S(2)}) collective-permute-start(f32[16,64,128]{2,1,0:T(8,128)S(1)} %get-tuple-element.78.v_ref), channel_id=1, source_target_pairs={{0,2},{1,3},{4,6},{5,7},{8,10},{9,11},{12,14},{13,15},{16,18},{17,... | collective-permute-start | bytes 1572872 | tf_op jit(solution)/shard_map/ppermute | solution.py:225
  74.2 1.3 %collective-permute-start.16 = (f32[16,64,128]{2,1,0:T(8,128)S(1)}, f32[16,64,128]{2,1,0:T(8,128)S(1)}, u32[]{:S(2)}, u32[]{:S(2)}) collective-permute-start(f32[16,64,128]{2,1,0:T(8,128)S(1)} %get-tuple-element.75.refs_0_), channel_id=1, source_target_pairs={{2,4},{3,5},{6,8},{7,9},{10,12},{11,13},{14,16},{15,17},{18,20},{1... | collective-permute-start | bytes 1572872 | tf_op jit(solution)/shard_map/ppermute | solution.py:225
  75.5 3.3 %collective-permute-start.14 = (f32[1,64,128]{2,1,0:T(8,128)S(1)}, f32[1,64,128]{2,1,0:T(8,128)S(1)}, u32[]{:S(2)}, u32[]{:S(2)}) collective-permute-start(f32[1,64,128]{2,1,0:T(8,128)S(1)} %get-tuple-element.80), channel_id=1, source_target_pairs={{0,1},{1,0},{4,5},{5,4},{8,9},{9,8},{12,13},{13,12},{16,17},{17,16... | collective-permute-start | bytes 98312 | tf_op jit(solution)/shard_map/ppermute | solution.py:225
  78.8 0.7 collective-permute-start.13
  79.4 1.9 %collective-permute-done.14.h2_ref = f32[1,64,128]{2,1,0:T(8,128)S(1)} collective-permute-done((f32[1,64,128]{2,1,0:T(8,128)S(1)}, f32[1,64,128]{2,1,0:T(8,128)S(1)}, u32[]{:S(2)}, u32[]{:S(2)}) %collective-permute-start.14) | collective-permute-done | bytes 32800 | tf_op jit(solution)/shard_map/ppermute | solution.py:225
  81.3 0.0 collective-permute-done.13.h_ref
  81.3 0.0 collective-permute-done.15.p_ref
  81.3 14.1 %collective-permute-done.16.p2_ref = f32[16,64,128]{2,1,0:T(8,128)S(1)} collective-permute-done((f32[16,64,128]{2,1,0:T(8,128)S(1)}, f32[16,64,128]{2,1,0:T(8,128)S(1)}, u32[]{:S(2)}, u32[]{:S(2)}) %collective-permute-start.16) | collective-permute-done | bytes 524320 | tf_op jit(solution)/shard_map/ppermute | solution.py:225
  95.4 1.7 %shard_map.68 = (f32[16,64,128]{2,1,0:T(8,128)}, f32[16,64,128]{2,1,0:T(8,128)}) custom-call(s32[2]{0:T(128)S(1)} %pad_add_fusion.scal, f32[16,64,128]{2,1,0:T(8,128)S(1)} %get-tuple-element.78.v_ref, f32[1,64,128]{2,1,0:T(8,128)S(1)} %collective-permute-done.13.h_ref, f32[1,64,128]{2,1,0:T(8,128)S(1)} %collective-permute-done.14.h2_ref, ...), custom_call_target="tpu_custom_call" | custom-call | tf_op jit(solution)/shard_map/pallas_call | solution.py:22
Async XLA Ops:
  0.7 2.5 %copy-start = (f32[1,16,64,128]{3,2,1,0:T(8,128)S(1)}, f32[1,16,64,128]{3,2,1,0:T(8,128)}, u32[]{:S(2)}) copy-start(f32[1,16,64,128]{3,2,1,0:T(8,128)} %param.4) | copy-start | bytes 1572868
  2.5 10.3 %collective-permute-start.3 = (f32[12,64,128]{2,1,0:T(8,128)S(1)}, f32[12,64,128]{2,1,0:T(8,128)S(1)}, u32[]{:S(2)}, u32[]{:S(2)}) collective-permute-start(f32[12,64,128]{2,1,0:T(8,128)S(1)} %get-tuple-element.46), channel_id=1, source_target_pairs={{3,2},{7,6},{11,10},{15,14},{19,18},{23,22},{27,26},{31,30},{35,34... | collective-permute-start | bytes 1179656 | tf_op jit(solution)/shard_map/ppermute | solution.py:225
  3.2 31.7 %collective-permute-start.1 = (f32[16,64,128]{2,1,0:T(8,128)S(1)}, f32[16,64,128]{2,1,0:T(8,128)S(1)}, u32[]{:S(2)}, u32[]{:S(2)}) collective-permute-start(f32[16,64,128]{2,1,0:T(8,128)S(1)} %bitcast.12), channel_id=1, source_target_pairs={{0,2},{1,3},{4,6},{5,7},{8,10},{9,11},{12,14},{13,15},{16,18},{17,... | collective-permute-start | bytes 1572872 | tf_op jit(solution)/shard_map/ppermute | solution.py:225
  6.2 39.6 %collective-permute-start.4 = (f32[16,64,128]{2,1,0:T(8,128)S(1)}, f32[16,64,128]{2,1,0:T(8,128)S(1)}, u32[]{:S(2)}, u32[]{:S(2)}) collective-permute-start(f32[16,64,128]{2,1,0:T(8,128)S(1)} %bitcast.13), channel_id=1, source_target_pairs={{2,4},{3,5},{6,8},{7,9},{10,12},{11,13},{14,16},{15,17},{18,20},{1... | collective-permute-start | bytes 1572872 | tf_op jit(solution)/shard_map/ppermute | solution.py:225
  7.5 22.8 %collective-permute-start = (f32[7,64,128]{2,1,0:T(8,128)S(1)}, f32[7,64,128]{2,1,0:T(8,128)S(1)}, u32[]{:S(2)}, u32[]{:S(2)}) collective-permute-start(f32[7,64,128]{2,1,0:T(8,128)S(1)} %get-tuple-element.44), channel_id=1, source_target_pairs={{0,1},{1,0},{4,5},{5,4},{8,9},{9,8},{12,13},{13,12},{16,17},{17,16... | collective-permute-start | bytes 688136 | tf_op jit(solution)/shard_map/ppermute | solution.py:225
  12.8 25.2 %collective-permute-start.6 = (f32[12,64,128]{2,1,0:T(8,128)S(1)}, f32[12,64,128]{2,1,0:T(8,128)S(1)}, u32[]{:S(2)}, u32[]{:S(2)}) collective-permute-start(f32[12,64,128]{2,1,0:T(8,128)S(1)} %collective-permute-done.3.refs_0_), channel_id=1, source_target_pairs={{2,0},{3,1},{6,4},{7,5},{10,8},{11,9},{14,12},{15,13},{18,16},{19,... | collective-permute-start | bytes 1179656 | tf_op jit(solution)/shard_map/ppermute | solution.py:225
  30.4 4.5 %collective-permute-start.2 = (f32[7,64,128]{2,1,0:T(8,128)S(1)}, f32[7,64,128]{2,1,0:T(8,128)S(1)}, u32[]{:S(2)}, u32[]{:S(2)}) collective-permute-start(f32[7,64,128]{2,1,0:T(8,128)S(1)} %collective-permute-done.refs_1_.refs_3_.refs_2_.refs_4_), channel_id=1, source_target_pairs={{0,2},{1,3},{4,6},{5,7},{8,10},{9,11},{12,14},{13,15},{16,18},{17,... | collective-permute-start | bytes 688136 | tf_op jit(solution)/shard_map/ppermute | solution.py:225
  32.4 13.4 %collective-permute-start.5 = (f32[3,64,128]{2,1,0:T(8,128)S(1)}, f32[3,64,128]{2,1,0:T(8,128)S(1)}, u32[]{:S(2)}, u32[]{:S(2)}) collective-permute-start(f32[3,64,128]{2,1,0:T(8,128)S(1)} %get-tuple-element.61), channel_id=1, source_target_pairs={{2,5},{3,4},{6,9},{7,8},{10,13},{11,12},{14,17},{15,16},{18,21},{1... | collective-permute-start | bytes 294920 | tf_op jit(solution)/shard_map/ppermute | solution.py:225
  48.2 8.8 %collective-permute-start.8 = (f32[16,64,128]{2,1,0:T(8,128)S(1)}, f32[16,64,128]{2,1,0:T(8,128)S(1)}, u32[]{:S(2)}, u32[]{:S(2)}) collective-permute-start(f32[16,64,128]{2,1,0:T(8,128)S(1)} %get-tuple-element.72.refs_0_.refs_1_), channel_id=1, source_target_pairs={{0,2},{1,3},{4,6},{5,7},{8,10},{9,11},{12,14},{13,15},{16,18},{17,... | collective-permute-start | bytes 1572872 | tf_op jit(solution)/shard_map/ppermute | solution.py:225
  49.5 20.9 %collective-permute-start.11 = (f32[16,64,128]{2,1,0:T(8,128)S(1)}, f32[16,64,128]{2,1,0:T(8,128)S(1)}, u32[]{:S(2)}, u32[]{:S(2)}) collective-permute-start(f32[16,64,128]{2,1,0:T(8,128)S(1)} %get-tuple-element.57.refs_0_), channel_id=1, source_target_pairs={{2,4},{3,5},{6,8},{7,9},{10,12},{11,13},{14,16},{15,17},{18,20},{1... | collective-permute-start | bytes 1572872 | tf_op jit(solution)/shard_map/ppermute | solution.py:225
  50.8 3.9 %collective-permute-start.7 = (f32[4,64,128]{2,1,0:T(8,128)S(1)}, f32[4,64,128]{2,1,0:T(8,128)S(1)}, u32[]{:S(2)}, u32[]{:S(2)}) collective-permute-start(f32[4,64,128]{2,1,0:T(8,128)S(1)} %get-tuple-element.73), channel_id=1, source_target_pairs={{2,3},{3,2},{6,7},{7,6},{10,11},{11,10},{14,15},{15,14},{18,19},{1... | collective-permute-start | bytes 393224 | tf_op jit(solution)/shard_map/ppermute | solution.py:225
  51.5 18.9 %collective-permute-start.10 = (f32[4,64,128]{2,1,0:T(8,128)S(1)}, f32[4,64,128]{2,1,0:T(8,128)S(1)}, u32[]{:S(2)}, u32[]{:S(2)}) collective-permute-start(f32[4,64,128]{2,1,0:T(8,128)S(1)} %get-tuple-element.76), channel_id=1, source_target_pairs={{0,1},{1,0},{4,5},{5,4},{8,9},{9,8},{12,13},{13,12},{16,17},{17,16... | collective-permute-start | bytes 393224 | tf_op jit(solution)/shard_map/ppermute | solution.py:225
  53.5 3.5 %collective-permute-start.9 = (f32[3,64,128]{2,1,0:T(8,128)S(1)}, f32[3,64,128]{2,1,0:T(8,128)S(1)}, u32[]{:S(2)}, u32[]{:S(2)}) collective-permute-start(f32[3,64,128]{2,1,0:T(8,128)S(1)} %get-tuple-element.74), channel_id=1, source_target_pairs={{0,3},{1,2},{4,7},{5,6},{8,11},{9,10},{12,15},{13,14},{16,19},{17,... | collective-permute-start | bytes 294920 | tf_op jit(solution)/shard_map/ppermute | solution.py:225
  54.8 15.7 %collective-permute-start.12 = (f32[3,64,128]{2,1,0:T(8,128)S(1)}, f32[3,64,128]{2,1,0:T(8,128)S(1)}, u32[]{:S(2)}, u32[]{:S(2)}) collective-permute-start(f32[3,64,128]{2,1,0:T(8,128)S(1)} %get-tuple-element.77), channel_id=1, source_target_pairs={{2,5},{3,4},{6,9},{7,8},{10,13},{11,12},{14,17},{15,16},{18,21},{1... | collective-permute-start | bytes 294920 | tf_op jit(solution)/shard_map/ppermute | solution.py:225
  72.9 8.4 %collective-permute-start.15 = (f32[16,64,128]{2,1,0:T(8,128)S(1)}, f32[16,64,128]{2,1,0:T(8,128)S(1)}, u32[]{:S(2)}, u32[]{:S(2)}) collective-permute-start(f32[16,64,128]{2,1,0:T(8,128)S(1)} %get-tuple-element.78.v_ref), channel_id=1, source_target_pairs={{0,2},{1,3},{4,6},{5,7},{8,10},{9,11},{12,14},{13,15},{16,18},{17,... | collective-permute-start | bytes 1572872 | tf_op jit(solution)/shard_map/ppermute | solution.py:225
  74.2 21.2 %collective-permute-start.16 = (f32[16,64,128]{2,1,0:T(8,128)S(1)}, f32[16,64,128]{2,1,0:T(8,128)S(1)}, u32[]{:S(2)}, u32[]{:S(2)}) collective-permute-start(f32[16,64,128]{2,1,0:T(8,128)S(1)} %get-tuple-element.75.refs_0_), channel_id=1, source_target_pairs={{2,4},{3,5},{6,8},{7,9},{10,12},{11,13},{14,16},{15,17},{18,20},{1... | collective-permute-start | bytes 1572872 | tf_op jit(solution)/shard_map/ppermute | solution.py:225
  75.5 5.8 %collective-permute-start.14 = (f32[1,64,128]{2,1,0:T(8,128)S(1)}, f32[1,64,128]{2,1,0:T(8,128)S(1)}, u32[]{:S(2)}, u32[]{:S(2)}) collective-permute-start(f32[1,64,128]{2,1,0:T(8,128)S(1)} %get-tuple-element.80), channel_id=1, source_target_pairs={{0,1},{1,0},{4,5},{5,4},{8,9},{9,8},{12,13},{13,12},{16,17},{17,16... | collective-permute-start | bytes 98312 | tf_op jit(solution)/shard_map/ppermute | solution.py:225
  78.8 2.5 %collective-permute-start.13 = (f32[1,64,128]{2,1,0:T(8,128)S(1)}, f32[1,64,128]{2,1,0:T(8,128)S(1)}, u32[]{:S(2)}, u32[]{:S(2)}) collective-permute-start(f32[1,64,128]{2,1,0:T(8,128)S(1)} %get-tuple-element.79), channel_id=1, source_target_pairs={{2,3},{3,2},{6,7},{7,6},{10,11},{11,10},{14,15},{15,14},{18,19},{1... | collective-permute-start | bytes 98312 | tf_op jit(solution)/shard_map/ppermute | solution.py:225

commit v4 on v3

v4 whole, which is shorter than its diff:
```python
import functools

import jax
import jax.numpy as jnp
from jax import lax
from jax.experimental import pallas as pl
from jax.experimental.pallas import tpu as pltpu
from jax.sharding import PartitionSpec as P


ITERS = 4
THIN = ITERS - 1
HALO = ITERS + 1
F32 = jnp.float32
ROLE, SIDE = 0, 1
ROW, RUNS = 16, 4
HELPER = 6


def call(kernel, outs, scalars, *operands, far=(), scratch=(), aliases=None):
    far = [pltpu.with_memory_space_constraint(o, pltpu.HBM) for o in far]
    near = [pltpu.with_memory_space_constraint(o, pltpu.VMEM) for o in operands]
    return pl.pallas_call(
        kernel,
        out_shape=[o if not isinstance(o, tuple) else pltpu.VMEM(o, F32) for o in outs],
        in_specs=[pl.BlockSpec(memory_space=pltpu.SMEM)]
        + [pl.BlockSpec(memory_space=pltpu.HBM)] * len(far)
        + [pl.BlockSpec(memory_space=pltpu.VMEM)] * len(near),
        out_specs=[pl.BlockSpec(memory_space=pltpu.VMEM if isinstance(o, tuple) else pltpu.HBM) for o in outs],
        scratch_shapes=list(scratch),
        input_output_aliases=aliases or {},
        compiler_params=pltpu.CompilerParams(vmem_limit_bytes=16 * 1024 * 1024),
    )(scalars, *far, *near)


def pack_kernel(scal, init_ref, source_ref, spread_ref, upwind_ref, coef_out, field_out, thin_out, full_out, sem):
    side = scal[SIDE]
    depth = init_ref.shape[0]
    thin = pl.ds((1 - side) * (depth - THIN), THIN)
    wide = pl.ds((1 - side) * (depth - ITERS), ITERS)
    copies = [
        pltpu.make_async_copy(init_ref.at[wide], field_out.at[pl.ds(0, ITERS)], sem.at[0]),
        pltpu.make_async_copy(source_ref.at[wide], field_out.at[pl.ds(ITERS, ITERS)], sem.at[1]),
        pltpu.make_async_copy(init_ref.at[thin], thin_out, sem.at[6]),
        pltpu.make_async_copy(init_ref, full_out.at[pl.ds(0, depth)], sem.at[7]),
        pltpu.make_async_copy(spread_ref.at[wide], coef_out.at[pl.ds(0, ITERS)], sem.at[2]),
    ]
    for i in range(3):
        copies.append(pltpu.make_async_copy(upwind_ref.at[i, wide], coef_out.at[pl.ds((1 + i) * ITERS, ITERS)], sem.at[3 + i]))
    for copy in copies:
        copy.start()
    for copy in copies:
        copy.wait()


def weights(spread, ux, uy, uz, at, refs):
    c_ref, x_ref, y_ref, z_ref, inv_ref = refs
    nx, ny = spread.shape
    row = lax.broadcasted_iota(jnp.int32, (nx, ny), 0)
    lane = lax.broadcasted_iota(jnp.int32, (nx, ny), 1)
    diagonal = 1.0 + 6.0 * spread + (ux + uy + uz)
    inv = 1.0 / diagonal
    c_ref[at] = spread * inv
    x_ref[at] = jnp.where(row == 0, 0.0, (spread + ux) * inv)
    y_ref[at] = jnp.where(lane == 0, 0.0, (spread + uy) * inv)
    z_ref[at] = (spread + uz) * inv
    inv_ref[at] = inv
    return diagonal


def own_kernel(scal, source_far, spread_far, upwind_far, c_ref, x_ref, y_ref, z_ref, inv_ref, diag_ref, source_ref, spread_ref, upwind_ref, sem):
    side = scal[SIDE]
    depth = source_far.shape[0]
    copies = [
        pltpu.make_async_copy(spread_far, spread_ref, sem.at[0]),
        pltpu.make_async_copy(upwind_far, upwind_ref, sem.at[1]),
        pltpu.make_async_copy(source_far, source_ref, sem.at[2]),
    ]
    for copy in copies:
        copy.start()
    for copy in copies[:2]:
        copy.wait()

    def own(z, carry):
        diag_ref[z] = weights(
            spread_ref[z], upwind_ref[0, z], upwind_ref[1, z], upwind_ref[2, z], HALO * side + z, (c_ref, x_ref, y_ref, z_ref, inv_ref)
        )
        return carry

    lax.fori_loop(0, depth, own, 0, unroll=2)
    copies[2].wait()


def join_kernel(scal, field_ref, held_ref, full_ref):
    depth = full_ref.shape[0] - ITERS
    for q in range(ITERS):
        full_ref[depth + q] = field_ref[q]


def stencil(below, here, above, c, cx, cy, cz, row_last, lane_last):
    nx, ny = here.shape
    low_x = pltpu.roll(here, 1, 0)
    high_x = jnp.where(row_last, 0.0, pltpu.roll(here, nx - 1, 0))
    low_y = pltpu.roll(here, 1, 1)
    high_y = jnp.where(lane_last, 0.0, pltpu.roll(here, ny - 1, 1))
    return c * ((above + high_x) + high_y) + (cx * low_x + cz * below) + cy * low_y


def last_masks(nx, ny):
    row = lax.broadcasted_iota(jnp.int32, (nx, ny), 0)
    lane = lax.broadcasted_iota(jnp.int32, (nx, ny), 1)
    return row == nx - 1, lane == ny - 1


def sweep_kernel(role, pass_on, widths, extra, fields, v_at, p_halo, rims, scal, *refs):
    if pass_on:
        others, refs = refs[: 1 + extra], refs[1 + extra :]
    va, vb, g = refs[-3:]
    count = 4 + fields + 1 + rims + 5
    outs, rest = refs[count : count + 1 + extra], refs[count + 1 + extra : -3]
    edge_refs, made = rest[: len(widths)], rest[len(widths) :]
    v_ref, vh_ref, s_ref, rim_ref = refs[:4]
    p_refs, ph_ref = refs[4 : 4 + fields], refs[4 + fields]
    rim_sources = refs[5 + fields : 5 + fields + rims]
    c_ref, x_ref, y_ref, z_ref, inv_ref = made if rims else refs[count - 5 : count]
    p_at, reach = p_halo
    out_ref = outs[0]
    side = scal[SIDE]
    depth, nx, ny = out_ref.shape
    held_v, held_f = ITERS + extra, THIN + extra

    @pl.when(scal[ROLE] == role)
    def _():
        for q in range(ITERS if rims else 0):
            at = jnp.where(side == 1, HALO - ITERS + q, depth + q)
            parts = [sum(ref[i * ITERS + q] for ref in rim_sources) for i in range(4)]
            weights(*parts, at, (c_ref, x_ref, y_ref, z_ref, inv_ref))
        row_last, lane_last = last_masks(nx, ny)
        zero = jnp.zeros((nx, ny), F32)
        for buf in (va, vb):
            buf[0] = zero
            buf[depth + HALO + 1] = zero

        def fill(z, carry):
            at = HALO * side + z
            va[1 + at] = v_ref[z]
            g[at] = (s_ref[z] + sum(ref[z] for ref in p_refs)) * inv_ref[at]
            return carry

        lax.fori_loop(0, depth, fill, 0, unroll=4)
        for q in range(held_v):
            va[1 + jnp.where(side == 1, HALO - held_v + q, depth + q)] = vh_ref[v_at + q]
        for q in range(held_f):
            at = jnp.where(side == 1, HALO - held_f + q, depth + q)
            rim = rim_ref[ITERS + (ITERS - held_f) * side + q]
            g[at] = (rim + ph_ref[p_at + (reach - held_f) * side + q]) * inv_ref[at]
        src, dst = va, vb
        for k in range(ITERS):
            start = side * (HALO - held_f + k)
            direct = k == ITERS - 1 and extra == 0

            def layer(j, carry, src=src, dst=dst, start=start, direct=direct):
                e = start + j
                new = g[e] + stencil(
                    src[e], src[e + 1], src[e + 2], c_ref[e], x_ref[e], y_ref[e], z_ref[e], row_last, lane_last
                )
                if direct:
                    out_ref[j] = new
                else:
                    dst[e + 1] = new
                return carry

            lax.fori_loop(0, depth + held_f - k, layer, 0, unroll=True)
            src, dst = dst, src
        if extra:
            for z in range(depth):
                out_ref[z] = src[1 + HALO * side + z]
            outs[1][0] = src[1 + jnp.where(side == 1, HALO - 1, depth)]

    if pass_on:

        @pl.when(scal[ROLE] != role)
        def _():
            for other, out in zip(others, outs):
                out[...] = other[...]

    for width, edge_ref in zip(widths, edge_refs):
        for q in range(width):
            edge_ref[q] = out_ref[jnp.where(side == 1, q, depth - width + q)]


def residual_kernel(scal, v_ref, h_ref, s_ref, c_ref, x_ref, y_ref, z_ref, diag_ref, p_ref, p2_ref, far_v, far_out, va, out_ref, sem):
    side = scal[SIDE]
    depth, nx, ny = v_ref.shape
    copies = [pltpu.make_async_copy(v_ref, far_v, sem.at[0])]
    copies[0].start()
    row_last, lane_last = last_masks(nx, ny)
    zero = jnp.zeros((nx, ny), F32)
    halo = h_ref[0]
    va[0] = jnp.where(side == 1, halo, zero)
    va[depth + 1] = jnp.where(side == 1, zero, halo)
    for z in range(depth):
        va[1 + z] = v_ref[z]
    pieces = sem.shape[0] - 1
    size = depth // pieces
    for z in range(depth):
        e = HALO * side + z
        here = va[1 + z]
        m = stencil(va[z], here, va[z + 2], c_ref[e], x_ref[e], y_ref[e], z_ref[e], row_last, lane_last)
        out_ref[z] = (s_ref[z] - diag_ref[z] * (here - m)) + (p_ref[z] + p2_ref[z])
        if (z + 1) % size == 0:
            part = pl.ds(z + 1 - size, size)
            copies.append(pltpu.make_async_copy(out_ref.at[part], far_out.at[part], sem.at[len(copies)]))
            copies[-1].start()
    for copy in copies:
        copy.wait()


def body(initial, source, diffusion, advection):
    tm, space = (lax.axis_size("tm"), lax.axis_size("space"))
    role = lax.axis_index("tm") % 2
    side = lax.axis_index("space")
    scalars = jnp.stack([role, side]).astype(jnp.int32)
    shape = initial.shape[1:]
    depth = shape[0]
    initial, source = (initial[0], source[0])

    def number(t, s):
        return (t % tm) * space + s

    def permute(value, pairs):
        return lax.ppermute(value, ("tm", "space"), pairs)

    sides = range(space)
    stride, group = ROW, ROW * RUNS
    even, odd = range(0, tm, 2), range(1, tm, 2)
    into_odd = [(number(t, s), number(t + 1, s)) for t in even for s in sides]
    into_even = [(number(t, s), number(t + 1, s)) for t in odd for s in sides]
    short_even = [(number(t, s), number(t + 1, s)) for t in odd for s in sides if t % ROW < ROW - 1 or s == 0]
    last = [t for t in odd if t % ROW == ROW - 1]
    last_along = [(number(t, 1), number(t + ROW, 1)) for t in last]
    last_around = [(number(t, 1), number(t + 1 - ROW, 1)) for t in last]
    across_even = [(number(t, s), number(t, 1 - s)) for t in even for s in sides]
    across_odd = [(number(t, s), number(t, 1 - s)) for t in odd for s in sides]
    odd_across = [(number(t, s), number(t + 1, 1 - s)) for t in even for s in sides]
    even_across = [(number(t, s), number(t + 1, 1 - s)) for t in odd for s in sides]
    lower_odd = []
    for t in odd:
        run, first = (t % group) // stride, t % stride == 1
        lower_odd.append((number(t, 1) if first else number(t - stride, 1) if run else number(t - 1, 1), number(t, 0)))
        if run < RUNS - 1:
            lower_odd.append((number(t + stride, 0), number(t, 1)))
        else:
            lower_odd.append((number(t - t % group + HELPER if first else t - 1, 0), number(t, 1)))
    back = [(number(t, s), number(t - 1, s)) for t in odd for s in sides]

    plane = shape[1:]
    ext = (depth + HALO,) + plane
    padded = (depth + HALO + 2,) + plane
    scratch = [pltpu.VMEM(padded, F32), pltpu.VMEM(padded, F32), pltpu.VMEM(ext, F32)]
    thin = (THIN,) + plane
    far = (initial, source, diffusion, advection)

    coef_edge, field_edge, thin_edge, full = call(
        pack_kernel,
        [(4 * ITERS,) + plane, (2 * ITERS,) + plane, thin, (depth + ITERS,) + plane],
        scalars,
        far=far,
        scratch=[pltpu.SemaphoreType.DMA((8,))],
    )
    si = permute(field_edge, across_even + across_odd)
    de = permute(thin_edge, even_across)
    b1 = permute(initial, into_even)
    sc = permute(coef_edge, lower_odd)
    *coefs, diag, source_near = call(
        own_kernel,
        [ext] * 5 + [shape] * 2,
        scalars,
        far=far[1:],
        scratch=[pltpu.VMEM(shape, F32), pltpu.VMEM((3,) + shape, F32), pltpu.SemaphoreType.DMA((3,))],
    )
    (full,) = call(join_kernel, [(depth + ITERS,) + plane], scalars, si, full, aliases={2: 0})
    a1 = permute(full, into_odd)
    ac = permute(sc, back)

    def sweep(mine, others, v, vh, p, ph, p_halo, v_at=0, widths=(), extra=0, rims=()):
        nonlocal coefs
        outs = [shape] + [(w,) + plane for w in (1,) * extra + widths]
        kernel = functools.partial(sweep_kernel, mine, bool(others), widths, extra, len(p), v_at, p_halo, len(rims))
        operands = (*others, v, vh, source_near, si, *p, ph, *rims)
        made = [ext] * 5 if rims else []
        aliases = {1 + len(operands) + i: len(outs) + i for i in range(len(made))}
        out = call(kernel, outs + made, scalars, *operands, *coefs, scratch=scratch, aliases=aliases)
        if rims:
            out, coefs = out[:-5], out[-5:]
        return out

    x, xw, xt = sweep(1, (), full, full, (a1,), a1, (depth, ITERS), depth, (HALO, ITERS), rims=(sc,))
    b2 = permute(x, short_even)
    sx = permute(xw, across_odd)
    zh = permute(x, last_along)
    s1, yw = sweep(0, (x,), full, full, (b1,), de, (0, THIN), depth, (HALO,), rims=(ac,))
    dy = permute(yw, odd_across)
    a2 = permute(s1, into_odd)
    dx = permute(xt, even_across)
    yh = permute(zh, last_around)
    z, zh1 = sweep(1, (), s1, sx, (a2,), dy, (0, HALO), extra=1)
    b3 = permute(z, into_even)
    ey = permute(dy, back)
    s2, s2h = sweep(0, (z, zh1), s1, ey, (b2, yh), dx, (0, ITERS), extra=1)
    a3 = permute(s2, into_odd)
    s2_far, residual = call(
        residual_kernel,
        [pltpu.HBM(shape, F32)] * 2,
        scalars,
        s2,
        s2h,
        source_near,
        *coefs[:4],
        diag,
        a3,
        b3,
        scratch=[pltpu.VMEM((depth + 2,) + plane, F32), pltpu.VMEM(shape, F32), pltpu.SemaphoreType.DMA((5,))],
    )
    return (s2_far[None], residual[None])


def solution(mesh):
    in_specs = (
        P("tm", "space", None, None),
        P("tm", "space", None, None),
        P("space", None, None),
        P(None, "space", None, None),
    )
    out_specs = (P("tm", "space", None, None), P("tm", "space", None, None))
    return jax.shard_map(body, mesh=mesh, in_specs=in_specs, out_specs=out_specs, check_vma=False)
```

time: 97.5 us -> 91.7 us (0.941)
  the two profiles are of different devices: /device:TPU:64 before, /device:TPU:6 now
where the time goes in v4:
time: 91.7 us; the launch traced here: 90.1 us
  waiting for transfers between devices  54.8 us (60%)
  starting transfers between devices  21.5 us (23%)
  Pallas kernels  12.8 us (14%)
    ppermute x16, waiting for transfers between devices, permute(): return lax.ppermute(value, ('tm', 'space'), pairs)  54.8 us
    ppermute x16, starting transfers between devices, permute(): return lax.ppermute(value, ('tm', 'space'), pairs)  21.5 us
    pallas_call x8, Pallas kernels, call(): pl.pallas_call(kernel, out_shape=[o if not isinstance(o, tuple) else pltp...  12.8 us
  transfers between devices with their start and end apart: 16, of which 5 were waited for; matrix products, arithmetic and copies ran while one was open for 0% of the time, Pallas kernels for 10%

profile of v4, /device:TPU:6, one launch (start us, length us, event | category | flops | bytes accessed | tf_op | source)
XLA Modules:
  0.0 90.1 jit_solution(8452222905179421882)
XLA Ops:
  0.6 0.1 pad_add_fusion.scal
  0.7 2.0 %shard_map.59 = (f32[16,64,128]{2,1,0:T(8,128)S(1)}, f32[8,64,128]{2,1,0:T(8,128)S(1)}, f32[3,64,128]{2,1,0:T(8,128)S(1)}, f32[20,64,128]{2,1,0:T(8,128)S(1)}) custom-call(s32[2]{0:T(128)S(1)} %pad_add_fusion.scal, f32[16,64,128]{2,1,0:T(8,128)} %bitcast.8, f32[16,64,128]{2,1,0:T(8,128)} %bitcast.6, f32[16,64,128]{2,1,0:T(8,128)} %spread_far.1, ...), custom_call_target="tpu_custom_call" | custom-call | tf_op jit(solution)/shard_map/pallas_call | solution.py:23
  2.7 0.0 copy-start
  2.7 4.4 %collective-permute-start = (f32[8,64,128]{2,1,0:T(8,128)S(1)}, f32[8,64,128]{2,1,0:T(8,128)S(1)}, u32[]{:S(2)}, u32[]{:S(2)}) collective-permute-start(f32[8,64,128]{2,1,0:T(8,128)S(1)} %get-tuple-element.34), channel_id=1, source_target_pairs={{0,1},{1,0},{4,5},{5,4},{8,9},{9,8},{12,13},{13,12},{16,17},{17,16... | collective-permute-start | bytes 786440 | tf_op jit(solution)/shard_map/ppermute | solution.py:232
  7.1 6.3 %collective-permute-done.field_ref.refs_3_.refs_4_.refs_5_ = f32[8,64,128]{2,1,0:T(8,128)S(1)} collective-permute-done((f32[8,64,128]{2,1,0:T(8,128)S(1)}, f32[8,64,128]{2,1,0:T(8,128)S(1)}, u32[]{:S(2)}, u32[]{:S(2)}) %collective-permute-start) | collective-permute-done | bytes 262176 | tf_op jit(solution)/shard_map/ppermute | solution.py:232
  13.4 0.5 shard_map.60.refs_0_.refs_1_.refs_2_
  14.0 1.3 %collective-permute-start.1 = (f32[20,64,128]{2,1,0:T(8,128)S(1)}, f32[20,64,128]{2,1,0:T(8,128)S(1)}, u32[]{:S(2)}, u32[]{:S(2)}) collective-permute-start(f32[20,64,128]{2,1,0:T(8,128)S(1)} %shard_map.60.refs_0_.refs_1_.refs_2_), channel_id=1, source_target_pairs={{0,2},{1,3},{4,6},{5,7},{8,10},{9,11},{12,14},{13,15},{16,18},{17,... | collective-permute-start | bytes 1966088 | tf_op jit(solution)/shard_map/ppermute | solution.py:232
  15.3 0.7 collective-permute-start.2
  16.0 0.0 copy-done
  16.0 1.3 %collective-permute-start.3 = (f32[16,64,128]{2,1,0:T(8,128)S(1)}, f32[16,64,128]{2,1,0:T(8,128)S(1)}, u32[]{:S(2)}, u32[]{:S(2)}) collective-permute-start(f32[16,64,128]{2,1,0:T(8,128)S(1)} %bitcast.9), channel_id=1, source_target_pairs={{2,4},{3,5},{6,8},{7,9},{10,12},{11,13},{14,16},{15,17},{18,20},{1... | collective-permute-start | bytes 1572872 | tf_op jit(solution)/shard_map/ppermute | solution.py:232
  17.3 0.0 collective-permute-done.2.refs_6_
  17.3 1.3 %collective-permute-start.5 = (f32[16,64,128]{2,1,0:T(8,128)S(1)}, f32[16,64,128]{2,1,0:T(8,128)S(1)}, u32[]{:S(2)}, u32[]{:S(2)}) collective-permute-start(f32[16,64,128]{2,1,0:T(8,128)S(1)} %collective-permute-done.2.refs_6_), channel_id=1, source_target_pairs={{2,0},{3,1},{6,4},{7,5},{10,8},{11,9},{14,12},{15,13},{18,16},{19,... | collective-permute-start | bytes 1572872 | tf_op jit(solution)/shard_map/ppermute | solution.py:232
  18.6 2.4 %shard_map.61 = (f32[21,64,128]{2,1,0:T(8,128)S(1)}, f32[21,64,128]{2,1,0:T(8,128)S(1)}, f32[21,64,128]{2,1,0:T(8,128)S(1)}, f32[21,64,128]{2,1,0:T(8,128)S(1)},...) custom-call(s32[2]{0:T(128)S(1)} %pad_add_fusion.scal, ...), custom_call_target="tpu_custom_call" | custom-call | tf_op jit(solution)/shard_map/pallas_call | solution.py:23
  21.1 0.0 collective-permute-done.1.refs_4_.refs_5_
  21.1 0.6 shard_map.62
  21.7 0.7 collective-permute-start.11
  22.4 1.3 %collective-permute-start.4 = (f32[3,64,128]{2,1,0:T(8,128)S(1)}, f32[3,64,128]{2,1,0:T(8,128)S(1)}, u32[]{:S(2)}, u32[]{:S(2)}) collective-permute-start(f32[3,64,128]{2,1,0:T(8,128)S(1)} %get-tuple-element.44), channel_id=1, source_target_pairs={{2,5},{3,4},{6,9},{7,8},{10,13},{11,12},{14,17},{15,16},{18,21},{1... | collective-permute-start | bytes 294920 | tf_op jit(solution)/shard_map/ppermute | solution.py:232
  23.7 24.6 %collective-permute-done.4.refs_6_ = f32[3,64,128]{2,1,0:T(8,128)S(1)} collective-permute-done((f32[3,64,128]{2,1,0:T(8,128)S(1)}, f32[3,64,128]{2,1,0:T(8,128)S(1)}, u32[]{:S(2)}, u32[]{:S(2)}) %collective-permute-start.4) | collective-permute-done | bytes 98336 | tf_op jit(solution)/shard_map/ppermute | solution.py:232
  48.3 0.0 collective-permute-done.3.refs_5_
  48.3 0.0 collective-permute-done.5.refs_7_
  48.3 2.5 %shard_map.63 = (f32[16,64,128]{2,1,0:T(8,128)S(1)}, f32[5,64,128]{2,1,0:T(8,128)S(1)}, f32[21,64,128]{2,1,0:T(8,128)S(1)}, f32[21,64,128]{2,1,0:T(8,128)S(1)}, ...) custom-call(s32[2]{0:T(128)S(1)} %pad_add_fusion.scal, ...), custom_call_target="tpu_custom_call", output_to_operand_aliasing={{2}: (9, {}), {3}: (10, {}), {4}: (11, {}), {5}: (12, {}), ... | custom-call | tf_op jit(solution)/shard_map/pallas_call | solution.py:23
  50.8 1.3 %collective-permute-start.7 = (f32[16,64,128]{2,1,0:T(8,128)S(1)}, f32[16,64,128]{2,1,0:T(8,128)S(1)}, u32[]{:S(2)}, u32[]{:S(2)}) collective-permute-start(f32[16,64,128]{2,1,0:T(8,128)S(1)} %get-tuple-element.50.refs_0_.refs_2_), channel_id=1, source_target_pairs={{0,2},{1,3},{4,6},{5,7},{8,10},{9,11},{12,14},{13,15},{16,18},{17,... | collective-permute-start | bytes 1572872 | tf_op jit(solution)/shard_map/ppermute | solution.py:232
  52.1 1.3 %collective-permute-start.10 = (f32[16,64,128]{2,1,0:T(8,128)S(1)}, f32[16,64,128]{2,1,0:T(8,128)S(1)}, u32[]{:S(2)}, u32[]{:S(2)}) collective-permute-start(f32[16,64,128]{2,1,0:T(8,128)S(1)} %get-tuple-element.43.refs_0_), channel_id=1, source_target_pairs={{2,4},{3,5},{6,8},{7,9},{10,12},{11,13},{14,16},{15,17},{18,20},{1... | collective-permute-start | bytes 1572872 | tf_op jit(solution)/shard_map/ppermute | solution.py:232
  53.4 0.0 collective-permute-done.11
  53.4 0.7 collective-permute-start.12
  54.1 1.3 %collective-permute-start.8 = (f32[5,64,128]{2,1,0:T(8,128)S(1)}, f32[5,64,128]{2,1,0:T(8,128)S(1)}, u32[]{:S(2)}, u32[]{:S(2)}) collective-permute-start(f32[5,64,128]{2,1,0:T(8,128)S(1)} %get-tuple-element.52), channel_id=1, source_target_pairs={{0,3},{1,2},{4,7},{5,6},{8,11},{9,10},{12,15},{13,14},{16,19},{17,... | collective-permute-start | bytes 491528 | tf_op jit(solution)/shard_map/ppermute | solution.py:232
  55.4 0.7 collective-permute-start.6
  56.1 7.0 %collective-permute-done.8.refs_5_ = f32[5,64,128]{2,1,0:T(8,128)S(1)} collective-permute-done((f32[5,64,128]{2,1,0:T(8,128)S(1)}, f32[5,64,128]{2,1,0:T(8,128)S(1)}, u32[]{:S(2)}, u32[]{:S(2)}) %collective-permute-start.8) | collective-permute-done | bytes 163872 | tf_op jit(solution)/shard_map/ppermute | solution.py:232
  63.1 1.3 %collective-permute-start.9 = (f32[5,64,128]{2,1,0:T(8,128)S(1)}, f32[5,64,128]{2,1,0:T(8,128)S(1)}, u32[]{:S(2)}, u32[]{:S(2)}) collective-permute-start(f32[5,64,128]{2,1,0:T(8,128)S(1)} %collective-permute-done.8.refs_5_), channel_id=1, source_target_pairs={{2,0},{3,1},{6,4},{7,5},{10,8},{11,9},{14,12},{15,13},{18,16},{19,... | collective-permute-start | bytes 491528 | tf_op jit(solution)/shard_map/ppermute | solution.py:232
  64.4 0.0 collective-permute-done.6.refs_1_
  64.4 1.3 %collective-permute-start.13 = (f32[4,64,128]{2,1,0:T(8,128)S(1)}, f32[4,64,128]{2,1,0:T(8,128)S(1)}, u32[]{:S(2)}, u32[]{:S(2)}) collective-permute-start(f32[4,64,128]{2,1,0:T(8,128)S(1)} %get-tuple-element.60), channel_id=1, source_target_pairs={{2,5},{3,4},{6,9},{7,8},{10,13},{11,12},{14,17},{15,16},{18,21},{1... | collective-permute-start | bytes 393224 | tf_op jit(solution)/shard_map/ppermute | solution.py:232
  65.7 0.0 collective-permute-done.7.refs_4_
  65.7 0.6 shard_map.64
  66.3 1.3 %collective-permute-start.15 = (f32[16,64,128]{2,1,0:T(8,128)S(1)}, f32[16,64,128]{2,1,0:T(8,128)S(1)}, u32[]{:S(2)}, u32[]{:S(2)}) collective-permute-start(f32[16,64,128]{2,1,0:T(8,128)S(1)} %get-tuple-element.58.refs_0_), channel_id=1, source_target_pairs={{2,4},{3,5},{6,8},{7,9},{10,12},{11,13},{14,16},{15,17},{18,20},{1... | collective-permute-start | bytes 1572872 | tf_op jit(solution)/shard_map/ppermute | solution.py:232
  67.6 8.3 %collective-permute-done.13.refs_8_ = f32[4,64,128]{2,1,0:T(8,128)S(1)} collective-permute-done((f32[4,64,128]{2,1,0:T(8,128)S(1)}, f32[4,64,128]{2,1,0:T(8,128)S(1)}, u32[]{:S(2)}, u32[]{:S(2)}) %collective-permute-start.13) | collective-permute-done | bytes 131104 | tf_op jit(solution)/shard_map/ppermute | solution.py:232
  75.9 0.0 collective-permute-done.9.refs_3_
  75.9 0.0 collective-permute-done.10.refs_6_
  75.9 0.0 collective-permute-done.12.refs_7_
  75.9 2.6 %shard_map.65 = (f32[16,64,128]{2,1,0:T(8,128)S(1)}, f32[1,64,128]{2,1,0:T(8,128)S(1)}) custom-call(s32[2]{0:T(128)S(1)} %pad_add_fusion.scal, f32[16,64,128]{2,1,0:T(8,128)S(1)} %get-tuple-element.58.refs_0_, f32[1,64,128]{2,1,0:T(8,128)S(1)} %get-tuple-element.59.refs_1_, f32[16,64,128]{2,1,0:T(8,128)S(1)} %get-tuple-element.50.refs_0_.refs_2_, ...), custom_call_target="tpu_custom_call" | custom-call | tf_op jit(solution)/shard_map/pallas_call | solution.py:23
  78.5 1.3 %collective-permute-start.14 = (f32[16,64,128]{2,1,0:T(8,128)S(1)}, f32[16,64,128]{2,1,0:T(8,128)S(1)}, u32[]{:S(2)}, u32[]{:S(2)}) collective-permute-start(f32[16,64,128]{2,1,0:T(8,128)S(1)} %get-tuple-element.61.v_ref), channel_id=1, source_target_pairs={{0,2},{1,3},{4,6},{5,7},{8,10},{9,11},{12,14},{13,15},{16,18},{17,... | collective-permute-start | bytes 1572872 | tf_op jit(solution)/shard_map/ppermute | solution.py:232
  79.9 8.6 %collective-permute-done.15.p2_ref = f32[16,64,128]{2,1,0:T(8,128)S(1)} collective-permute-done((f32[16,64,128]{2,1,0:T(8,128)S(1)}, f32[16,64,128]{2,1,0:T(8,128)S(1)}, u32[]{:S(2)}, u32[]{:S(2)}) %collective-permute-start.15) | collective-permute-done | bytes 524320 | tf_op jit(solution)/shard_map/ppermute | solution.py:232
  88.4 0.0 collective-permute-done.14.p_ref
  88.4 1.7 %shard_map.66 = (f32[16,64,128]{2,1,0:T(8,128)}, f32[16,64,128]{2,1,0:T(8,128)}) custom-call(s32[2]{0:T(128)S(1)} %pad_add_fusion.scal, f32[16,64,128]{2,1,0:T(8,128)S(1)} %get-tuple-element.61.v_ref, f32[1,64,128]{2,1,0:T(8,128)S(1)} %get-tuple-element.62.h_ref, f32[16,64,128]{2,1,0:T(8,128)S(1)} %get-tuple-element.36.refs_2_.refs_3_.refs_4_.s_ref, ...), custom_call_target="tpu_custom_call" | custom-call | tf_op jit(solution)/shard_map/pallas_call | solution.py:23
Async XLA Ops:
  2.7 13.3 %copy-start = (f32[1,16,64,128]{3,2,1,0:T(8,128)S(1)}, f32[1,16,64,128]{3,2,1,0:T(8,128)}, u32[]{:S(2)}) copy-start(f32[1,16,64,128]{3,2,1,0:T(8,128)} %param.4) | copy-start | bytes 1572868
  2.7 10.7 %collective-permute-start = (f32[8,64,128]{2,1,0:T(8,128)S(1)}, f32[8,64,128]{2,1,0:T(8,128)S(1)}, u32[]{:S(2)}, u32[]{:S(2)}) collective-permute-start(f32[8,64,128]{2,1,0:T(8,128)S(1)} %get-tuple-element.34), channel_id=1, source_target_pairs={{0,1},{1,0},{4,5},{5,4},{8,9},{9,8},{12,13},{13,12},{16,17},{17,16... | collective-permute-start | bytes 786440 | tf_op jit(solution)/shard_map/ppermute | solution.py:232
  14.0 7.1 %collective-permute-start.1 = (f32[20,64,128]{2,1,0:T(8,128)S(1)}, f32[20,64,128]{2,1,0:T(8,128)S(1)}, u32[]{:S(2)}, u32[]{:S(2)}) collective-permute-start(f32[20,64,128]{2,1,0:T(8,128)S(1)} %shard_map.60.refs_0_.refs_1_.refs_2_), channel_id=1, source_target_pairs={{0,2},{1,3},{4,6},{5,7},{8,10},{9,11},{12,14},{13,15},{16,18},{17,... | collective-permute-start | bytes 1966088 | tf_op jit(solution)/shard_map/ppermute | solution.py:232
  15.3 2.0 %collective-permute-start.2 = (f32[16,64,128]{2,1,0:T(8,128)S(1)}, f32[16,64,128]{2,1,0:T(8,128)S(1)}, u32[]{:S(2)}, u32[]{:S(2)}) collective-permute-start(f32[16,64,128]{2,1,0:T(8,128)S(1)} %get-tuple-element.37), channel_id=1, source_target_pairs={{3,2},{34,3},{5,6},{38,7},{9,10},{42,11},{13,14},{46,15},{17,18},{... | collective-permute-start | bytes 1572872 | tf_op jit(solution)/shard_map/ppermute | solution.py:232
  16.0 32.3 %collective-permute-start.3 = (f32[16,64,128]{2,1,0:T(8,128)S(1)}, f32[16,64,128]{2,1,0:T(8,128)S(1)}, u32[]{:S(2)}, u32[]{:S(2)}) collective-permute-start(f32[16,64,128]{2,1,0:T(8,128)S(1)} %bitcast.9), channel_id=1, source_target_pairs={{2,4},{3,5},{6,8},{7,9},{10,12},{11,13},{14,16},{15,17},{18,20},{1... | collective-permute-start | bytes 1572872 | tf_op jit(solution)/shard_map/ppermute | solution.py:232
  17.3 31.0 %collective-permute-start.5 = (f32[16,64,128]{2,1,0:T(8,128)S(1)}, f32[16,64,128]{2,1,0:T(8,128)S(1)}, u32[]{:S(2)}, u32[]{:S(2)}) collective-permute-start(f32[16,64,128]{2,1,0:T(8,128)S(1)} %collective-permute-done.2.refs_6_), channel_id=1, source_target_pairs={{2,0},{3,1},{6,4},{7,5},{10,8},{11,9},{14,12},{15,13},{18,16},{19,... | collective-permute-start | bytes 1572872 | tf_op jit(solution)/shard_map/ppermute | solution.py:232
  21.7 31.7 %collective-permute-start.11 = (f32[16,64,128]{2,1,0:T(8,128)S(1)}, f32[16,64,128]{2,1,0:T(8,128)S(1)}, u32[]{:S(2)}, u32[]{:S(2)}) collective-permute-start(f32[16,64,128]{2,1,0:T(8,128)S(1)} %get-tuple-element.43.refs_0_), channel_id=1, source_target_pairs={{31,63},{63,95},{95,127},{127,159},{159,191},{191,223},{223,255},{... | collective-permute-start | bytes 1572872 | tf_op jit(solution)/shard_map/ppermute | solution.py:232
  22.4 25.9 %collective-permute-start.4 = (f32[3,64,128]{2,1,0:T(8,128)S(1)}, f32[3,64,128]{2,1,0:T(8,128)S(1)}, u32[]{:S(2)}, u32[]{:S(2)}) collective-permute-start(f32[3,64,128]{2,1,0:T(8,128)S(1)} %get-tuple-element.44), channel_id=1, source_target_pairs={{2,5},{3,4},{6,9},{7,8},{10,13},{11,12},{14,17},{15,16},{18,21},{1... | collective-permute-start | bytes 294920 | tf_op jit(solution)/shard_map/ppermute | solution.py:232
  50.8 14.9 %collective-permute-start.7 = (f32[16,64,128]{2,1,0:T(8,128)S(1)}, f32[16,64,128]{2,1,0:T(8,128)S(1)}, u32[]{:S(2)}, u32[]{:S(2)}) collective-permute-start(f32[16,64,128]{2,1,0:T(8,128)S(1)} %get-tuple-element.50.refs_0_.refs_2_), channel_id=1, source_target_pairs={{0,2},{1,3},{4,6},{5,7},{8,10},{9,11},{12,14},{13,15},{16,18},{17,... | collective-permute-start | bytes 1572872 | tf_op jit(solution)/shard_map/ppermute | solution.py:232
  52.1 23.8 %collective-permute-start.10 = (f32[16,64,128]{2,1,0:T(8,128)S(1)}, f32[16,64,128]{2,1,0:T(8,128)S(1)}, u32[]{:S(2)}, u32[]{:S(2)}) collective-permute-start(f32[16,64,128]{2,1,0:T(8,128)S(1)} %get-tuple-element.43.refs_0_), channel_id=1, source_target_pairs={{2,4},{3,5},{6,8},{7,9},{10,12},{11,13},{14,16},{15,17},{18,20},{1... | collective-permute-start | bytes 1572872 | tf_op jit(solution)/shard_map/ppermute | solution.py:232
  53.4 22.5 %collective-permute-start.12 = (f32[16,64,128]{2,1,0:T(8,128)S(1)}, f32[16,64,128]{2,1,0:T(8,128)S(1)}, u32[]{:S(2)}, u32[]{:S(2)}) collective-permute-start(f32[16,64,128]{2,1,0:T(8,128)S(1)} %collective-permute-done.11), channel_id=1, source_target_pairs={{31,1},{63,33},{95,65},{127,97},{159,129},{191,161},{223,193},{255... | collective-permute-start | bytes 1572872 | tf_op jit(solution)/shard_map/ppermute | solution.py:232
  54.1 9.0 %collective-permute-start.8 = (f32[5,64,128]{2,1,0:T(8,128)S(1)}, f32[5,64,128]{2,1,0:T(8,128)S(1)}, u32[]{:S(2)}, u32[]{:S(2)}) collective-permute-start(f32[5,64,128]{2,1,0:T(8,128)S(1)} %get-tuple-element.52), channel_id=1, source_target_pairs={{0,3},{1,2},{4,7},{5,6},{8,11},{9,10},{12,15},{13,14},{16,19},{17,... | collective-permute-start | bytes 491528 | tf_op jit(solution)/shard_map/ppermute | solution.py:232
  55.4 9.0 %collective-permute-start.6 = (f32[5,64,128]{2,1,0:T(8,128)S(1)}, f32[5,64,128]{2,1,0:T(8,128)S(1)}, u32[]{:S(2)}, u32[]{:S(2)}) collective-permute-start(f32[5,64,128]{2,1,0:T(8,128)S(1)} %get-tuple-element.51), channel_id=1, source_target_pairs={{2,3},{3,2},{6,7},{7,6},{10,11},{11,10},{14,15},{15,14},{18,19},{1... | collective-permute-start | bytes 491528 | tf_op jit(solution)/shard_map/ppermute | solution.py:232
  63.1 12.8 %collective-permute-start.9 = (f32[5,64,128]{2,1,0:T(8,128)S(1)}, f32[5,64,128]{2,1,0:T(8,128)S(1)}, u32[]{:S(2)}, u32[]{:S(2)}) collective-permute-start(f32[5,64,128]{2,1,0:T(8,128)S(1)} %collective-permute-done.8.refs_5_), channel_id=1, source_target_pairs={{2,0},{3,1},{6,4},{7,5},{10,8},{11,9},{14,12},{15,13},{18,16},{19,... | collective-permute-start | bytes 491528 | tf_op jit(solution)/shard_map/ppermute | solution.py:232
  64.4 11.5 %collective-permute-start.13 = (f32[4,64,128]{2,1,0:T(8,128)S(1)}, f32[4,64,128]{2,1,0:T(8,128)S(1)}, u32[]{:S(2)}, u32[]{:S(2)}) collective-permute-start(f32[4,64,128]{2,1,0:T(8,128)S(1)} %get-tuple-element.60), channel_id=1, source_target_pairs={{2,5},{3,4},{6,9},{7,8},{10,13},{11,12},{14,17},{15,16},{18,21},{1... | collective-permute-start | bytes 393224 | tf_op jit(solution)/shard_map/ppermute | solution.py:232
  66.3 22.1 %collective-permute-start.15 = (f32[16,64,128]{2,1,0:T(8,128)S(1)}, f32[16,64,128]{2,1,0:T(8,128)S(1)}, u32[]{:S(2)}, u32[]{:S(2)}) collective-permute-start(f32[16,64,128]{2,1,0:T(8,128)S(1)} %get-tuple-element.58.refs_0_), channel_id=1, source_target_pairs={{2,4},{3,5},{6,8},{7,9},{10,12},{11,13},{14,16},{15,17},{18,20},{1... | collective-permute-start | bytes 1572872 | tf_op jit(solution)/shard_map/ppermute | solution.py:232
  78.5 9.9 %collective-permute-start.14 = (f32[16,64,128]{2,1,0:T(8,128)S(1)}, f32[16,64,128]{2,1,0:T(8,128)S(1)}, u32[]{:S(2)}, u32[]{:S(2)}) collective-permute-start(f32[16,64,128]{2,1,0:T(8,128)S(1)} %get-tuple-element.61.v_ref), channel_id=1, source_target_pairs={{0,2},{1,3},{4,6},{5,7},{8,10},{9,11},{12,14},{13,15},{16,18},{17,... | collective-permute-start | bytes 1572872 | tf_op jit(solution)/shard_map/ppermute | solution.py:232

commit v5 on v4

--- a/solution.py
+++ b/solution.py
@@ -13,7 +13,7 @@
 HALO = ITERS + 1
 F32 = jnp.float32
 ROLE, SIDE = 0, 1
-ROW, RUNS = 16, 4
+ROW, RUNS, CORES = 16, 4, 2
 HELPER = 6
 
 
@@ -33,7 +33,7 @@
     )(scalars, *far, *near)
 
 
-def pack_kernel(scal, init_ref, source_ref, spread_ref, upwind_ref, coef_out, field_out, thin_out, full_out, sem):
+def pack_kernel(scal, init_ref, source_ref, spread_ref, upwind_ref, coef_out, field_out, thin_out, sem):
     side = scal[SIDE]
     depth = init_ref.shape[0]
     thin = pl.ds((1 - side) * (depth - THIN), THIN)
@@ -42,7 +42,6 @@
         pltpu.make_async_copy(init_ref.at[wide], field_out.at[pl.ds(0, ITERS)], sem.at[0]),
         pltpu.make_async_copy(source_ref.at[wide], field_out.at[pl.ds(ITERS, ITERS)], sem.at[1]),
         pltpu.make_async_copy(init_ref.at[thin], thin_out, sem.at[6]),
-        pltpu.make_async_copy(init_ref, full_out.at[pl.ds(0, depth)], sem.at[7]),
         pltpu.make_async_copy(spread_ref.at[wide], coef_out.at[pl.ds(0, ITERS)], sem.at[2]),
     ]
     for i in range(3):
@@ -68,13 +67,14 @@
     return diagonal
 
 
-def own_kernel(scal, source_far, spread_far, upwind_far, c_ref, x_ref, y_ref, z_ref, inv_ref, diag_ref, source_ref, spread_ref, upwind_ref, sem):
+def own_kernel(scal, init_far, source_far, spread_far, upwind_far, c_ref, x_ref, y_ref, z_ref, inv_ref, diag_ref, source_ref, full_ref, spread_ref, upwind_ref, sem):
     side = scal[SIDE]
     depth = source_far.shape[0]
     copies = [
         pltpu.make_async_copy(spread_far, spread_ref, sem.at[0]),
         pltpu.make_async_copy(upwind_far, upwind_ref, sem.at[1]),
         pltpu.make_async_copy(source_far, source_ref, sem.at[2]),
+        pltpu.make_async_copy(init_far, full_ref.at[pl.ds(0, depth)], sem.at[3]),
     ]
     for copy in copies:
         copy.start()
@@ -88,7 +88,8 @@
         return carry
 
     lax.fori_loop(0, depth, own, 0, unroll=2)
-    copies[2].wait()
+    for copy in copies[2:]:
+        copy.wait()
 
 
 def join_kernel(scal, field_ref, held_ref, full_ref):
@@ -238,8 +239,8 @@
     into_even = [(number(t, s), number(t + 1, s)) for t in odd for s in sides]
     short_even = [(number(t, s), number(t + 1, s)) for t in odd for s in sides if t % ROW < ROW - 1 or s == 0]
     last = [t for t in odd if t % ROW == ROW - 1]
-    last_along = [(number(t, 1), number(t + ROW, 1)) for t in last]
-    last_around = [(number(t, 1), number(t + 1 - ROW, 1)) for t in last]
+    last_along = [(number(t, 1), number(t + 1 + CORES, 1)) for t in last]
+    last_around = [(number(t + 1 + CORES, 1), number(t + 1, 1)) for t in last]
     across_even = [(number(t, s), number(t, 1 - s)) for t in even for s in sides]
     across_odd = [(number(t, s), number(t, 1 - s)) for t in odd for s in sides]
     odd_across = [(number(t, s), number(t + 1, 1 - s)) for t in even for s in sides]
@@ -251,7 +252,9 @@
         if run < RUNS - 1:
             lower_odd.append((number(t + stride, 0), number(t, 1)))
         else:
-            lower_odd.append((number(t - t % group + HELPER if first else t - 1, 0), number(t, 1)))
+            end = t % stride == stride - 1
+            base = t - t % group
+            lower_odd.append((number(base + HELPER if first else base + stride - CORES if end else t - 1, 0), number(t, 1)))
     back = [(number(t, s), number(t - 1, s)) for t in odd for s in sides]
 
     plane = shape[1:]
@@ -261,23 +264,19 @@
     thin = (THIN,) + plane
     far = (initial, source, diffusion, advection)
 
-    coef_edge, field_edge, thin_edge, full = call(
-        pack_kernel,
-        [(4 * ITERS,) + plane, (2 * ITERS,) + plane, thin, (depth + ITERS,) + plane],
-        scalars,
-        far=far,
-        scratch=[pltpu.SemaphoreType.DMA((8,))],
+    coef_edge, field_edge, thin_edge = call(
+        pack_kernel, [(4 * ITERS,) + plane, (2 * ITERS,) + plane, thin], scalars, far=far, scratch=[pltpu.SemaphoreType.DMA((7,))]
     )
     si = permute(field_edge, across_even + across_odd)
     de = permute(thin_edge, even_across)
     b1 = permute(initial, into_even)
     sc = permute(coef_edge, lower_odd)
-    *coefs, diag, source_near = call(
+    *coefs, diag, source_near, full = call(
         own_kernel,
-        [ext] * 5 + [shape] * 2,
+        [ext] * 5 + [shape] * 2 + [(depth + ITERS,) + plane],
         scalars,
-        far=far[1:],
-        scratch=[pltpu.VMEM(shape, F32), pltpu.VMEM((3,) + shape, F32), pltpu.SemaphoreType.DMA((3,))],
+        far=far,
+        scratch=[pltpu.VMEM(shape, F32), pltpu.VMEM((3,) + shape, F32), pltpu.SemaphoreType.DMA((4,))],
     )
     (full,) = call(join_kernel, [(depth + ITERS,) + plane], scalars, si, full, aliases={2: 0})
     a1 = permute(full, into_odd)

time: 91.7 us -> 93.2 us (1.016); the launches traced: 90.1 us -> 92.7 us
  waiting for transfers between devices: 54.8 us -> 57.7 us
    ppermute x16, waiting for transfers between devices: 54.8 us -> 57.7 us  [permute(): return lax.ppermute(value, ('tm', 'space'), pairs)]
  transfers between devices with their start and end apart: 16 -> 16, of which waited for: 5 -> 5; matrix products, arithmetic and copies ran while one was open for 0% -> 0% of each run, Pallas kernels for 10% -> 9%
where the time goes in v5:
time: 93.2 us; the launch traced here: 92.7 us
  waiting for transfers between devices  57.7 us (62%)
  starting transfers between devices  21.3 us (23%)
  Pallas kernels  12.7 us (14%)
    ppermute x16, waiting for transfers between devices, permute(): return lax.ppermute(value, ('tm', 'space'), pairs)  57.7 us
    ppermute x16, starting transfers between devices, permute(): return lax.ppermute(value, ('tm', 'space'), pairs)  21.3 us
    pallas_call x8, Pallas kernels, call(): pl.pallas_call(kernel, out_shape=[o if not isinstance(o, tuple) else pltp...  12.7 us
  transfers between devices with their start and end apart: 16, of which 5 were waited for; matrix products, arithmetic and copies ran while one was open for 0% of the time, Pallas kernels for 9%

profile of v5, /device:TPU:6, one launch (start us, length us, event | category | flops | bytes accessed | tf_op | source)
XLA Modules:
  0.0 92.7 jit_solution(10228882729311577853)
XLA Ops:
  0.6 0.1 pad_add_fusion.scal
  0.7 1.9 %shard_map.59 = (f32[16,64,128]{2,1,0:T(8,128)S(1)}, f32[8,64,128]{2,1,0:T(8,128)S(1)}, f32[3,64,128]{2,1,0:T(8,128)S(1)}) custom-call(s32[2]{0:T(128)S(1)} %pad_add_fusion.scal, f32[16,64,128]{2,1,0:T(8,128)} %bitcast.8, f32[16,64,128]{2,1,0:T(8,128)} %bitcast.6, f32[16,64,128]{2,1,0:T(8,128)} %spread_far.1, f32[3,16,64,128]{3,2,1,0:T(8,128)} %upwind_far.1), custom_call_target="tpu_custom_call" | custom-call | tf_op jit(solution)/shard_map/pallas_call | solution.py:23
  2.6 4.3 %collective-permute-start = (f32[8,64,128]{2,1,0:T(8,128)S(1)}, f32[8,64,128]{2,1,0:T(8,128)S(1)}, u32[]{:S(2)}, u32[]{:S(2)}) collective-permute-start(f32[8,64,128]{2,1,0:T(8,128)S(1)} %get-tuple-element.34), channel_id=1, source_target_pairs={{0,1},{1,0},{4,5},{5,4},{8,9},{9,8},{12,13},{13,12},{16,17},{17,16... | collective-permute-start | bytes 786440 | tf_op jit(solution)/shard_map/ppermute | solution.py:233
  6.9 2.5 %shard_map.60 = (f32[21,64,128]{2,1,0:T(8,128)S(1)}, f32[21,64,128]{2,1,0:T(8,128)S(1)}, f32[21,64,128]{2,1,0:T(8,128)S(1)}, f32[21,64,128]{2,1,0:T(8,128)S(1)},...) custom-call(s32[2]{0:T(128)S(1)} %pad_add_fusion.scal, ...), custom_call_target="tpu_custom_call" | custom-call | tf_op jit(solution)/shard_map/pallas_call | solution.py:23
  9.3 0.0 copy-start
  9.3 3.8 %collective-permute-done.field_ref.refs_3_.refs_4_.refs_5_ = f32[8,64,128]{2,1,0:T(8,128)S(1)} collective-permute-done((f32[8,64,128]{2,1,0:T(8,128)S(1)}, f32[8,64,128]{2,1,0:T(8,128)S(1)}, u32[]{:S(2)}, u32[]{:S(2)}) %collective-permute-start) | collective-permute-done | bytes 262176 | tf_op jit(solution)/shard_map/ppermute | solution.py:233
  13.2 0.5 shard_map.61.refs_0_.refs_1_.refs_2_
  13.7 1.3 %collective-permute-start.1 = (f32[20,64,128]{2,1,0:T(8,128)S(1)}, f32[20,64,128]{2,1,0:T(8,128)S(1)}, u32[]{:S(2)}, u32[]{:S(2)}) collective-permute-start(f32[20,64,128]{2,1,0:T(8,128)S(1)} %shard_map.61.refs_0_.refs_1_.refs_2_), channel_id=1, source_target_pairs={{0,2},{1,3},{4,6},{5,7},{8,10},{9,11},{12,14},{13,15},{16,18},{17,... | collective-permute-start | bytes 1966088 | tf_op jit(solution)/shard_map/ppermute | solution.py:233
  15.1 0.7 collective-permute-start.2
  15.8 0.0 copy-done
  15.8 1.3 %collective-permute-start.3 = (f32[16,64,128]{2,1,0:T(8,128)S(1)}, f32[16,64,128]{2,1,0:T(8,128)S(1)}, u32[]{:S(2)}, u32[]{:S(2)}) collective-permute-start(f32[16,64,128]{2,1,0:T(8,128)S(1)} %bitcast.10), channel_id=1, source_target_pairs={{2,4},{3,5},{6,8},{7,9},{10,12},{11,13},{14,16},{15,17},{18,20},{1... | collective-permute-start | bytes 1572872 | tf_op jit(solution)/shard_map/ppermute | solution.py:233
  17.1 0.0 collective-permute-done.2.refs_6_
  17.1 1.3 %collective-permute-start.5 = (f32[16,64,128]{2,1,0:T(8,128)S(1)}, f32[16,64,128]{2,1,0:T(8,128)S(1)}, u32[]{:S(2)}, u32[]{:S(2)}) collective-permute-start(f32[16,64,128]{2,1,0:T(8,128)S(1)} %collective-permute-done.2.refs_6_), channel_id=1, source_target_pairs={{2,0},{3,1},{6,4},{7,5},{10,8},{11,9},{14,12},{15,13},{18,16},{19,... | collective-permute-start | bytes 1572872 | tf_op jit(solution)/shard_map/ppermute | solution.py:233
  18.4 0.0 collective-permute-done.1.refs_4_.refs_5_
  18.4 0.6 shard_map.62
  19.0 0.7 collective-permute-start.11
  19.7 1.3 %collective-permute-start.4 = (f32[3,64,128]{2,1,0:T(8,128)S(1)}, f32[3,64,128]{2,1,0:T(8,128)S(1)}, u32[]{:S(2)}, u32[]{:S(2)}) collective-permute-start(f32[3,64,128]{2,1,0:T(8,128)S(1)} %get-tuple-element.44), channel_id=1, source_target_pairs={{2,5},{3,4},{6,9},{7,8},{10,13},{11,12},{14,17},{15,16},{18,21},{1... | collective-permute-start | bytes 294920 | tf_op jit(solution)/shard_map/ppermute | solution.py:233
  21.0 29.0 %collective-permute-done.4.refs_6_ = f32[3,64,128]{2,1,0:T(8,128)S(1)} collective-permute-done((f32[3,64,128]{2,1,0:T(8,128)S(1)}, f32[3,64,128]{2,1,0:T(8,128)S(1)}, u32[]{:S(2)}, u32[]{:S(2)}) %collective-permute-start.4) | collective-permute-done | bytes 98336 | tf_op jit(solution)/shard_map/ppermute | solution.py:233
  49.9 0.0 collective-permute-done.3.refs_5_
  49.9 0.0 collective-permute-done.5.refs_7_
  49.9 2.5 %shard_map.63 = (f32[16,64,128]{2,1,0:T(8,128)S(1)}, f32[5,64,128]{2,1,0:T(8,128)S(1)}, f32[21,64,128]{2,1,0:T(8,128)S(1)}, f32[21,64,128]{2,1,0:T(8,128)S(1)}, ...) custom-call(s32[2]{0:T(128)S(1)} %pad_add_fusion.scal, ...), custom_call_target="tpu_custom_call", output_to_operand_aliasing={{2}: (9, {}), {3}: (10, {}), {4}: (11, {}), {5}: (12, {}), ... | custom-call | tf_op jit(solution)/shard_map/pallas_call | solution.py:23
  52.4 1.3 %collective-permute-start.7 = (f32[16,64,128]{2,1,0:T(8,128)S(1)}, f32[16,64,128]{2,1,0:T(8,128)S(1)}, u32[]{:S(2)}, u32[]{:S(2)}) collective-permute-start(f32[16,64,128]{2,1,0:T(8,128)S(1)} %get-tuple-element.50.refs_0_.refs_2_), channel_id=1, source_target_pairs={{0,2},{1,3},{4,6},{5,7},{8,10},{9,11},{12,14},{13,15},{16,18},{17,... | collective-permute-start | bytes 1572872 | tf_op jit(solution)/shard_map/ppermute | solution.py:233
  53.8 1.3 %collective-permute-start.10 = (f32[16,64,128]{2,1,0:T(8,128)S(1)}, f32[16,64,128]{2,1,0:T(8,128)S(1)}, u32[]{:S(2)}, u32[]{:S(2)}) collective-permute-start(f32[16,64,128]{2,1,0:T(8,128)S(1)} %get-tuple-element.43.refs_0_), channel_id=1, source_target_pairs={{2,4},{3,5},{6,8},{7,9},{10,12},{11,13},{14,16},{15,17},{18,20},{1... | collective-permute-start | bytes 1572872 | tf_op jit(solution)/shard_map/ppermute | solution.py:233
  55.1 0.0 collective-permute-done.11
  55.1 0.7 collective-permute-start.12
  55.8 1.3 %collective-permute-start.8 = (f32[5,64,128]{2,1,0:T(8,128)S(1)}, f32[5,64,128]{2,1,0:T(8,128)S(1)}, u32[]{:S(2)}, u32[]{:S(2)}) collective-permute-start(f32[5,64,128]{2,1,0:T(8,128)S(1)} %get-tuple-element.52), channel_id=1, source_target_pairs={{0,3},{1,2},{4,7},{5,6},{8,11},{9,10},{12,15},{13,14},{16,19},{17,... | collective-permute-start | bytes 491528 | tf_op jit(solution)/shard_map/ppermute | solution.py:233
  57.1 0.7 collective-permute-start.6
  57.8 2.7 %collective-permute-done.8.refs_5_ = f32[5,64,128]{2,1,0:T(8,128)S(1)} collective-permute-done((f32[5,64,128]{2,1,0:T(8,128)S(1)}, f32[5,64,128]{2,1,0:T(8,128)S(1)}, u32[]{:S(2)}, u32[]{:S(2)}) %collective-permute-start.8) | collective-permute-done | bytes 163872 | tf_op jit(solution)/shard_map/ppermute | solution.py:233
  60.5 1.3 %collective-permute-start.9 = (f32[5,64,128]{2,1,0:T(8,128)S(1)}, f32[5,64,128]{2,1,0:T(8,128)S(1)}, u32[]{:S(2)}, u32[]{:S(2)}) collective-permute-start(f32[5,64,128]{2,1,0:T(8,128)S(1)} %collective-permute-done.8.refs_5_), channel_id=1, source_target_pairs={{2,0},{3,1},{6,4},{7,5},{10,8},{11,9},{14,12},{15,13},{18,16},{19,... | collective-permute-start | bytes 491528 | tf_op jit(solution)/shard_map/ppermute | solution.py:233
  61.8 0.0 collective-permute-done.6.refs_1_
  61.8 1.3 %collective-permute-start.13 = (f32[4,64,128]{2,1,0:T(8,128)S(1)}, f32[4,64,128]{2,1,0:T(8,128)S(1)}, u32[]{:S(2)}, u32[]{:S(2)}) collective-permute-start(f32[4,64,128]{2,1,0:T(8,128)S(1)} %get-tuple-element.60), channel_id=1, source_target_pairs={{2,5},{3,4},{6,9},{7,8},{10,13},{11,12},{14,17},{15,16},{18,21},{1... | collective-permute-start | bytes 393224 | tf_op jit(solution)/shard_map/ppermute | solution.py:233
  63.1 0.0 collective-permute-done.7.refs_4_
  63.1 0.6 shard_map.64
  63.7 1.3 %collective-permute-start.15 = (f32[16,64,128]{2,1,0:T(8,128)S(1)}, f32[16,64,128]{2,1,0:T(8,128)S(1)}, u32[]{:S(2)}, u32[]{:S(2)}) collective-permute-start(f32[16,64,128]{2,1,0:T(8,128)S(1)} %get-tuple-element.58.refs_0_), channel_id=1, source_target_pairs={{2,4},{3,5},{6,8},{7,9},{10,12},{11,13},{14,16},{15,17},{18,20},{1... | collective-permute-start | bytes 1572872 | tf_op jit(solution)/shard_map/ppermute | solution.py:233
  65.0 12.8 %collective-permute-done.13.refs_8_ = f32[4,64,128]{2,1,0:T(8,128)S(1)} collective-permute-done((f32[4,64,128]{2,1,0:T(8,128)S(1)}, f32[4,64,128]{2,1,0:T(8,128)S(1)}, u32[]{:S(2)}, u32[]{:S(2)}) %collective-permute-start.13) | collective-permute-done | bytes 131104 | tf_op jit(solution)/shard_map/ppermute | solution.py:233
  77.8 0.0 collective-permute-done.9.refs_3_
  77.8 0.0 collective-permute-done.10.refs_6_
  77.8 0.0 collective-permute-done.12.refs_7_
  77.8 2.6 %shard_map.65 = (f32[16,64,128]{2,1,0:T(8,128)S(1)}, f32[1,64,128]{2,1,0:T(8,128)S(1)}) custom-call(s32[2]{0:T(128)S(1)} %pad_add_fusion.scal, f32[16,64,128]{2,1,0:T(8,128)S(1)} %get-tuple-element.58.refs_0_, f32[1,64,128]{2,1,0:T(8,128)S(1)} %get-tuple-element.59.refs_1_, f32[16,64,128]{2,1,0:T(8,128)S(1)} %get-tuple-element.50.refs_0_.refs_2_, ...), custom_call_target="tpu_custom_call" | custom-call | tf_op jit(solution)/shard_map/pallas_call | solution.py:23
  80.4 1.3 %collective-permute-start.14 = (f32[16,64,128]{2,1,0:T(8,128)S(1)}, f32[16,64,128]{2,1,0:T(8,128)S(1)}, u32[]{:S(2)}, u32[]{:S(2)}) collective-permute-start(f32[16,64,128]{2,1,0:T(8,128)S(1)} %get-tuple-element.61.v_ref), channel_id=1, source_target_pairs={{0,2},{1,3},{4,6},{5,7},{8,10},{9,11},{12,14},{13,15},{16,18},{17,... | collective-permute-start | bytes 1572872 | tf_op jit(solution)/shard_map/ppermute | solution.py:233
  81.7 9.4 %collective-permute-done.15.p2_ref = f32[16,64,128]{2,1,0:T(8,128)S(1)} collective-permute-done((f32[16,64,128]{2,1,0:T(8,128)S(1)}, f32[16,64,128]{2,1,0:T(8,128)S(1)}, u32[]{:S(2)}, u32[]{:S(2)}) %collective-permute-start.15) | collective-permute-done | bytes 524320 | tf_op jit(solution)/shard_map/ppermute | solution.py:233
  91.1 0.0 collective-permute-done.14.p_ref
  91.1 1.7 %shard_map.66 = (f32[16,64,128]{2,1,0:T(8,128)}, f32[16,64,128]{2,1,0:T(8,128)}) custom-call(s32[2]{0:T(128)S(1)} %pad_add_fusion.scal, f32[16,64,128]{2,1,0:T(8,128)S(1)} %get-tuple-element.61.v_ref, f32[1,64,128]{2,1,0:T(8,128)S(1)} %get-tuple-element.62.h_ref, f32[16,64,128]{2,1,0:T(8,128)S(1)} %get-tuple-element.36.refs_2_.refs_3_.refs_4_.s_ref, ...), custom_call_target="tpu_custom_call" | custom-call | tf_op jit(solution)/shard_map/pallas_call | solution.py:23
Async XLA Ops:
  2.6 10.6 %collective-permute-start = (f32[8,64,128]{2,1,0:T(8,128)S(1)}, f32[8,64,128]{2,1,0:T(8,128)S(1)}, u32[]{:S(2)}, u32[]{:S(2)}) collective-permute-start(f32[8,64,128]{2,1,0:T(8,128)S(1)} %get-tuple-element.34), channel_id=1, source_target_pairs={{0,1},{1,0},{4,5},{5,4},{8,9},{9,8},{12,13},{13,12},{16,17},{17,16... | collective-permute-start | bytes 786440 | tf_op jit(solution)/shard_map/ppermute | solution.py:233
  9.3 6.4 %copy-start = (f32[1,16,64,128]{3,2,1,0:T(8,128)S(1)}, f32[1,16,64,128]{3,2,1,0:T(8,128)}, u32[]{:S(2)}) copy-start(f32[1,16,64,128]{3,2,1,0:T(8,128)} %param.4) | copy-start | bytes 1572868
  13.7 4.7 %collective-permute-start.1 = (f32[20,64,128]{2,1,0:T(8,128)S(1)}, f32[20,64,128]{2,1,0:T(8,128)S(1)}, u32[]{:S(2)}, u32[]{:S(2)}) collective-permute-start(f32[20,64,128]{2,1,0:T(8,128)S(1)} %shard_map.61.refs_0_.refs_1_.refs_2_), channel_id=1, source_target_pairs={{0,2},{1,3},{4,6},{5,7},{8,10},{9,11},{12,14},{13,15},{16,18},{17,... | collective-permute-start | bytes 1966088 | tf_op jit(solution)/shard_map/ppermute | solution.py:233
  15.1 2.0 %collective-permute-start.2 = (f32[16,64,128]{2,1,0:T(8,128)S(1)}, f32[16,64,128]{2,1,0:T(8,128)S(1)}, u32[]{:S(2)}, u32[]{:S(2)}) collective-permute-start(f32[16,64,128]{2,1,0:T(8,128)S(1)} %get-tuple-element.37), channel_id=1, source_target_pairs={{3,2},{34,3},{5,6},{38,7},{9,10},{42,11},{13,14},{46,15},{17,18},{... | collective-permute-start | bytes 1572872 | tf_op jit(solution)/shard_map/ppermute | solution.py:233
  15.8 34.2 %collective-permute-start.3 = (f32[16,64,128]{2,1,0:T(8,128)S(1)}, f32[16,64,128]{2,1,0:T(8,128)S(1)}, u32[]{:S(2)}, u32[]{:S(2)}) collective-permute-start(f32[16,64,128]{2,1,0:T(8,128)S(1)} %bitcast.10), channel_id=1, source_target_pairs={{2,4},{3,5},{6,8},{7,9},{10,12},{11,13},{14,16},{15,17},{18,20},{1... | collective-permute-start | bytes 1572872 | tf_op jit(solution)/shard_map/ppermute | solution.py:233
  17.1 32.9 %collective-permute-start.5 = (f32[16,64,128]{2,1,0:T(8,128)S(1)}, f32[16,64,128]{2,1,0:T(8,128)S(1)}, u32[]{:S(2)}, u32[]{:S(2)}) collective-permute-start(f32[16,64,128]{2,1,0:T(8,128)S(1)} %collective-permute-done.2.refs_6_), channel_id=1, source_target_pairs={{2,0},{3,1},{6,4},{7,5},{10,8},{11,9},{14,12},{15,13},{18,16},{19,... | collective-permute-start | bytes 1572872 | tf_op jit(solution)/shard_map/ppermute | solution.py:233
  19.0 36.1 %collective-permute-start.11 = (f32[16,64,128]{2,1,0:T(8,128)S(1)}, f32[16,64,128]{2,1,0:T(8,128)S(1)}, u32[]{:S(2)}, u32[]{:S(2)}) collective-permute-start(f32[16,64,128]{2,1,0:T(8,128)S(1)} %get-tuple-element.43.refs_0_), channel_id=1, source_target_pairs={{31,37},{63,69},{95,101},{127,133},{159,165},{191,197},{223,229},{... | collective-permute-start | bytes 1572872 | tf_op jit(solution)/shard_map/ppermute | solution.py:233
  19.7 30.3 %collective-permute-start.4 = (f32[3,64,128]{2,1,0:T(8,128)S(1)}, f32[3,64,128]{2,1,0:T(8,128)S(1)}, u32[]{:S(2)}, u32[]{:S(2)}) collective-permute-start(f32[3,64,128]{2,1,0:T(8,128)S(1)} %get-tuple-element.44), channel_id=1, source_target_pairs={{2,5},{3,4},{6,9},{7,8},{10,13},{11,12},{14,17},{15,16},{18,21},{1... | collective-permute-start | bytes 294920 | tf_op jit(solution)/shard_map/ppermute | solution.py:233
  52.4 10.7 %collective-permute-start.7 = (f32[16,64,128]{2,1,0:T(8,128)S(1)}, f32[16,64,128]{2,1,0:T(8,128)S(1)}, u32[]{:S(2)}, u32[]{:S(2)}) collective-permute-start(f32[16,64,128]{2,1,0:T(8,128)S(1)} %get-tuple-element.50.refs_0_.refs_2_), channel_id=1, source_target_pairs={{0,2},{1,3},{4,6},{5,7},{8,10},{9,11},{12,14},{13,15},{16,18},{17,... | collective-permute-start | bytes 1572872 | tf_op jit(solution)/shard_map/ppermute | solution.py:233
  53.8 24.0 %collective-permute-start.10 = (f32[16,64,128]{2,1,0:T(8,128)S(1)}, f32[16,64,128]{2,1,0:T(8,128)S(1)}, u32[]{:S(2)}, u32[]{:S(2)}) collective-permute-start(f32[16,64,128]{2,1,0:T(8,128)S(1)} %get-tuple-element.43.refs_0_), channel_id=1, source_target_pairs={{2,4},{3,5},{6,8},{7,9},{10,12},{11,13},{14,16},{15,17},{18,20},{1... | collective-permute-start | bytes 1572872 | tf_op jit(solution)/shard_map/ppermute | solution.py:233
  55.1 22.7 %collective-permute-start.12 = (f32[16,64,128]{2,1,0:T(8,128)S(1)}, f32[16,64,128]{2,1,0:T(8,128)S(1)}, u32[]{:S(2)}, u32[]{:S(2)}) collective-permute-start(f32[16,64,128]{2,1,0:T(8,128)S(1)} %collective-permute-done.11), channel_id=1, source_target_pairs={{37,33},{69,65},{101,97},{133,129},{165,161},{197,193},{229,225},{... | collective-permute-start | bytes 1572872 | tf_op jit(solution)/shard_map/ppermute | solution.py:233
  55.8 4.7 %collective-permute-start.8 = (f32[5,64,128]{2,1,0:T(8,128)S(1)}, f32[5,64,128]{2,1,0:T(8,128)S(1)}, u32[]{:S(2)}, u32[]{:S(2)}) collective-permute-start(f32[5,64,128]{2,1,0:T(8,128)S(1)} %get-tuple-element.52), channel_id=1, source_target_pairs={{0,3},{1,2},{4,7},{5,6},{8,11},{9,10},{12,15},{13,14},{16,19},{17,... | collective-permute-start | bytes 491528 | tf_op jit(solution)/shard_map/ppermute | solution.py:233
  57.1 4.7 %collective-permute-start.6 = (f32[5,64,128]{2,1,0:T(8,128)S(1)}, f32[5,64,128]{2,1,0:T(8,128)S(1)}, u32[]{:S(2)}, u32[]{:S(2)}) collective-permute-start(f32[5,64,128]{2,1,0:T(8,128)S(1)} %get-tuple-element.51), channel_id=1, source_target_pairs={{2,3},{3,2},{6,7},{7,6},{10,11},{11,10},{14,15},{15,14},{18,19},{1... | collective-permute-start | bytes 491528 | tf_op jit(solution)/shard_map/ppermute | solution.py:233
  60.5 17.3 %collective-permute-start.9 = (f32[5,64,128]{2,1,0:T(8,128)S(1)}, f32[5,64,128]{2,1,0:T(8,128)S(1)}, u32[]{:S(2)}, u32[]{:S(2)}) collective-permute-start(f32[5,64,128]{2,1,0:T(8,128)S(1)} %collective-permute-done.8.refs_5_), channel_id=1, source_target_pairs={{2,0},{3,1},{6,4},{7,5},{10,8},{11,9},{14,12},{15,13},{18,16},{19,... | collective-permute-start | bytes 491528 | tf_op jit(solution)/shard_map/ppermute | solution.py:233
  61.8 16.0 %collective-permute-start.13 = (f32[4,64,128]{2,1,0:T(8,128)S(1)}, f32[4,64,128]{2,1,0:T(8,128)S(1)}, u32[]{:S(2)}, u32[]{:S(2)}) collective-permute-start(f32[4,64,128]{2,1,0:T(8,128)S(1)} %get-tuple-element.60), channel_id=1, source_target_pairs={{2,5},{3,4},{6,9},{7,8},{10,13},{11,12},{14,17},{15,16},{18,21},{1... | collective-permute-start | bytes 393224 | tf_op jit(solution)/shard_map/ppermute | solution.py:233
  63.7 27.4 %collective-permute-start.15 = (f32[16,64,128]{2,1,0:T(8,128)S(1)}, f32[16,64,128]{2,1,0:T(8,128)S(1)}, u32[]{:S(2)}, u32[]{:S(2)}) collective-permute-start(f32[16,64,128]{2,1,0:T(8,128)S(1)} %get-tuple-element.58.refs_0_), channel_id=1, source_target_pairs={{2,4},{3,5},{6,8},{7,9},{10,12},{11,13},{14,16},{15,17},{18,20},{1... | collective-permute-start | bytes 1572872 | tf_op jit(solution)/shard_map/ppermute | solution.py:233
  80.4 10.7 %collective-permute-start.14 = (f32[16,64,128]{2,1,0:T(8,128)S(1)}, f32[16,64,128]{2,1,0:T(8,128)S(1)}, u32[]{:S(2)}, u32[]{:S(2)}) collective-permute-start(f32[16,64,128]{2,1,0:T(8,128)S(1)} %get-tuple-element.61.v_ref), channel_id=1, source_target_pairs={{0,2},{1,3},{4,6},{5,7},{8,10},{9,11},{12,14},{13,15},{16,18},{17,... | collective-permute-start | bytes 1572872 | tf_op jit(solution)/shard_map/ppermute | solution.py:233

commit v6 on v5

--- a/solution.py
+++ b/solution.py
@@ -190,11 +190,11 @@
             edge_ref[q] = out_ref[jnp.where(side == 1, q, depth - width + q)]
 
 
-def residual_kernel(scal, v_ref, h_ref, s_ref, c_ref, x_ref, y_ref, z_ref, diag_ref, p_ref, p2_ref, far_v, far_out, va, out_ref, sem):
+def defect_kernel(scal, v_ref, h_ref, s_ref, c_ref, x_ref, y_ref, z_ref, diag_ref, far_v, out_ref, va, sem):
     side = scal[SIDE]
     depth, nx, ny = v_ref.shape
-    copies = [pltpu.make_async_copy(v_ref, far_v, sem.at[0])]
-    copies[0].start()
+    copy = pltpu.make_async_copy(v_ref, far_v, sem)
+    copy.start()
     row_last, lane_last = last_masks(nx, ny)
     zero = jnp.zeros((nx, ny), F32)
     halo = h_ref[0]
@@ -202,17 +202,24 @@
     va[depth + 1] = jnp.where(side == 1, zero, halo)
     for z in range(depth):
         va[1 + z] = v_ref[z]
-    pieces = sem.shape[0] - 1
-    size = depth // pieces
     for z in range(depth):
         e = HALO * side + z
         here = va[1 + z]
         m = stencil(va[z], here, va[z + 2], c_ref[e], x_ref[e], y_ref[e], z_ref[e], row_last, lane_last)
-        out_ref[z] = (s_ref[z] - diag_ref[z] * (here - m)) + (p_ref[z] + p2_ref[z])
-        if (z + 1) % size == 0:
-            part = pl.ds(z + 1 - size, size)
-            copies.append(pltpu.make_async_copy(out_ref.at[part], far_out.at[part], sem.at[len(copies)]))
-            copies[-1].start()
+        out_ref[z] = s_ref[z] - diag_ref[z] * (here - m)
+    copy.wait()
+
+
+def add_kernel(scal, d_ref, p_ref, p2_ref, far_out, out_ref, sem):
+    pieces = sem.shape[0]
+    size = out_ref.shape[0] // pieces
+    copies = []
+    for i in range(pieces):
+        part = pl.ds(i * size, size)
+        for z in range(i * size, (i + 1) * size):
+            out_ref[z] = d_ref[z] + (p_ref[z] + p2_ref[z])
+        copies.append(pltpu.make_async_copy(out_ref.at[part], far_out.at[part], sem.at[i]))
+        copies[-1].start()
     for copy in copies:
         copy.wait()
 
@@ -298,28 +305,29 @@
     b2 = permute(x, short_even)
     sx = permute(xw, across_odd)
     zh = permute(x, last_along)
-    s1, yw = sweep(0, (x,), full, full, (b1,), de, (0, THIN), depth, (HALO,), rims=(ac,))
+    s1, yw = sweep(0, (), full, full, (b1,), de, (0, THIN), depth, (HALO,), rims=(ac,))
     dy = permute(yw, odd_across)
     a2 = permute(s1, into_odd)
     dx = permute(xt, even_across)
     yh = permute(zh, last_around)
-    z, zh1 = sweep(1, (), s1, sx, (a2,), dy, (0, HALO), extra=1)
+    z, zh1 = sweep(1, (), x, sx, (a2,), dy, (0, HALO), extra=1)
     b3 = permute(z, into_even)
     ey = permute(dy, back)
     s2, s2h = sweep(0, (z, zh1), s1, ey, (b2, yh), dx, (0, ITERS), extra=1)
     a3 = permute(s2, into_odd)
-    s2_far, residual = call(
-        residual_kernel,
-        [pltpu.HBM(shape, F32)] * 2,
+    s2_far, defect = call(
+        defect_kernel,
+        [pltpu.HBM(shape, F32), shape],
         scalars,
         s2,
         s2h,
         source_near,
         *coefs[:4],
         diag,
-        a3,
-        b3,
-        scratch=[pltpu.VMEM((depth + 2,) + plane, F32), pltpu.VMEM(shape, F32), pltpu.SemaphoreType.DMA((5,))],
+        scratch=[pltpu.VMEM((depth + 2,) + plane, F32), pltpu.SemaphoreType.DMA],
+    )
+    (residual,) = call(
+        add_kernel, [pltpu.HBM(shape, F32)], scalars, defect, a3, b3, scratch=[pltpu.VMEM(shape, F32), pltpu.SemaphoreType.DMA((2,))]
     )
     return (s2_far[None], residual[None])
 

time: 93.2 us -> 92.9 us (level)
  waiting for transfers between devices: 57.7 us -> 56.4 us
  Pallas kernels: 12.7 us -> 13.8 us
    ppermute x16, waiting for transfers between devices: 57.7 us -> 56.4 us  [permute(): return lax.ppermute(value, ('tm', 'space'), pairs)]
    pallas_call x8 -> x9, Pallas kernels: 12.7 us -> 13.8 us  [call(): pl.pallas_call(kernel, out_shape=[o if not isinstance(o, tuple) else pltp...]
  transfers between devices with their start and end apart: 16 -> 16, of which waited for: 5 -> 5; matrix products, arithmetic and copies ran while one was open for 0% -> 0% of each run, Pallas kernels for 9% -> 11%
where the time goes in v6:
time: 92.9 us; the launch traced here: 92.5 us
  waiting for transfers between devices  56.4 us (61%)
  starting transfers between devices  21.3 us (23%)
  Pallas kernels  13.8 us (15%)
    ppermute x16, waiting for transfers between devices, permute(): return lax.ppermute(value, ('tm', 'space'), pairs)  56.4 us
    ppermute x16, starting transfers between devices, permute(): return lax.ppermute(value, ('tm', 'space'), pairs)  21.3 us
    pallas_call x9, Pallas kernels, call(): pl.pallas_call(kernel, out_shape=[o if not isinstance(o, tuple) else pltp...  13.8 us
  transfers between devices with their start and end apart: 16, of which 5 were waited for; matrix products, arithmetic and copies ran while one was open for 0% of the time, Pallas kernels for 11%

profile of v6, /device:TPU:6, one launch (start us, length us, event | category | flops | bytes accessed | tf_op | source)
XLA Modules:
  0.0 92.5 jit_solution(1036946303880898829)
XLA Ops:
  0.6 0.1 pad_add_fusion.scal
  0.7 1.9 %shard_map.59 = (f32[16,64,128]{2,1,0:T(8,128)S(1)}, f32[8,64,128]{2,1,0:T(8,128)S(1)}, f32[3,64,128]{2,1,0:T(8,128)S(1)}) custom-call(s32[2]{0:T(128)S(1)} %pad_add_fusion.scal, f32[16,64,128]{2,1,0:T(8,128)} %bitcast.8, f32[16,64,128]{2,1,0:T(8,128)} %bitcast.6, f32[16,64,128]{2,1,0:T(8,128)} %spread_far.1, f32[3,16,64,128]{3,2,1,0:T(8,128)} %upwind_far.1), custom_call_target="tpu_custom_call" | custom-call | tf_op jit(solution)/shard_map/pallas_call | solution.py:23
  2.6 4.3 %collective-permute-start = (f32[8,64,128]{2,1,0:T(8,128)S(1)}, f32[8,64,128]{2,1,0:T(8,128)S(1)}, u32[]{:S(2)}, u32[]{:S(2)}) collective-permute-start(f32[8,64,128]{2,1,0:T(8,128)S(1)} %get-tuple-element.34), channel_id=1, source_target_pairs={{0,1},{1,0},{4,5},{5,4},{8,9},{9,8},{12,13},{13,12},{16,17},{17,16... | collective-permute-start | bytes 786440 | tf_op jit(solution)/shard_map/ppermute | solution.py:240
  6.9 2.5 %shard_map.60 = (f32[21,64,128]{2,1,0:T(8,128)S(1)}, f32[21,64,128]{2,1,0:T(8,128)S(1)}, f32[21,64,128]{2,1,0:T(8,128)S(1)}, f32[21,64,128]{2,1,0:T(8,128)S(1)},...) custom-call(s32[2]{0:T(128)S(1)} %pad_add_fusion.scal, ...), custom_call_target="tpu_custom_call" | custom-call | tf_op jit(solution)/shard_map/pallas_call | solution.py:23
  9.3 0.0 copy-start
  9.3 3.8 %collective-permute-done.field_ref.refs_3_.refs_5_ = f32[8,64,128]{2,1,0:T(8,128)S(1)} collective-permute-done((f32[8,64,128]{2,1,0:T(8,128)S(1)}, f32[8,64,128]{2,1,0:T(8,128)S(1)}, u32[]{:S(2)}, u32[]{:S(2)}) %collective-permute-start) | collective-permute-done | bytes 262176 | tf_op jit(solution)/shard_map/ppermute | solution.py:240
  13.2 0.5 shard_map.61.refs_0_.refs_1_
  13.7 1.3 %collective-permute-start.1 = (f32[20,64,128]{2,1,0:T(8,128)S(1)}, f32[20,64,128]{2,1,0:T(8,128)S(1)}, u32[]{:S(2)}, u32[]{:S(2)}) collective-permute-start(f32[20,64,128]{2,1,0:T(8,128)S(1)} %shard_map.61.refs_0_.refs_1_), channel_id=1, source_target_pairs={{0,2},{1,3},{4,6},{5,7},{8,10},{9,11},{12,14},{13,15},{16,18},{17,... | collective-permute-start | bytes 1966088 | tf_op jit(solution)/shard_map/ppermute | solution.py:240
  15.1 0.7 collective-permute-start.2
  15.8 0.0 copy-done
  15.8 1.3 %collective-permute-start.4 = (f32[16,64,128]{2,1,0:T(8,128)S(1)}, f32[16,64,128]{2,1,0:T(8,128)S(1)}, u32[]{:S(2)}, u32[]{:S(2)}) collective-permute-start(f32[16,64,128]{2,1,0:T(8,128)S(1)} %bitcast.10), channel_id=1, source_target_pairs={{2,4},{3,5},{6,8},{7,9},{10,12},{11,13},{14,16},{15,17},{18,20},{1... | collective-permute-start | bytes 1572872 | tf_op jit(solution)/shard_map/ppermute | solution.py:240
  17.1 0.0 collective-permute-done.2.refs_6_
  17.1 1.3 %collective-permute-start.6 = (f32[16,64,128]{2,1,0:T(8,128)S(1)}, f32[16,64,128]{2,1,0:T(8,128)S(1)}, u32[]{:S(2)}, u32[]{:S(2)}) collective-permute-start(f32[16,64,128]{2,1,0:T(8,128)S(1)} %collective-permute-done.2.refs_6_), channel_id=1, source_target_pairs={{2,0},{3,1},{6,4},{7,5},{10,8},{11,9},{14,12},{15,13},{18,16},{19,... | collective-permute-start | bytes 1572872 | tf_op jit(solution)/shard_map/ppermute | solution.py:240
  18.4 0.0 collective-permute-done.1.refs_4_.refs_5_
  18.4 0.6 shard_map.62
  19.0 0.7 collective-permute-start.11
  19.7 1.3 %collective-permute-start.5 = (f32[3,64,128]{2,1,0:T(8,128)S(1)}, f32[3,64,128]{2,1,0:T(8,128)S(1)}, u32[]{:S(2)}, u32[]{:S(2)}) collective-permute-start(f32[3,64,128]{2,1,0:T(8,128)S(1)} %get-tuple-element.45), channel_id=1, source_target_pairs={{2,5},{3,4},{6,9},{7,8},{10,13},{11,12},{14,17},{15,16},{18,21},{1... | collective-permute-start | bytes 294920 | tf_op jit(solution)/shard_map/ppermute | solution.py:240
  21.0 29.0 %collective-permute-done.5.refs_5_ = f32[3,64,128]{2,1,0:T(8,128)S(1)} collective-permute-done((f32[3,64,128]{2,1,0:T(8,128)S(1)}, f32[3,64,128]{2,1,0:T(8,128)S(1)}, u32[]{:S(2)}, u32[]{:S(2)}) %collective-permute-start.5) | collective-permute-done | bytes 98336 | tf_op jit(solution)/shard_map/ppermute | solution.py:240
  49.9 0.0 collective-permute-done.4.refs_4_
  49.9 0.0 collective-permute-done.6.refs_6_
  49.9 2.5 %shard_map.63 = (f32[16,64,128]{2,1,0:T(8,128)S(1)}, f32[5,64,128]{2,1,0:T(8,128)S(1)}, f32[21,64,128]{2,1,0:T(8,128)S(1)}, f32[21,64,128]{2,1,0:T(8,128)S(1)}, ...) custom-call(s32[2]{0:T(128)S(1)} %pad_add_fusion.scal, ...), custom_call_target="tpu_custom_call", output_to_operand_aliasing={{2}: (8, {}), {3}: (9, {}), {4}: (10, {}), {5}: (11, {}), {... | custom-call | tf_op jit(solution)/shard_map/pallas_call | solution.py:23
  52.4 1.3 %collective-permute-start.7 = (f32[16,64,128]{2,1,0:T(8,128)S(1)}, f32[16,64,128]{2,1,0:T(8,128)S(1)}, u32[]{:S(2)}, u32[]{:S(2)}) collective-permute-start(f32[16,64,128]{2,1,0:T(8,128)S(1)} %get-tuple-element.51.refs_2_), channel_id=1, source_target_pairs={{0,2},{1,3},{4,6},{5,7},{8,10},{9,11},{12,14},{13,15},{16,18},{17,... | collective-permute-start | bytes 1572872 | tf_op jit(solution)/shard_map/ppermute | solution.py:240
  53.8 1.3 %collective-permute-start.10 = (f32[16,64,128]{2,1,0:T(8,128)S(1)}, f32[16,64,128]{2,1,0:T(8,128)S(1)}, u32[]{:S(2)}, u32[]{:S(2)}) collective-permute-start(f32[16,64,128]{2,1,0:T(8,128)S(1)} %get-tuple-element.43.refs_0_), channel_id=1, source_target_pairs={{2,4},{3,5},{6,8},{7,9},{10,12},{11,13},{14,16},{15,17},{18,20},{1... | collective-permute-start | bytes 1572872 | tf_op jit(solution)/shard_map/ppermute | solution.py:240
  55.1 0.0 collective-permute-done.11
  55.1 0.7 collective-permute-start.12
  55.8 1.3 %collective-permute-start.8 = (f32[5,64,128]{2,1,0:T(8,128)S(1)}, f32[5,64,128]{2,1,0:T(8,128)S(1)}, u32[]{:S(2)}, u32[]{:S(2)}) collective-permute-start(f32[5,64,128]{2,1,0:T(8,128)S(1)} %get-tuple-element.52), channel_id=1, source_target_pairs={{0,3},{1,2},{4,7},{5,6},{8,11},{9,10},{12,15},{13,14},{16,19},{17,... | collective-permute-start | bytes 491528 | tf_op jit(solution)/shard_map/ppermute | solution.py:240
  57.1 0.7 collective-permute-start.3
  57.8 2.7 %collective-permute-done.8.refs_5_ = f32[5,64,128]{2,1,0:T(8,128)S(1)} collective-permute-done((f32[5,64,128]{2,1,0:T(8,128)S(1)}, f32[5,64,128]{2,1,0:T(8,128)S(1)}, u32[]{:S(2)}, u32[]{:S(2)}) %collective-permute-start.8) | collective-permute-done | bytes 163872 | tf_op jit(solution)/shard_map/ppermute | solution.py:240
  60.5 1.3 %collective-permute-start.9 = (f32[5,64,128]{2,1,0:T(8,128)S(1)}, f32[5,64,128]{2,1,0:T(8,128)S(1)}, u32[]{:S(2)}, u32[]{:S(2)}) collective-permute-start(f32[5,64,128]{2,1,0:T(8,128)S(1)} %collective-permute-done.8.refs_5_), channel_id=1, source_target_pairs={{2,0},{3,1},{6,4},{7,5},{10,8},{11,9},{14,12},{15,13},{18,16},{19,... | collective-permute-start | bytes 491528 | tf_op jit(solution)/shard_map/ppermute | solution.py:240
  61.8 0.0 collective-permute-done.3.refs_1_
  61.8 1.3 %collective-permute-start.13 = (f32[4,64,128]{2,1,0:T(8,128)S(1)}, f32[4,64,128]{2,1,0:T(8,128)S(1)}, u32[]{:S(2)}, u32[]{:S(2)}) collective-permute-start(f32[4,64,128]{2,1,0:T(8,128)S(1)} %get-tuple-element.60), channel_id=1, source_target_pairs={{2,5},{3,4},{6,9},{7,8},{10,13},{11,12},{14,17},{15,16},{18,21},{1... | collective-permute-start | bytes 393224 | tf_op jit(solution)/shard_map/ppermute | solution.py:240
  63.1 0.0 collective-permute-done.7.refs_4_
  63.1 0.6 shard_map.64
  63.7 1.3 %collective-permute-start.15 = (f32[16,64,128]{2,1,0:T(8,128)S(1)}, f32[16,64,128]{2,1,0:T(8,128)S(1)}, u32[]{:S(2)}, u32[]{:S(2)}) collective-permute-start(f32[16,64,128]{2,1,0:T(8,128)S(1)} %get-tuple-element.58.refs_0_), channel_id=1, source_target_pairs={{2,4},{3,5},{6,8},{7,9},{10,12},{11,13},{14,16},{15,17},{18,20},{1... | collective-permute-start | bytes 1572872 | tf_op jit(solution)/shard_map/ppermute | solution.py:240
  65.0 12.9 %collective-permute-done.13.refs_8_ = f32[4,64,128]{2,1,0:T(8,128)S(1)} collective-permute-done((f32[4,64,128]{2,1,0:T(8,128)S(1)}, f32[4,64,128]{2,1,0:T(8,128)S(1)}, u32[]{:S(2)}, u32[]{:S(2)}) %collective-permute-start.13) | collective-permute-done | bytes 131104 | tf_op jit(solution)/shard_map/ppermute | solution.py:240
  77.8 0.0 collective-permute-done.9.refs_3_
  77.8 0.0 collective-permute-done.10.refs_6_
  77.8 0.0 collective-permute-done.12.refs_7_
  77.8 2.6 %shard_map.65 = (f32[16,64,128]{2,1,0:T(8,128)S(1)}, f32[1,64,128]{2,1,0:T(8,128)S(1)}) custom-call(s32[2]{0:T(128)S(1)} %pad_add_fusion.scal, f32[16,64,128]{2,1,0:T(8,128)S(1)} %get-tuple-element.58.refs_0_, f32[1,64,128]{2,1,0:T(8,128)S(1)} %get-tuple-element.59.refs_1_, f32[16,64,128]{2,1,0:T(8,128)S(1)} %get-tuple-element.51.refs_2_, ...), custom_call_target="tpu_custom_call" | custom-call | tf_op jit(solution)/shard_map/pallas_call | solution.py:23
  80.4 1.3 %collective-permute-start.14 = (f32[16,64,128]{2,1,0:T(8,128)S(1)}, f32[16,64,128]{2,1,0:T(8,128)S(1)}, u32[]{:S(2)}, u32[]{:S(2)}) collective-permute-start(f32[16,64,128]{2,1,0:T(8,128)S(1)} %get-tuple-element.61.v_ref), channel_id=1, source_target_pairs={{0,2},{1,3},{4,6},{5,7},{8,10},{9,11},{12,14},{13,15},{16,18},{17,... | collective-permute-start | bytes 1572872 | tf_op jit(solution)/shard_map/ppermute | solution.py:240
  81.7 1.3 %shard_map.66 = (f32[16,64,128]{2,1,0:T(8,128)}, f32[16,64,128]{2,1,0:T(8,128)S(1)}) custom-call(s32[2]{0:T(128)S(1)} %pad_add_fusion.scal, f32[16,64,128]{2,1,0:T(8,128)S(1)} %get-tuple-element.61.v_ref, f32[1,64,128]{2,1,0:T(8,128)S(1)} %get-tuple-element.62.h_ref, f32[16,64,128]{2,1,0:T(8,128)S(1)} %get-tuple-element.36.refs_2_.refs_4_.s_ref, ...), custom_call_target="tpu_custom_call" | custom-call | tf_op jit(solution)/shard_map/pallas_call | solution.py:23
  83.1 8.0 %collective-permute-done.15.p2_ref = f32[16,64,128]{2,1,0:T(8,128)S(1)} collective-permute-done((f32[16,64,128]{2,1,0:T(8,128)S(1)}, f32[16,64,128]{2,1,0:T(8,128)S(1)}, u32[]{:S(2)}, u32[]{:S(2)}) %collective-permute-start.15) | collective-permute-done | bytes 524320 | tf_op jit(solution)/shard_map/ppermute | solution.py:240
  91.1 0.0 collective-permute-done.14.p_ref
  91.1 1.4 %shard_map.67 = f32[16,64,128]{2,1,0:T(8,128)} custom-call(s32[2]{0:T(128)S(1)} %pad_add_fusion.scal, f32[16,64,128]{2,1,0:T(8,128)S(1)} %get-tuple-element.65.d_ref, f32[16,64,128]{2,1,0:T(8,128)S(1)} %collective-permute-done.14.p_ref, f32[16,64,128]{2,1,0:T(8,128)S(1)} %collective-permute-done.15.p2_ref), custom_call_target="tpu_custom_call" | custom-call | tf_op jit(solution)/shard_map/pallas_call | solution.py:23
Async XLA Ops:
  2.6 10.6 %collective-permute-start = (f32[8,64,128]{2,1,0:T(8,128)S(1)}, f32[8,64,128]{2,1,0:T(8,128)S(1)}, u32[]{:S(2)}, u32[]{:S(2)}) collective-permute-start(f32[8,64,128]{2,1,0:T(8,128)S(1)} %get-tuple-element.34), channel_id=1, source_target_pairs={{0,1},{1,0},{4,5},{5,4},{8,9},{9,8},{12,13},{13,12},{16,17},{17,16... | collective-permute-start | bytes 786440 | tf_op jit(solution)/shard_map/ppermute | solution.py:240
  9.3 6.4 %copy-start = (f32[1,16,64,128]{3,2,1,0:T(8,128)S(1)}, f32[1,16,64,128]{3,2,1,0:T(8,128)}, u32[]{:S(2)}) copy-start(f32[1,16,64,128]{3,2,1,0:T(8,128)} %param.4) | copy-start | bytes 1572868
  13.7 4.7 %collective-permute-start.1 = (f32[20,64,128]{2,1,0:T(8,128)S(1)}, f32[20,64,128]{2,1,0:T(8,128)S(1)}, u32[]{:S(2)}, u32[]{:S(2)}) collective-permute-start(f32[20,64,128]{2,1,0:T(8,128)S(1)} %shard_map.61.refs_0_.refs_1_), channel_id=1, source_target_pairs={{0,2},{1,3},{4,6},{5,7},{8,10},{9,11},{12,14},{13,15},{16,18},{17,... | collective-permute-start | bytes 1966088 | tf_op jit(solution)/shard_map/ppermute | solution.py:240
  15.1 2.0 %collective-permute-start.2 = (f32[16,64,128]{2,1,0:T(8,128)S(1)}, f32[16,64,128]{2,1,0:T(8,128)S(1)}, u32[]{:S(2)}, u32[]{:S(2)}) collective-permute-start(f32[16,64,128]{2,1,0:T(8,128)S(1)} %get-tuple-element.37), channel_id=1, source_target_pairs={{3,2},{34,3},{5,6},{38,7},{9,10},{42,11},{13,14},{46,15},{17,18},{... | collective-permute-start | bytes 1572872 | tf_op jit(solution)/shard_map/ppermute | solution.py:240
  15.8 34.2 %collective-permute-start.4 = (f32[16,64,128]{2,1,0:T(8,128)S(1)}, f32[16,64,128]{2,1,0:T(8,128)S(1)}, u32[]{:S(2)}, u32[]{:S(2)}) collective-permute-start(f32[16,64,128]{2,1,0:T(8,128)S(1)} %bitcast.10), channel_id=1, source_target_pairs={{2,4},{3,5},{6,8},{7,9},{10,12},{11,13},{14,16},{15,17},{18,20},{1... | collective-permute-start | bytes 1572872 | tf_op jit(solution)/shard_map/ppermute | solution.py:240
  17.1 32.9 %collective-permute-start.6 = (f32[16,64,128]{2,1,0:T(8,128)S(1)}, f32[16,64,128]{2,1,0:T(8,128)S(1)}, u32[]{:S(2)}, u32[]{:S(2)}) collective-permute-start(f32[16,64,128]{2,1,0:T(8,128)S(1)} %collective-permute-done.2.refs_6_), channel_id=1, source_target_pairs={{2,0},{3,1},{6,4},{7,5},{10,8},{11,9},{14,12},{15,13},{18,16},{19,... | collective-permute-start | bytes 1572872 | tf_op jit(solution)/shard_map/ppermute | solution.py:240
  19.0 36.1 %collective-permute-start.11 = (f32[16,64,128]{2,1,0:T(8,128)S(1)}, f32[16,64,128]{2,1,0:T(8,128)S(1)}, u32[]{:S(2)}, u32[]{:S(2)}) collective-permute-start(f32[16,64,128]{2,1,0:T(8,128)S(1)} %get-tuple-element.43.refs_0_), channel_id=1, source_target_pairs={{31,37},{63,69},{95,101},{127,133},{159,165},{191,197},{223,229},{... | collective-permute-start | bytes 1572872 | tf_op jit(solution)/shard_map/ppermute | solution.py:240
  19.7 30.3 %collective-permute-start.5 = (f32[3,64,128]{2,1,0:T(8,128)S(1)}, f32[3,64,128]{2,1,0:T(8,128)S(1)}, u32[]{:S(2)}, u32[]{:S(2)}) collective-permute-start(f32[3,64,128]{2,1,0:T(8,128)S(1)} %get-tuple-element.45), channel_id=1, source_target_pairs={{2,5},{3,4},{6,9},{7,8},{10,13},{11,12},{14,17},{15,16},{18,21},{1... | collective-permute-start | bytes 294920 | tf_op jit(solution)/shard_map/ppermute | solution.py:240
  52.4 10.7 %collective-permute-start.7 = (f32[16,64,128]{2,1,0:T(8,128)S(1)}, f32[16,64,128]{2,1,0:T(8,128)S(1)}, u32[]{:S(2)}, u32[]{:S(2)}) collective-permute-start(f32[16,64,128]{2,1,0:T(8,128)S(1)} %get-tuple-element.51.refs_2_), channel_id=1, source_target_pairs={{0,2},{1,3},{4,6},{5,7},{8,10},{9,11},{12,14},{13,15},{16,18},{17,... | collective-permute-start | bytes 1572872 | tf_op jit(solution)/shard_map/ppermute | solution.py:240
  53.8 24.1 %collective-permute-start.10 = (f32[16,64,128]{2,1,0:T(8,128)S(1)}, f32[16,64,128]{2,1,0:T(8,128)S(1)}, u32[]{:S(2)}, u32[]{:S(2)}) collective-permute-start(f32[16,64,128]{2,1,0:T(8,128)S(1)} %get-tuple-element.43.refs_0_), channel_id=1, source_target_pairs={{2,4},{3,5},{6,8},{7,9},{10,12},{11,13},{14,16},{15,17},{18,20},{1... | collective-permute-start | bytes 1572872 | tf_op jit(solution)/shard_map/ppermute | solution.py:240
  55.1 22.8 %collective-permute-start.12 = (f32[16,64,128]{2,1,0:T(8,128)S(1)}, f32[16,64,128]{2,1,0:T(8,128)S(1)}, u32[]{:S(2)}, u32[]{:S(2)}) collective-permute-start(f32[16,64,128]{2,1,0:T(8,128)S(1)} %collective-permute-done.11), channel_id=1, source_target_pairs={{37,33},{69,65},{101,97},{133,129},{165,161},{197,193},{229,225},{... | collective-permute-start | bytes 1572872 | tf_op jit(solution)/shard_map/ppermute | solution.py:240
  55.8 4.7 %collective-permute-start.8 = (f32[5,64,128]{2,1,0:T(8,128)S(1)}, f32[5,64,128]{2,1,0:T(8,128)S(1)}, u32[]{:S(2)}, u32[]{:S(2)}) collective-permute-start(f32[5,64,128]{2,1,0:T(8,128)S(1)} %get-tuple-element.52), channel_id=1, source_target_pairs={{0,3},{1,2},{4,7},{5,6},{8,11},{9,10},{12,15},{13,14},{16,19},{17,... | collective-permute-start | bytes 491528 | tf_op jit(solution)/shard_map/ppermute | solution.py:240
  57.1 4.7 %collective-permute-start.3 = (f32[5,64,128]{2,1,0:T(8,128)S(1)}, f32[5,64,128]{2,1,0:T(8,128)S(1)}, u32[]{:S(2)}, u32[]{:S(2)}) collective-permute-start(f32[5,64,128]{2,1,0:T(8,128)S(1)} %get-tuple-element.44), channel_id=1, source_target_pairs={{2,3},{3,2},{6,7},{7,6},{10,11},{11,10},{14,15},{15,14},{18,19},{1... | collective-permute-start | bytes 491528 | tf_op jit(solution)/shard_map/ppermute | solution.py:240
  60.5 17.3 %collective-permute-start.9 = (f32[5,64,128]{2,1,0:T(8,128)S(1)}, f32[5,64,128]{2,1,0:T(8,128)S(1)}, u32[]{:S(2)}, u32[]{:S(2)}) collective-permute-start(f32[5,64,128]{2,1,0:T(8,128)S(1)} %collective-permute-done.8.refs_5_), channel_id=1, source_target_pairs={{2,0},{3,1},{6,4},{7,5},{10,8},{11,9},{14,12},{15,13},{18,16},{19,... | collective-permute-start | bytes 491528 | tf_op jit(solution)/shard_map/ppermute | solution.py:240
  61.8 16.0 %collective-permute-start.13 = (f32[4,64,128]{2,1,0:T(8,128)S(1)}, f32[4,64,128]{2,1,0:T(8,128)S(1)}, u32[]{:S(2)}, u32[]{:S(2)}) collective-permute-start(f32[4,64,128]{2,1,0:T(8,128)S(1)} %get-tuple-element.60), channel_id=1, source_target_pairs={{2,5},{3,4},{6,9},{7,8},{10,13},{11,12},{14,17},{15,16},{18,21},{1... | collective-permute-start | bytes 393224 | tf_op jit(solution)/shard_map/ppermute | solution.py:240
  63.7 27.4 %collective-permute-start.15 = (f32[16,64,128]{2,1,0:T(8,128)S(1)}, f32[16,64,128]{2,1,0:T(8,128)S(1)}, u32[]{:S(2)}, u32[]{:S(2)}) collective-permute-start(f32[16,64,128]{2,1,0:T(8,128)S(1)} %get-tuple-element.58.refs_0_), channel_id=1, source_target_pairs={{2,4},{3,5},{6,8},{7,9},{10,12},{11,13},{14,16},{15,17},{18,20},{1... | collective-permute-start | bytes 1572872 | tf_op jit(solution)/shard_map/ppermute | solution.py:240
  80.4 10.7 %collective-permute-start.14 = (f32[16,64,128]{2,1,0:T(8,128)S(1)}, f32[16,64,128]{2,1,0:T(8,128)S(1)}, u32[]{:S(2)}, u32[]{:S(2)}) collective-permute-start(f32[16,64,128]{2,1,0:T(8,128)S(1)} %get-tuple-element.61.v_ref), channel_id=1, source_target_pairs={{0,2},{1,3},{4,6},{5,7},{8,10},{9,11},{12,14},{13,15},{16,18},{17,... | collective-permute-start | bytes 1572872 | tf_op jit(solution)/shard_map/ppermute | solution.py:240
